TPU v7x, 32 devices: a whole 2x2x4 slice. The times are simulated.
32 devices in a mesh: gx: 8 (over y, x, core), gz: 4 (over z).
Axes of the slice: x: 2, y: 2, z: 4, core: 2. Of those that a mesh axis runs over, the one named last changes fastest.
Arguments:
- velocity: float32 [3, 64, 64, 512], P(None, 'gx', None, 'gz'), may hold values from -40 to 40
Outputs:
- coefficient: float32 [64], replicated
- eddy_viscosity: float32 [64, 64, 512], P('gx', None, 'gz')
All inputs are finite; a program needn't handle non-finite values.
Results may differ from a plain program's by a relative error of at most 0.0001.
Values sent between devices are 32-bit elements; how exact they have to be, the bound alone decides.
No kernel may reach another device: no remote copies, remote signals or barrier semaphores. Data moves between devices by JAX's collectives and lax.ppermute only.
A program may use at most 64 MiB of HBM per device.

v0:
```python
import jax
import jax.numpy as jnp
from jax import lax
from jax.sharding import PartitionSpec as P

index_pairs = ((0, 0), (1, 1), (2, 2), (0, 1), (0, 2), (1, 2))
pair_weights = (1.0, 1.0, 1.0, 2.0, 2.0, 2.0)


def extended(block, sides, width):
    for axis, dim in sides:
        count = lax.axis_size(axis)
        forward = [(i, i + 1) for i in range(count - 1)]
        forward.append((count - 1, 0))
        backward = [(target, source) for source, target in forward]
        low = lax.ppermute(
            lax.slice_in_dim(block, block.shape[dim] - width, None, axis=dim), axis, forward
        )
        high = lax.ppermute(lax.slice_in_dim(block, 0, width, axis=dim), axis, backward)
        block = jnp.concatenate([low, block, high], axis=dim)
    return block


def trim_edges(field):
    return field[..., 1:-1, :, 1:-1]


def along_x(field):
    return 0.5 * (field[..., 2:, :, 1:-1] - field[..., :-2, :, 1:-1])


def along_z(field):
    return 0.5 * (field[..., 1:-1, :, 2:] - field[..., 1:-1, :, :-2])


def along_y(field):
    inside = trim_edges(field)
    middle = 0.5 * (inside[..., 2:, :] - inside[..., :-2, :])
    bottom = inside[..., 1:2, :] - inside[..., 0:1, :]
    upper_end = inside[..., -1:, :] - inside[..., -2:-1, :]
    return jnp.concatenate([bottom, middle, upper_end], axis=-2)


def strain(velocity):
    gradients = [along_x(velocity), along_y(velocity), along_z(velocity)]
    strain_rate = jnp.stack(
        [
            0.5 * (gradients[col_idx][row_idx] + gradients[row_idx][col_idx])
            for row_idx, col_idx in index_pairs
        ]
    )
    weights = jnp.array(pair_weights, dtype=jnp.float32)[:, None, None, None]
    magnitude = jnp.sqrt(2.0 * jnp.sum(weights * strain_rate * strain_rate, axis=0))
    return (strain_rate, magnitude)


def box_filter(field):
    streamwise = 0.25 * (
        field[..., :-2, :, :] + 2.0 * field[..., 1:-1, :, :] + field[..., 2:, :, :]
    )
    return 0.25 * (streamwise[..., :-2] + 2.0 * streamwise[..., 1:-1] + streamwise[..., 2:])


def pair_products(velocity):
    return jnp.stack([velocity[row_idx] * velocity[col_idx] for row_idx, col_idx in index_pairs])


def on_device(velocity):
    wide = extended(velocity, (("gx", 1), ("gz", 3)), 2)
    strain_ext, magnitude_ext = strain(wide)
    filt_prod = box_filter(pair_products(trim_edges(wide)))
    filt_stress = box_filter(magnitude_ext[None] * strain_ext)
    filt_ext = box_filter(wide)
    test_rate, test_mag = strain(filt_ext)
    filt_vel = trim_edges(filt_ext)
    grid_mag = trim_edges(magnitude_ext)
    numer = jnp.zeros((velocity.shape[2],), jnp.float32)
    denom = jnp.zeros((velocity.shape[2],), jnp.float32)
    for slot, (row_idx, col_idx) in enumerate(index_pairs):
        leonard = filt_prod[slot] - filt_vel[row_idx] * filt_vel[col_idx]
        model_term = 2.0 * (filt_stress[slot] - 4.0 * test_mag * test_rate[slot])
        numer = numer + pair_weights[slot] * jnp.sum(leonard * model_term, axis=(0, 2))
        denom = denom + pair_weights[slot] * jnp.sum(model_term * model_term, axis=(0, 2))
    numer, denom = lax.psum((numer, denom), "gx")
    numer, denom = lax.psum((numer, denom), "gz")
    cells = velocity.shape[1] * lax.axis_size("gx") * velocity.shape[3] * lax.axis_size("gz")
    coefficient = numer / cells / (denom / cells + 1e-06)
    eddy_viscosity = coefficient[None, :, None] * grid_mag
    return (coefficient, eddy_viscosity)


def solution(mesh):
    in_specs = (P(None, "gx", None, "gz"),)
    out_specs = (P(), P("gx", None, "gz"))
    return jax.shard_map(
        on_device, mesh=mesh, in_specs=in_specs, out_specs=out_specs, check_vma=False
    )
```

profile of v0, /device:TPU:0, one launch (start us, length us, event | category | flops | bytes accessed | tf_op | source)
XLA Modules:
  0.0 66.7 jit_solution(1675543667405583980)
XLA Ops:
  0.6 1.6 %copy.9 = f32[3,8,64,128]{2,3,1,0:T(8,128)S(1)} copy(f32[3,8,64,128]{3,2,1,0:T(8,128)} %param.3) | data formatting | bytes 1572864 | tf_op args[0]
  2.3 3.4 %collective-permute-start.1 = (f32[3,2,64,128]{2,3,1,0:T(8,128)S(1)}, f32[3,2,64,128]{2,3,1,0:T(8,128)S(1)}, u32[]{:S(2)}, u32[]{:S(2)}) collective-permute-start(f32[3,2,64,128]{2,3,1,0:T(8,128)S(1)} %get-tuple-element.45), channel_id=1, source_target_pairs={{4,0},{8,4},{12,8},{16,12},{20,16},{24,20},{28,24},{0,28},{5,1},{9... | collective-permute-start | bytes 589832 | tf_op jit(solution)/shard_map/ppermute | solution.py:19
  5.7 8.6 %collective-permute-done.1 = f32[3,2,64,128]{2,3,1,0:T(8,128)S(1)} collective-permute-done((f32[3,2,64,128]{2,3,1,0:T(8,128)S(1)}, f32[3,2,64,128]{2,3,1,0:T(8,128)S(1)}, u32[]{:S(2)}, u32[]{:S(2)}) %collective-permute-start.1) | collective-permute-done | bytes 196640 | tf_op jit(solution)/shard_map/ppermute | solution.py:19
  14.3 1.9 %collective-permute-done = f32[3,2,64,128]{2,3,1,0:T(8,128)S(1)} collective-permute-done((f32[3,2,64,128]{2,3,1,0:T(8,128)S(1)}, f32[3,2,64,128]{2,3,1,0:T(8,128)S(1)}, u32[]{:S(2)}, u32[]{:S(2)}) %collective-permute-start) | collective-permute-done | bytes 196640 | tf_op jit(solution)/shard_map/ppermute | solution.py:16
  16.3 3.7 %collective-permute-start.3 = (f32[3,12,64,2]{2,3,1,0:T(2,128)S(1)}, f32[3,12,64,2]{2,3,1,0:T(2,128)S(1)}, u32[]{:S(2)}, u32[]{:S(2)}) collective-permute-start(f32[3,12,64,2]{2,3,1,0:T(2,128)S(1)} %get-tuple-element.39), channel_id=1, source_target_pairs={{1,0},{2,1},{3,2},{0,3},{5,4},{6,5},{7,6},{4,7},{9,8},{10,9},{11,1... | collective-permute-start | bytes 55304 | tf_op jit(solution)/shard_map/ppermute | solution.py:19
  19.9 1.6 %collective-permute-done.3 = f32[3,12,64,2]{2,3,1,0:T(2,128)S(1)} collective-permute-done((f32[3,12,64,2]{2,3,1,0:T(2,128)S(1)}, f32[3,12,64,2]{2,3,1,0:T(2,128)S(1)}, u32[]{:S(2)}, u32[]{:S(2)}) %collective-permute-start.3) | collective-permute-done | bytes 18464 | tf_op jit(solution)/shard_map/ppermute | solution.py:19
  21.6 4.1 %collective-permute-done.2 = f32[3,12,64,2]{2,3,1,0:T(2,128)S(1)} collective-permute-done((f32[3,12,64,2]{2,3,1,0:T(2,128)S(1)}, f32[3,12,64,2]{2,3,1,0:T(2,128)S(1)}, u32[]{:S(2)}, u32[]{:S(2)}) %collective-permute-start.2) | collective-permute-done | bytes 18464 | tf_op jit(solution)/shard_map/ppermute | solution.py:16
  25.7 0.3 pad_maximum_fusion
  26.0 1.7 %slice_subtract_fusion.2 = (f32[3,10,1,130]{2,3,1,0:T(8,128)S(1)}, f32[3,10,1,130]{2,3,1,0:T(8,128)S(1)}) fusion(f32[3,12,64,132]{2,3,1,0:T(8,128)S(1)} %pad_maximum_fusion), kind=kLoop, calls=%fused_computation.32 | loop fusion | flops 7800 | bytes 93600 | tf_op jit(solution)/shard_map/sub | solution.py:39
  27.7 0.6 fusion.12
  28.3 0.3 fusion.16
  28.6 0.5 fusion.14
  29.1 2.4 %slice_subtract_fusion.7 = (f32[3,8,1,128]{2,3,1,0:T(8,128)S(1)}, f32[3,8,1,128]{2,3,1,0:T(8,128)}) fusion(f32[3,10,64,130]{2,3,1,0:T(8,128)S(1)} %fusion.14), kind=kLoop, calls=%fused_computation.50 | loop fusion | flops 6144 | bytes 73728 | tf_op jit(solution)/shard_map/sub | solution.py:39
  31.6 1.6 %fusion.19 = f32[3,8,62,128]{2,3,1,0:T(8,128)} fusion(f32[3,10,64,130]{2,3,1,0:T(8,128)S(1)} %fusion.14), kind=kLoop, calls=%fused_computation.49 | loop fusion | flops 380928 | bytes 2285568 | tf_op jit(solution)/shard_map/mul | solution.py:38
  33.3 1.4 %fusion.13 = (f32[3,10,64,130]{2,3,1,0:T(8,128)S(1)}, f32[3,10,64,130]{2,3,1,0:T(8,128)S(1)}) fusion(f32[3,12,64,132]{2,3,1,0:T(8,128)S(1)} %pad_maximum_fusion, f32[3,10,1,130]{2,3,1,0:T(8,128)S(1)} %get-tuple-element.37, f32[3,10,62,130]{2,3,1,0:T(8,128)S(1)} %fusion.12, f32[3,10,1,130]{2,3,1,0:T(8,128)S(1)} %get-tuple-element.36), kind=kLoop, calls=%fused_computation.34 | loop fusion | flops 998400 | bytes 4992000 | tf_op jit(solution)/shard_map/mul | solution.py:29
  34.8 0.4 fusion.11
  35.5 0.5 copy-done.2
  36.0 0.6 fusion
  36.8 0.3 broadcast_multiply_fusion
  37.2 0.4 fusion.1
  37.6 0.8 %fusion.6 = f32[6,8,64,128]{2,3,1,0:T(8,128)S(1)} fusion(f32[6,8,64,130]{2,3,1,0:T(8,128)S(1)} %fusion.1), kind=kLoop, calls=%fused_computation.13 | loop fusion | flops 1572864 | bytes 6291456 | tf_op jit(solution)/shard_map/mul | solution.py:61
  38.5 0.6 copy-done
  39.0 0.5 copy-done.1
  39.5 1.3 %fusion.18 = (f32[3,8,64,128]{2,3,1,0:T(8,128)S(1)}, f32[3,8,64,128]{2,3,1,0:T(8,128)S(1)}, f32[3,8,64,128]{2,3,1,0:T(8,128)S(1)}) fusion(f32[3,10,64,130]{2,3,1,0:T(8,128)S(1)} %fusion.14, f32[3,8,1,128]{2,3,1,0:T(8,128)S(1)} %copy-done, f32[3,8,62,128]{2,3,1,0:T(8,128)S(1)} %copy-done.1, f32[3,8,1,128]{2,3,1,0:T(8,128)S(1)} %get-tuple-element.42), kind=kLoop, calls=%fused_computation.46 | loop fusion | flops 1179648 | bytes 6291456 | tf_op jit(solution)/shard_map/mul | solution.py:33
  41.1 0.5 fusion.5
  42.4 0.4 fusion.3
  42.8 0.8 %fusion.8 = f32[6,8,64,128]{2,3,1,0:T(8,128)S(1)} fusion(f32[6,8,64,130]{2,3,1,0:T(8,128)S(1)} %fusion.3), kind=kLoop, calls=%fused_computation.17 | loop fusion | flops 1572864 | bytes 6291456 | tf_op jit(solution)/shard_map/mul | solution.py:61
  43.6 0.9 %fusion.65 = (f32[8,64,128]{1,2,0:T(8,128)S(1)}, f32[8,64,128]{1,2,0:T(8,128)S(1)}, f32[8,64,128]{1,2,0:T(8,128)S(1)}, f32[8,64,128]{1,2,0:T(8,128)S(1)}, f32[8,...) fusion(f32[6,8,64,128]{2,3,1,0:T(8,128)S(1)} %fusion.6, f32[3,8,64,128]{2,3,1,0:T(8,128)S(1)} %get-tuple-element.41, ...), kind=kLoop, calls=%fused_computation.129 | loop fusion | flops 2097152 | bytes 5767168 | tf_op jit(solution)/shard_map/mul | solution.py:81
  44.5 1.0 %fusion.68 = (f32[64]{0:T(128)S(1)}, f32[64]{0:T(128)S(1)}, f32[64]{0:T(128)S(1)}, f32[64]{0:T(128)S(1)}, f32[64]{0:T(128)S(1)}, /*index=5*/f32[64]{0:T(128)S(1)...) fusion(f32[8,64,128]{1,2,0:T(8,128)S(1)} %get-tuple-element.20,, ...), kind=kLoop, calls=%fused_computation.133 | loop fusion | flops 2358528 | bytes 3935232 | tf_op jit(solution)/shard_map/reduce_sum | solution.py:82
  45.6 11.8 %all-reduce = (f32[64]{0:T(128)S(1)}, f32[64]{0:T(128)S(1)}) all-reduce(f32[64]{0:T(128)S(1)} %multiply_add_fusion, f32[64]{0:T(128)S(1)} %multiply_add_fusion.1), channel_id=1, replica_groups=mesh['gx'=8,'gz'=4] {'gx'}, use_global_device_ids=true, to_apply=%region_16.0 | all-reduce | flops 128 | bytes 1024 | tf_op jit(solution)/shard_map/psum | solution.py:84
  57.4 8.4 %all-reduce.1 = (f32[64]{0:T(128)S(1)}, f32[64]{0:T(128)S(1)}) all-reduce(f32[64]{0:T(128)S(1)} %get-tuple-element.16, f32[64]{0:T(128)S(1)} %get-tuple-element.17), channel_id=1, replica_groups=mesh['gx'=8,'gz'=4] {'gz'}, use_global_device_ids=true, to_apply=%region_17.0 | all-reduce | flops 128 | bytes 1024 | tf_op jit(solution)/shard_map/psum | solution.py:85
  65.8 0.9 %copy.12 = f32[8,64,128]{2,1,0:T(8,128)} copy(f32[8,64,128]{1,2,0:T(8,128)S(1)} %slice_multiply_fusion.6) | data formatting | bytes 524288
  (32 shorter events, 1.9 us)
Async XLA Ops:
  2.3 12.0 %collective-permute-start.1 = (f32[3,2,64,128]{2,3,1,0:T(8,128)S(1)}, f32[3,2,64,128]{2,3,1,0:T(8,128)S(1)}, u32[]{:S(2)}, u32[]{:S(2)}) collective-permute-start(f32[3,2,64,128]{2,3,1,0:T(8,128)S(1)} %get-tuple-element.45), channel_id=1, source_target_pairs={{4,0},{8,4},{12,8},{16,12},{20,16},{24,20},{28,24},{0,28},{5,1},{9... | collective-permute-start | bytes 589832 | tf_op jit(solution)/shard_map/ppermute | solution.py:19
  5.7 10.5 %collective-permute-start = (f32[3,2,64,128]{2,3,1,0:T(8,128)S(1)}, f32[3,2,64,128]{2,3,1,0:T(8,128)S(1)}, u32[]{:S(2)}, u32[]{:S(2)}) collective-permute-start(f32[3,2,64,128]{2,3,1,0:T(8,128)S(1)} %get-tuple-element.44), channel_id=1, source_target_pairs={{0,4},{4,8},{8,12},{12,16},{16,20},{20,24},{24,28},{28,0},{1,5},{5... | collective-permute-start | bytes 589832 | tf_op jit(solution)/shard_map/ppermute | solution.py:16
  16.3 5.3 %collective-permute-start.3 = (f32[3,12,64,2]{2,3,1,0:T(2,128)S(1)}, f32[3,12,64,2]{2,3,1,0:T(2,128)S(1)}, u32[]{:S(2)}, u32[]{:S(2)}) collective-permute-start(f32[3,12,64,2]{2,3,1,0:T(2,128)S(1)} %get-tuple-element.39), channel_id=1, source_target_pairs={{1,0},{2,1},{3,2},{0,3},{5,4},{6,5},{7,6},{4,7},{9,8},{10,9},{11,1... | collective-permute-start | bytes 55304 | tf_op jit(solution)/shard_map/ppermute | solution.py:19
  19.9 5.8 %collective-permute-start.2 = (f32[3,12,64,2]{2,3,1,0:T(2,128)S(1)}, f32[3,12,64,2]{2,3,1,0:T(2,128)S(1)}, u32[]{:S(2)}, u32[]{:S(2)}) collective-permute-start(f32[3,12,64,2]{2,3,1,0:T(2,128)S(1)} %get-tuple-element.38), channel_id=1, source_target_pairs={{0,1},{1,2},{2,3},{3,0},{4,5},{5,6},{6,7},{7,4},{8,9},{9,10},{10,1... | collective-permute-start | bytes 55304 | tf_op jit(solution)/shard_map/ppermute | solution.py:16
  35.3 0.7 copy-start.2
  37.6 1.4 %copy-start = (f32[3,8,1,128]{2,3,1,0:T(8,128)S(1)}, f32[3,8,1,128]{2,3,1,0:T(8,128)}, u32[]{:S(2)}) copy-start(f32[3,8,1,128]{2,3,1,0:T(8,128)} %get-tuple-element.43) | copy-start | bytes 36868
  37.6 1.9 %copy-start.1 = (f32[3,8,62,128]{2,3,1,0:T(8,128)S(1)}, f32[3,8,62,128]{2,3,1,0:T(8,128)}, u32[]{:S(2)}) copy-start(f32[3,8,62,128]{2,3,1,0:T(8,128)} %fusion.19) | copy-start | bytes 2285572
  65.8 1.0 %copy-start.3 = (f32[64]{0:T(128)}, f32[64]{0:T(128)S(1)}, u32[]{:S(2)}) copy-start(f32[64]{0:T(128)S(1)} %add_divide_fusion) | copy-start | bytes 772
where the time goes:
time: 66.9 us; the launch traced here: 66.7 us
  blocking collectives  20.2 us (30%)
  other arithmetic  18.2 us (27%)
  waiting for transfers between devices  16.3 us (24%)
  starting transfers between devices  7.07 us (11%)
  local copies, waits for them, and re-layouts  4.06 us (6%)
  between operations  0.93 us (1%)
    psum x1, blocking collectives, on_device(): numer, denom = lax.psum((numer, denom), 'gx')  11.8 us
    ppermute x2, waiting for transfers between devices, extended(): lax.ppermute(lax.slice_in_dim(block, 0, width, axis=dim), axis, backward)  10.2 us
    psum x1, blocking collectives, on_device(): numer, denom = lax.psum((numer, denom), 'gz')  8.35 us
    ppermute x2, starting transfers between devices, extended(): lax.ppermute(lax.slice_in_dim(block, 0, width, axis=dim), axis, backward)  7.07 us
    ppermute x2, waiting for transfers between devices, extended(): lax.ppermute(lax.slice_in_dim(block, block.shape[dim] - width, None, axis...  6.04 us
    sub x2, other arithmetic, along_y(): bottom = inside[..., 1:2, :] - inside[..., 0:1, :]  4.1 us
    unnamed x10, local copies, waits for them, and re-layouts  4.01 us
    mul x2, other arithmetic, along_y(): middle = 0.5 * (inside[..., 2:, :] - inside[..., :-2, :])  2.25 us
  transfers between devices with their start and end apart: 4, of which 4 were waited for; matrix products, arithmetic and copies ran while one was open for 0% of the time, Pallas kernels for 0%

commit v1 on v0

--- a/solution.py
+++ b/solution.py
@@ -7,18 +7,39 @@
 pair_weights = (1.0, 1.0, 1.0, 2.0, 2.0, 2.0)
 
 
+def swap_edges(low_edge, high_edge, axis):
+    count = lax.axis_size(axis)
+    if count % 2:
+        forward = [(i, (i + 1) % count) for i in range(count)]
+        backward = [(target, source) for source, target in forward]
+        return (
+            lax.ppermute(high_edge, axis, forward),
+            lax.ppermute(low_edge, axis, backward),
+        )
+    odd = lax.axis_index(axis) % 2 == 1
+    far_pairs = [(i, (i + 1 if i % 2 else i - 1) % count) for i in range(count)]
+    near_pairs = [(i, i ^ 1) for i in range(count)]
+    far = lax.ppermute(jnp.where(odd, high_edge, low_edge), axis, far_pairs)
+    near = lax.ppermute(jnp.where(odd, low_edge, high_edge), axis, near_pairs)
+    return (jnp.where(odd, near, far), jnp.where(odd, far, near))
+
+
 def extended(block, sides, width):
     for axis, dim in sides:
-        count = lax.axis_size(axis)
-        forward = [(i, i + 1) for i in range(count - 1)]
-        forward.append((count - 1, 0))
-        backward = [(target, source) for source, target in forward]
-        low = lax.ppermute(
-            lax.slice_in_dim(block, block.shape[dim] - width, None, axis=dim), axis, forward
+        low, high = swap_edges(
+            lax.slice_in_dim(block, 0, width, axis=dim),
+            lax.slice_in_dim(block, block.shape[dim] - width, None, axis=dim),
+            axis,
         )
-        high = lax.ppermute(lax.slice_in_dim(block, 0, width, axis=dim), axis, backward)
         block = jnp.concatenate([low, block, high], axis=dim)
     return block
+
+
+def sum_over_devices(partial):
+    axes = ("gx", "gz")
+    count = lax.axis_size("gx") * lax.axis_size("gz")
+    sent = jnp.broadcast_to(partial[None], (count, *partial.shape))
+    return jnp.sum(lax.all_to_all(sent, axes, 0, 0, tiled=True), axis=0)
 
 
 def trim_edges(field):
@@ -81,8 +102,8 @@
         model_term = 2.0 * (filt_stress[slot] - 4.0 * test_mag * test_rate[slot])
         numer = numer + pair_weights[slot] * jnp.sum(leonard * model_term, axis=(0, 2))
         denom = denom + pair_weights[slot] * jnp.sum(model_term * model_term, axis=(0, 2))
-    numer, denom = lax.psum((numer, denom), "gx")
-    numer, denom = lax.psum((numer, denom), "gz")
+    sums = sum_over_devices(jnp.concatenate([numer, denom]))
+    numer, denom = jnp.split(sums, 2)
     cells = velocity.shape[1] * lax.axis_size("gx") * velocity.shape[3] * lax.axis_size("gz")
     coefficient = numer / cells / (denom / cells + 1e-06)
     eddy_viscosity = coefficient[None, :, None] * grid_mag

time: 66.9 us -> 53 us (0.79)
  blocking collectives: 20.2 us -> 11.1 us
  waiting for transfers between devices: 16.3 us -> 12.1 us
  other arithmetic: 18.2 us -> 16.5 us
  starting transfers between devices: 7.07 us -> 8.54 us
    psum x2 -> x0, blocking collectives: 20.2 us -> none  [the longest x1 11.8 us: on_device(): numer, denom = lax.psum((numer, denom), 'gx')]
    all_to_all x0 -> x1, blocking collectives: none -> 11.1 us  [sum_over_devices(): return jnp.sum(lax.all_to_all(sent, axes, 0, 0, tiled=True), axis=0)]
    ppermute x4, waiting for transfers between devices: 16.3 us -> 12.1 us  [the longest x2 12.1 us: swap_edges(): far = lax.ppermute(jnp.where(odd, high_edge, low_edge), axis, far_pairs)]
    ppermute x4, starting transfers between devices: 7.07 us -> 8.54 us  [the longest x2 6.02 us: swap_edges(): far = lax.ppermute(jnp.where(odd, high_edge, low_edge), axis, far_pairs)]
    mul x2, other arithmetic: 2.25 us -> 1.1 us  [along_y(): middle = 0.5 * (inside[..., 2:, :] - inside[..., :-2, :])]
    sub x2, other arithmetic: 4.1 us -> 2.96 us  [along_y(): bottom = inside[..., 1:2, :] - inside[..., 0:1, :]]
  transfers between devices with their start and end apart: 4 -> 4, of which waited for: 4 -> 2; matrix products, arithmetic and copies ran while one was open for 0% -> 0% of each run, Pallas kernels for 0% -> 0%
where the time goes in v1:
time: 53 us; the launch traced here: 52.8 us
  other arithmetic  16.5 us (31%)
  waiting for transfers between devices  12.1 us (23%)
  blocking collectives  11.1 us (21%)
  starting transfers between devices  8.54 us (16%)
  local copies, waits for them, and re-layouts  3.5 us (7%)
  between operations  0.98 us (2%)
    ppermute x2, waiting for transfers between devices, swap_edges(): far = lax.ppermute(jnp.where(odd, high_edge, low_edge), axis, far_pairs)  12.1 us
    all_to_all x1, blocking collectives, sum_over_devices(): return jnp.sum(lax.all_to_all(sent, axes, 0, 0, tiled=True), axis=0)  11.1 us
    ppermute x2, starting transfers between devices, swap_edges(): far = lax.ppermute(jnp.where(odd, high_edge, low_edge), axis, far_pairs)  6.02 us
    unnamed x10, local copies, waits for them, and re-layouts  3.48 us
    sub x2, other arithmetic, along_y(): bottom = inside[..., 1:2, :] - inside[..., 0:1, :]  2.96 us
    ppermute x2, starting transfers between devices, swap_edges(): near = lax.ppermute(jnp.where(odd, low_edge, high_edge), axis, near_pairs)  2.52 us
    mul x3, other arithmetic, box_filter(): 0.25 * (streamwise[..., :-2] + 2.0 * streamwise[..., 1:-1] + streamwise[....  2.17 us
    mul x2, other arithmetic, along_z(): return 0.5 * (field[..., 1:-1, :, 2:] - field[..., 1:-1, :, :-2])  1.82 us
  transfers between devices with their start and end apart: 4, of which 2 were waited for; matrix products, arithmetic and copies ran while one was open for 0% of the time, Pallas kernels for 0%

profile of v1, /device:TPU:0, one launch (start us, length us, event | category | flops | bytes accessed | tf_op | source)
XLA Modules:
  0.0 52.8 jit_solution(9748855061976088037)
XLA Ops:
  0.6 1.6 %copy.17 = f32[3,8,64,128]{2,3,1,0:T(8,128)S(1)} copy(f32[3,8,64,128]{3,2,1,0:T(8,128)} %param.3) | data formatting | bytes 1572864 | tf_op args[0]
  2.3 0.6 %collective-permute-start = (f32[3,2,64,128]{2,3,1,0:T(8,128)S(1)}, f32[3,2,64,128]{2,3,1,0:T(8,128)S(1)}, u32[]{:S(2)}, u32[]{:S(2)}) collective-permute-start(f32[3,2,64,128]{2,3,1,0:T(8,128)S(1)} %get-tuple-element.45), channel_id=1, source_target_pairs={{0,4},{4,0},{8,12},{12,8},{16,20},{20,16},{24,28},{28,24},{1,5},{5... | collective-permute-start | bytes 589832 | tf_op jit(solution)/shard_map/ppermute | solution.py:23
  2.9 3.5 %collective-permute-start.1 = (f32[3,2,64,128]{2,3,1,0:T(8,128)S(1)}, f32[3,2,64,128]{2,3,1,0:T(8,128)S(1)}, u32[]{:S(2)}, u32[]{:S(2)}) collective-permute-start(f32[3,2,64,128]{2,3,1,0:T(8,128)S(1)} %get-tuple-element.46), channel_id=1, source_target_pairs={{0,28},{4,8},{8,4},{12,16},{16,12},{20,24},{24,20},{28,0},{1,29},{... | collective-permute-start | bytes 589832 | tf_op jit(solution)/shard_map/ppermute | solution.py:22
  6.4 8.8 %collective-permute-done.1 = f32[3,2,64,128]{2,3,1,0:T(8,128)S(1)} collective-permute-done((f32[3,2,64,128]{2,3,1,0:T(8,128)S(1)}, f32[3,2,64,128]{2,3,1,0:T(8,128)S(1)}, u32[]{:S(2)}, u32[]{:S(2)}) %collective-permute-start.1) | collective-permute-done | bytes 196640 | tf_op jit(solution)/shard_map/ppermute | solution.py:22
  15.4 2.0 %collective-permute-start.2 = (f32[3,12,64,2]{2,3,1,0:T(2,128)S(1)}, f32[3,12,64,2]{2,3,1,0:T(2,128)S(1)}, u32[]{:S(2)}, u32[]{:S(2)}) collective-permute-start(f32[3,12,64,2]{2,3,1,0:T(2,128)S(1)} %get-tuple-element.20), channel_id=1, source_target_pairs={{0,1},{1,0},{2,3},{3,2},{4,5},{5,4},{6,7},{7,6},{8,9},{9,8},{10,11... | collective-permute-start | bytes 55304 | tf_op jit(solution)/shard_map/ppermute | solution.py:23
  17.4 2.5 %collective-permute-start.3 = (f32[3,12,64,2]{2,3,1,0:T(2,128)S(1)}, f32[3,12,64,2]{2,3,1,0:T(2,128)S(1)}, u32[]{:S(2)}, u32[]{:S(2)}) collective-permute-start(f32[3,12,64,2]{2,3,1,0:T(2,128)S(1)} %bitcast.111), channel_id=1, source_target_pairs={{0,3},{1,2},{2,1},{3,0},{4,7},{5,6},{6,5},{7,4},{8,11},{9,10},{10,... | collective-permute-start | bytes 55304 | tf_op jit(solution)/shard_map/ppermute | solution.py:22
  19.9 3.3 %collective-permute-done.3 = f32[3,12,64,2]{2,3,1,0:T(2,128)S(1)} collective-permute-done((f32[3,12,64,2]{2,3,1,0:T(2,128)S(1)}, f32[3,12,64,2]{2,3,1,0:T(2,128)S(1)}, u32[]{:S(2)}, u32[]{:S(2)}) %collective-permute-start.3) | collective-permute-done | bytes 18464 | tf_op jit(solution)/shard_map/ppermute | solution.py:22
  23.2 0.3 pad_maximum_fusion
  23.5 1.7 %slice_subtract_fusion.2 = (f32[3,10,1,130]{2,3,1,0:T(8,128)S(1)}, f32[3,10,1,130]{2,3,1,0:T(8,128)S(1)}) fusion(f32[3,12,64,132]{2,3,1,0:T(8,128)S(1)} %pad_maximum_fusion), kind=kLoop, calls=%fused_computation.32 | loop fusion | flops 7800 | bytes 93600 | tf_op jit(solution)/shard_map/sub | solution.py:60
  25.1 0.6 %fusion.12 = f32[3,10,62,130]{2,3,1,0:T(8,128)S(1)} fusion(f32[3,12,64,132]{2,3,1,0:T(8,128)S(1)} %pad_maximum_fusion), kind=kLoop, calls=%fused_computation.31 | loop fusion | flops 483600 | bytes 2901600 | tf_op jit(solution)/shard_map/mul | solution.py:59
  25.8 0.4 fusion.11
  26.1 0.3 fusion.16
  26.4 0.5 %fusion.14 = f32[3,10,64,130]{2,3,1,0:T(8,128)S(1)} fusion(f32[3,10,64,132]{2,3,1,0:T(8,128)S(1)} %fusion.16), kind=kLoop, calls=%fused_computation.36 | loop fusion | flops 998400 | bytes 3993600 | tf_op jit(solution)/shard_map/mul | solution.py:82
  27.0 1.3 %slice_subtract_fusion.7 = (f32[3,8,1,128]{2,3,1,0:T(8,128)S(1)}, f32[3,8,1,128]{2,3,1,0:T(8,128)S(1)}) fusion(f32[3,10,64,130]{2,3,1,0:T(8,128)S(1)} %fusion.14), kind=kLoop, calls=%fused_computation.50 | loop fusion | flops 6144 | bytes 73728 | tf_op jit(solution)/shard_map/sub | solution.py:60
  28.3 0.5 fusion.19
  28.8 1.4 %fusion.13 = (f32[3,10,64,130]{2,3,1,0:T(8,128)S(1)}, f32[3,10,64,130]{2,3,1,0:T(8,128)S(1)}) fusion(f32[3,12,64,132]{2,3,1,0:T(8,128)S(1)} %pad_maximum_fusion, f32[3,10,1,130]{2,3,1,0:T(8,128)S(1)} %get-tuple-element.40, f32[3,10,62,130]{2,3,1,0:T(8,128)S(1)} %fusion.12, f32[3,10,1,130]{2,3,1,0:T(8,128)S(1)} %get-tuple-element.39), kind=kLoop, calls=%fused_computation.34 | loop fusion | flops 998400 | bytes 4992000 | tf_op jit(solution)/shard_map/mul | solution.py:50
  30.4 0.1 fusion.26
  30.7 0.5 copy-done.2
  31.2 0.6 %fusion = f32[10,64,130]{1,2,0:T(8,128)S(1)} fusion(f32[6,10,64,130]{2,3,1,0:T(8,128)S(1)} %fusion.22, f32[6]{0:T(128)S(1)} %copy-done.2), kind=kLoop, calls=%fused_computation.2 | loop fusion | flops 1414400 | bytes 2329624 | tf_op jit(solution)/shard_map/reduce_sum | solution.py:74
  31.8 0.2 multiply_sqrt_fusion
  32.0 0.3 broadcast_multiply_fusion
  32.3 0.5 copy-done
  32.9 0.4 fusion.1
  33.3 0.8 %fusion.6 = f32[6,8,64,128]{2,3,1,0:T(8,128)S(1)} fusion(f32[6,8,64,130]{2,3,1,0:T(8,128)S(1)} %fusion.1), kind=kLoop, calls=%fused_computation.13 | loop fusion | flops 1572864 | bytes 6291456 | tf_op jit(solution)/shard_map/mul | solution.py:82
  34.1 1.5 %fusion.18 = (f32[3,8,64,128]{2,3,1,0:T(8,128)S(1)}, f32[3,8,64,128]{2,3,1,0:T(8,128)S(1)}, f32[3,8,64,128]{2,3,1,0:T(8,128)S(1)}) fusion(f32[3,10,64,130]{2,3,1,0:T(8,128)S(1)} %fusion.14, f32[3,8,1,128]{2,3,1,0:T(8,128)S(1)} %get-tuple-element.44, f32[3,8,62,128]{2,3,1,0:T(8,128)S(1)} %fusion.19, f32[3,8,1,128]{2,3,1,0:T(8,128)S(1)} %get-tuple-element.43), kind=kLoop, calls=%fused_computation.46 | loop fusion | flops 1179648 | bytes 6291456 | tf_op jit(solution)/shard_map/mul | solution.py:54
  35.9 0.5 fusion.5
  37.0 0.4 fusion.3
  37.4 0.8 %fusion.8 = f32[6,8,64,128]{2,3,1,0:T(8,128)S(1)} fusion(f32[6,8,64,130]{2,3,1,0:T(8,128)S(1)} %fusion.3), kind=kLoop, calls=%fused_computation.17 | loop fusion | flops 1572864 | bytes 6291456 | tf_op jit(solution)/shard_map/mul | solution.py:82
  38.2 1.2 %fusion.65 = (f32[8,64,128]{1,2,0:T(8,128)S(1)}, f32[8,64,128]{1,2,0:T(8,128)S(1)}, f32[8,64,128]{1,2,0:T(8,128)S(1)}, f32[8,64,128]{1,2,0:T(8,128)S(1)}, f32[8,...) fusion(f32[6,8,64,128]{2,3,1,0:T(8,128)S(1)} %fusion.6, f32[3,8,64,128]{2,3,1,0:T(8,128)S(1)} %get-tuple-element.42, ...), kind=kLoop, calls=%fused_computation.129 | loop fusion | flops 2097152 | bytes 5767168 | tf_op jit(solution)/shard_map/mul | solution.py:102
  39.5 1.0 %fusion.68 = (f32[64]{0:T(128)S(1)}, f32[64]{0:T(128)S(1)}, f32[64]{0:T(128)S(1)}, f32[64]{0:T(128)S(1)}, f32[64]{0:T(128)S(1)}, /*index=5*/f32[64]{0:T(128)S(1)...) fusion(f32[8,64,128]{1,2,0:T(8,128)S(1)} %get-tuple-element.23,, ...), kind=kLoop, calls=%fused_computation.133 | loop fusion | flops 2358528 | bytes 3935232 | tf_op jit(solution)/shard_map/reduce_sum | solution.py:103
  40.6 11.1 %all_to_all.6 = f32[32,1,128]{2,1,0:T(1,128)S(1)} all-to-all(f32[32,1,128]{2,1,0:T(1,128)S(1)} %broadcast_in_dim.2), channel_id=1, replica_groups=mesh['gx'=8,'gz'=4] {'gx','gz'}, dimensions={0} | all-to-all | bytes 32768 | tf_op jit(solution)/shard_map/all_to_all | solution.py:42
  51.9 0.9 %copy.21 = f32[8,64,128]{2,1,0:T(8,128)} copy(f32[8,64,128]{1,2,0:T(8,128)S(1)} %slice_multiply_fusion.6) | data formatting | bytes 524288
  (37 shorter events, 1.7 us)
Async XLA Ops:
  2.3 4.1 %collective-permute-start = (f32[3,2,64,128]{2,3,1,0:T(8,128)S(1)}, f32[3,2,64,128]{2,3,1,0:T(8,128)S(1)}, u32[]{:S(2)}, u32[]{:S(2)}) collective-permute-start(f32[3,2,64,128]{2,3,1,0:T(8,128)S(1)} %get-tuple-element.45), channel_id=1, source_target_pairs={{0,4},{4,0},{8,12},{12,8},{16,20},{20,16},{24,28},{28,24},{1,5},{5... | collective-permute-start | bytes 589832 | tf_op jit(solution)/shard_map/ppermute | solution.py:23
  2.9 12.4 %collective-permute-start.1 = (f32[3,2,64,128]{2,3,1,0:T(8,128)S(1)}, f32[3,2,64,128]{2,3,1,0:T(8,128)S(1)}, u32[]{:S(2)}, u32[]{:S(2)}) collective-permute-start(f32[3,2,64,128]{2,3,1,0:T(8,128)S(1)} %get-tuple-element.46), channel_id=1, source_target_pairs={{0,28},{4,8},{8,4},{12,16},{16,12},{20,24},{24,20},{28,0},{1,29},{... | collective-permute-start | bytes 589832 | tf_op jit(solution)/shard_map/ppermute | solution.py:22
  15.4 4.4 %collective-permute-start.2 = (f32[3,12,64,2]{2,3,1,0:T(2,128)S(1)}, f32[3,12,64,2]{2,3,1,0:T(2,128)S(1)}, u32[]{:S(2)}, u32[]{:S(2)}) collective-permute-start(f32[3,12,64,2]{2,3,1,0:T(2,128)S(1)} %get-tuple-element.20), channel_id=1, source_target_pairs={{0,1},{1,0},{2,3},{3,2},{4,5},{5,4},{6,7},{7,6},{8,9},{9,8},{10,11... | collective-permute-start | bytes 55304 | tf_op jit(solution)/shard_map/ppermute | solution.py:23
  17.4 5.8 %collective-permute-start.3 = (f32[3,12,64,2]{2,3,1,0:T(2,128)S(1)}, f32[3,12,64,2]{2,3,1,0:T(2,128)S(1)}, u32[]{:S(2)}, u32[]{:S(2)}) collective-permute-start(f32[3,12,64,2]{2,3,1,0:T(2,128)S(1)} %bitcast.111), channel_id=1, source_target_pairs={{0,3},{1,2},{2,1},{3,0},{4,7},{5,6},{6,5},{7,4},{8,11},{9,10},{10,... | collective-permute-start | bytes 55304 | tf_op jit(solution)/shard_map/ppermute | solution.py:22
  30.5 0.7 %copy-start.2 = (f32[6]{0:T(128)S(1)}, f32[6]{0:T(128)}, u32[]{:S(2)}) copy-start(f32[6]{0:T(128)} %constant.59.clone) | copy-start | bytes 76
  32.0 0.9 %copy-start = (f32[10,64,130]{1,2,0:T(8,128)}, f32[10,64,130]{1,2,0:T(8,128)S(1)}, u32[]{:S(2)}) copy-start(f32[10,64,130]{1,2,0:T(8,128)S(1)} %multiply_sqrt_fusion) | copy-start | bytes 998404
  39.4 12.4 %copy-start.1 = (f32[10,64,130]{1,2,0:T(8,128)S(1)}, f32[10,64,130]{1,2,0:T(8,128)}, u32[]{:S(2)}) copy-start(f32[10,64,130]{1,2,0:T(8,128)} %copy-done) | copy-start | bytes 998404
  51.8 1.0 %copy-start.3 = (f32[64]{0:T(128)}, f32[64]{0:T(128)S(1)}, u32[]{:S(2)}) copy-start(f32[64]{0:T(128)S(1)} %add_divide_fusion) | copy-start | bytes 772

commit v2 on v0

v2 whole, which is shorter than its diff:
```python
import functools

import jax
import jax.numpy as jnp
from jax import lax
from jax.experimental import pallas as pl
from jax.experimental.pallas import tpu as pltpu
from jax.sharding import PartitionSpec as P

WIDTH = 2
ROWS = 8
index_pairs = ((0, 0), (1, 1), (2, 2), (0, 1), (0, 2), (1, 2))
TOP = 9

VMEM = pl.BlockSpec(memory_space=pltpu.VMEM)


def swap_pairs(count):
    far = [(i, (i + 1 if i % 2 else i - 1) % count) for i in range(count)]
    near = [(i, i ^ 1) for i in range(count)]
    return far, near


def swap_edges(for_below, for_above, axis):
    count = lax.axis_size(axis)
    if count % 2:
        forward = [(i, (i + 1) % count) for i in range(count)]
        backward = [(target, source) for source, target in forward]
        return (
            lax.ppermute(for_above, axis, forward),
            lax.ppermute(for_below, axis, backward),
        )
    odd = lax.axis_index(axis) % 2 == 1
    far_pairs, near_pairs = swap_pairs(count)
    far = lax.ppermute(jnp.where(odd, for_above, for_below), axis, far_pairs)
    near = lax.ppermute(jnp.where(odd, for_below, for_above), axis, near_pairs)
    return (jnp.where(odd, near, far), jnp.where(odd, far, near))


def to_folded(plane):
    half = plane.shape[1] // 2
    return jnp.concatenate([plane[:, :half], plane[:, half:]], axis=0).T


def from_folded(folded):
    ny = folded.shape[1] // 2
    turned = folded.T
    return jnp.concatenate([turned[:ny], turned[ny:]], axis=1)


def fold_kernel(vel_ref, below_ref, above_ref, u_ref, edge_ref):
    nx, ny, nz = vel_ref.shape[1:]
    half = nz // 2
    lower = lax.broadcasted_iota(jnp.int32, (WIDTH, 2 * ny), 1) < ny

    def put(comp, slot, plane):
        folded = to_folded(plane)
        u_ref[comp, slot] = folded
        edge_ref[comp, slot] = jnp.where(lower, folded[:WIDTH], folded[half - WIDTH :])

    for comp in range(3):
        for layer in range(WIDTH):
            put(comp, layer, below_ref[comp, layer])
            put(comp, WIDTH + nx + layer, above_ref[comp, layer])

        def step(x, carry):
            put(comp, WIDTH + x, vel_ref[comp, x])
            return carry

        lax.fori_loop(0, nx, step, 0)


def slope_along_lanes(field, first, last, scale):
    lanes = field.shape[1]
    up = jnp.where(last, field, pltpu.roll(field, lanes - 1, 1))
    down = jnp.where(first, field, pltpu.roll(field, 1, 1))
    return (up - down) * scale


def rates(slopes):
    rate = [
        slopes[i][i] if i == j else slopes[i][j] + slopes[j][i] for i, j in index_pairs
    ]
    squares = [r * r for r in rate]
    straight = squares[0] + squares[1] + squares[2]
    crossed = squares[3] + squares[4] + squares[5]
    return rate, 0.5 * jnp.sqrt((straight + straight) + crossed)


def weighted(low, mid, high):
    return (low + high) + (mid + mid)


def main_kernel(
    u_ref, low_ref, high_ref, mag_ref, sums_ref, ue, tmp, fz, hz, hu, mag
):
    planes, half, lanes = u_ref.shape[1:]
    nx = planes - 2 * WIDTH
    ny = lanes // 2
    zero = jnp.minimum(lax.axis_index("gx"), 0)
    lane = lax.broadcasted_iota(jnp.int32, (ROWS, lanes), 1)
    row_y = lax.rem(lane, ny)
    first, last = row_y == 0, row_y == ny - 1
    scale = jnp.where(first | last, 2.0, 1.0).astype(jnp.float32)
    upper = lax.broadcasted_iota(jnp.int32, (WIDTH, lanes), 1) >= ny

    def rows(start, count=ROWS):
        return pl.ds(zero + start, count)

    def fill(x, carry):
        for comp in range(3):
            for k in range(half // ROWS):
                ue[comp, x, rows(TOP + ROWS * k)] = u_ref[comp, x, ROWS * k : ROWS * (k + 1)]
            below = jnp.where(upper, low_ref[comp, x], u_ref[comp, x, half - WIDTH :])
            above = jnp.where(upper, u_ref[comp, x, :WIDTH], high_ref[comp, x])
            ue[comp, x, rows(TOP - WIDTH, WIDTH)] = pltpu.roll(below, ny, 1)
            ue[comp, x, rows(TOP + half, WIDTH)] = pltpu.roll(above, ny, 1)
        return carry

    lax.fori_loop(0, planes, fill, 0)
    windows = half // ROWS + 1

    def filter_z(x, k, comp):
        at = TOP - 1 + ROWS * k
        return weighted(
            ue[comp, x, rows(at - 1)], ue[comp, x, rows(at)], ue[comp, x, rows(at + 1)]
        )

    for x in (0, planes - 1):
        for k in range(windows):
            for comp in range(3):
                hz[comp, x, ROWS * k : ROWS * (k + 1)] = filter_z(x, k, comp)

    def strain_plane(i, carry):
        for k in range(windows):
            at = TOP - 1 + ROWS * k
            here = pl.ds(ROWS * k, ROWS)
            mid = [ue[comp, i + 1, rows(at)] for comp in range(3)]
            after = [ue[comp, i + 1, rows(at + 1)] for comp in range(3)]
            before = [ue[comp, i + 1, rows(at - 1)] for comp in range(3)]
            slopes = [
                (
                    ue[comp, i + 2, rows(at)] - ue[comp, i, rows(at)],
                    slope_along_lanes(mid[comp], first, last, scale),
                    after[comp] - before[comp],
                )
                for comp in range(3)
            ]
            rate, size = rates(slopes)
            mag[i, here] = size
            scaled = size * 0.0625
            quarter = [0.25 * m for m in mid]
            for n, (a, b) in enumerate(index_pairs):
                tmp[n, here] = scaled * rate[n]
                tmp[6 + n, here] = quarter[a] * quarter[b]
            for comp in range(3):
                hz[comp, i + 1, here] = weighted(before[comp], mid[comp], after[comp])
        for n in range(12):
            for k in range(half // ROWS):
                fz[n, i, ROWS * k : ROWS * (k + 1)] = weighted(
                    tmp[n, rows(ROWS * k)], tmp[n, rows(ROWS * k + 1)], tmp[n, rows(ROWS * k + 2)]
                )
        return carry

    lax.fori_loop(0, nx + 2, strain_plane, 0)

    def hat_plane(i, carry):
        for comp in range(3):
            for k in range(windows):
                here = pl.ds(ROWS * k, ROWS)
                hu[comp, i, here] = 0.0625 * weighted(
                    hz[comp, i, here], hz[comp, i + 1, here], hz[comp, i + 2, here]
                )
        return carry

    lax.fori_loop(0, nx + 2, hat_plane, 0)

    def sum_plane(x, carry):
        numer, denom = carry
        for k in range(half // ROWS):
            at = 1 + ROWS * k
            here = pl.ds(ROWS * k, ROWS)
            mid = [hu[comp, x + 1, rows(at)] for comp in range(3)]
            slopes = [
                (
                    hu[comp, x + 2, rows(at)] - hu[comp, x, rows(at)],
                    slope_along_lanes(mid[comp], first, last, scale),
                    hu[comp, x + 1, rows(at + 1)] - hu[comp, x + 1, rows(at - 1)],
                )
                for comp in range(3)
            ]
            rate, size = rates(slopes)
            size = 4.0 * size
            top, straight, crossed = [], [], []
            for n, (a, b) in enumerate(index_pairs):
                stress = weighted(fz[n, x, here], fz[n, x + 1, here], fz[n, x + 2, here])
                product = weighted(
                    fz[6 + n, x, here], fz[6 + n, x + 1, here], fz[6 + n, x + 2, here]
                )
                model = stress - size * rate[n]
                leonard = product - mid[a] * mid[b]
                top.append(leonard * model)
                (straight if a == b else crossed).append(model * model)
            numer = numer + ((top[0] + top[1]) + (top[2] + top[3]) + (top[4] + top[5]))
            denom = denom + (
                (straight[0] + straight[1] + straight[2])
                + 0.5 * (crossed[0] + crossed[1] + crossed[2])
            )
        mag_ref[x] = from_folded(mag[x + 1, rows(1, half)])
        return numer, denom

    start = jnp.zeros((ROWS, lanes), jnp.float32)
    numer, denom = lax.fori_loop(0, nx, sum_plane, (start, start))
    numer = jnp.sum(numer, axis=0, keepdims=True)
    denom = jnp.sum(denom, axis=0, keepdims=True)
    numer = numer + pltpu.roll(numer, ny, 1)
    denom = denom + pltpu.roll(denom, ny, 1)
    both = jnp.where(lax.broadcasted_iota(jnp.int32, (1, lanes), 1) < ny, numer, denom)
    sums_ref[...] = jnp.broadcast_to(both, sums_ref.shape)


def finish_kernel(cells, parts_ref, mag_ref, coefficient_ref, eddy_ref):
    lanes = parts_ref.shape[1]
    ny = lanes // 2
    sums = jnp.sum(parts_ref[...], axis=0, keepdims=True)
    numer = sums[:, :ny]
    denom = pltpu.roll(sums, ny, 1)[:, :ny]
    coefficient = numer / cells / (denom / cells + 1e-06)
    coefficient_ref[...] = coefficient
    column = jnp.broadcast_to(coefficient, (mag_ref.shape[2], ny)).T
    for x in range(mag_ref.shape[0]):
        eddy_ref[x] = column * mag_ref[x]


def on_device(velocity):
    nx, ny, nz = velocity.shape[1:]
    half, lanes = nz // 2, 2 * ny
    planes = nx + 2 * WIDTH
    f32 = jnp.float32
    params = pltpu.CompilerParams(vmem_limit_bytes=24 * 1024 * 1024)

    below, above = swap_edges(velocity[:, :WIDTH], velocity[:, nx - WIDTH :], "gx")
    folded, edges = pl.pallas_call(
        fold_kernel,
        out_shape=(
            jax.ShapeDtypeStruct((3, planes, half, lanes), f32),
            jax.ShapeDtypeStruct((3, planes, WIDTH, lanes), f32),
        ),
        in_specs=[VMEM] * 3,
        out_specs=(VMEM, VMEM),
        compiler_params=params,
        name="fold",
    )(velocity, below, above)
    low, high = swap_edges(edges, edges, "gz")
    count = lax.axis_size("gx") * lax.axis_size("gz")
    tall = half + 3 * ROWS
    windowed = half + ROWS
    magnitude, sums = pl.pallas_call(
        main_kernel,
        out_shape=(
            jax.ShapeDtypeStruct((nx, ny, nz), f32),
            jax.ShapeDtypeStruct((count, lanes), f32),
        ),
        in_specs=[VMEM] * 3,
        out_specs=(VMEM, VMEM),
        scratch_shapes=[
            pltpu.VMEM((3, planes, tall, lanes), f32),
            pltpu.VMEM((12, windowed + ROWS, lanes), f32),
            pltpu.VMEM((12, nx + 2, half, lanes), f32),
            pltpu.VMEM((3, planes, windowed, lanes), f32),
            pltpu.VMEM((3, nx + 2, windowed, lanes), f32),
            pltpu.VMEM((nx + 2, windowed, lanes), f32),
        ],
        compiler_params=params,
        name="model",
    )(folded, low, high)
    parts = lax.all_to_all(sums, ("gx", "gz"), 0, 0, tiled=True)
    cells = nx * lax.axis_size("gx") * nz * lax.axis_size("gz")
    coefficient, eddy_viscosity = pl.pallas_call(
        functools.partial(finish_kernel, cells),
        out_shape=(
            jax.ShapeDtypeStruct((1, ny), f32),
            jax.ShapeDtypeStruct((nx, ny, nz), f32),
        ),
        in_specs=[VMEM] * 2,
        out_specs=(VMEM, VMEM),
        compiler_params=params,
        name="finish",
    )(parts, magnitude)
    return (coefficient[0], eddy_viscosity)


def solution(mesh):
    in_specs = (P(None, "gx", None, "gz"),)
    out_specs = (P(), P("gx", None, "gz"))
    return jax.shard_map(
        on_device, mesh=mesh, in_specs=in_specs, out_specs=out_specs, check_vma=False
    )
```

time: 66.9 us -> 40.5 us (0.61)
  other arithmetic: 18.2 us -> 1.16 us
  Pallas kernels: 0 us -> 11 us
  blocking collectives: 20.2 us -> 10.2 us
  waiting for transfers between devices: 16.3 us -> 8.56 us
  local copies, waits for them, and re-layouts: 4.06 us -> 0.01 us
  starting transfers between devices: 7.07 us -> 8.6 us
    psum x2 -> x0, blocking collectives: 20.2 us -> none  [the longest x1 11.8 us: on_device(): numer, denom = lax.psum((numer, denom), 'gx')]
    pallas_call x0 -> x3, Pallas kernels: none -> 11 us  [the longest x1 6.51 us: on_device(): pl.pallas_call(main_kernel, out_shape=(jax.ShapeDtypeStruct((nx, ny, nz),...]
    all_to_all x0 -> x1, blocking collectives: none -> 10.2 us  [on_device(): parts = lax.all_to_all(sums, ('gx', 'gz'), 0, 0, tiled=True)]
    mul x14 -> x0, other arithmetic: 9.9 us -> none  [the longest x2 2.25 us: along_y(): middle = 0.5 * (inside[..., 2:, :] - inside[..., :-2, :])]
    ppermute x4, waiting for transfers between devices: 16.3 us -> 8.56 us  [the longest x2 6.54 us: swap_edges(): far = lax.ppermute(jnp.where(odd, for_above, for_below), axis, far_pairs)]
    sub x2 -> x0, other arithmetic: 4.1 us -> none  [along_y(): bottom = inside[..., 1:2, :] - inside[..., 0:1, :]]
    unnamed x10 -> x2, local copies, waits for them, and re-layouts: 4.01 us -> 0.01 us
    reduce_sum x3 -> x0, other arithmetic: 2.17 us -> none  [the longest x2 1.15 us: strain(): jnp.sum(weights * strain_rate * strain_rate, axis=0)]
  transfers between devices with their start and end apart: 4 -> 4, of which waited for: 4 -> 3; matrix products, arithmetic and copies ran while one was open for 0% -> 0% of each run, Pallas kernels for 0% -> 0%
where the time goes in v2:
time: 40.5 us; the launch traced here: 40.3 us
  Pallas kernels  11 us (27%)
  blocking collectives  10.2 us (25%)
  starting transfers between devices  8.6 us (21%)
  waiting for transfers between devices  8.56 us (21%)
  other arithmetic  1.16 us (3%)
  between operations  0.72 us (2%)
    all_to_all x1, blocking collectives, on_device(): parts = lax.all_to_all(sums, ('gx', 'gz'), 0, 0, tiled=True)  10.2 us
    ppermute x2, starting transfers between devices, swap_edges(): far = lax.ppermute(jnp.where(odd, for_above, for_below), axis, far_pairs)  8.6 us
    ppermute x2, waiting for transfers between devices, swap_edges(): far = lax.ppermute(jnp.where(odd, for_above, for_below), axis, far_pairs)  6.54 us
    pallas_call x1, Pallas kernels, on_device(): pl.pallas_call(main_kernel, out_shape=(jax.ShapeDtypeStruct((nx, ny, nz),...  6.51 us
    pallas_call x1, Pallas kernels, on_device(): pl.pallas_call(fold_kernel, out_shape=(jax.ShapeDtypeStruct((3, planes, h...  3.66 us
    ppermute x2, waiting for transfers between devices, swap_edges(): near = lax.ppermute(jnp.where(odd, for_below, for_above), axis, near_pairs)  2.02 us
    select_n x1, other arithmetic, swap_edges(): far = lax.ppermute(jnp.where(odd, for_above, for_below), axis, far_pairs)  1.13 us
    pallas_call x1, Pallas kernels, on_device(): pl.pallas_call(functools.partial(finish_kernel, cells), out_shape=(jax.Sh...  0.88 us
  transfers between devices with their start and end apart: 4, of which 3 were waited for; matrix products, arithmetic and copies ran while one was open for 0% of the time, Pallas kernels for 0%

profile of v2, /device:TPU:0, one launch (start us, length us, event | category | flops | bytes accessed | tf_op | source)
XLA Modules:
  0.0 40.3 jit_solution(1541100678871140536)
XLA Ops:
  0.6 0.0 copy-start
  0.7 1.1 %slice_select_fusion = (f32[3,2,64,128]{3,2,1,0:T(8,128)S(1)}, f32[3,2,64,128]{3,2,1,0:T(8,128)S(1)}) fusion(f32[3,8,64,128]{3,2,1,0:T(8,128)} %vel_ref.1, pred[]{:T(512)S(6)} %eq.9), kind=kLoop, calls=%fused_computation | loop fusion | flops 98304 | bytes 786433 | tf_op jit(solution)/shard_map/jit(_where)/select_n | solution.py:35
  1.8 3.4 %collective-permute-start.1 = (f32[3,2,64,128]{3,2,1,0:T(8,128)S(1)}, f32[3,2,64,128]{3,2,1,0:T(8,128)S(1)}, u32[]{:S(2)}, u32[]{:S(2)}) collective-permute-start(f32[3,2,64,128]{3,2,1,0:T(8,128)S(1)} %get-tuple-element.14), channel_id=1, source_target_pairs={{0,28},{4,8},{8,4},{12,16},{16,12},{20,24},{24,20},{28,0},{1,29},{... | collective-permute-start | bytes 589832 | tf_op jit(solution)/shard_map/ppermute | solution.py:35
  5.2 0.0 collective-permute-start
  5.2 4.6 %collective-permute-done.1 = f32[3,2,64,128]{3,2,1,0:T(8,128)S(1)} collective-permute-done((f32[3,2,64,128]{3,2,1,0:T(8,128)S(1)}, f32[3,2,64,128]{3,2,1,0:T(8,128)S(1)}, u32[]{:S(2)}, u32[]{:S(2)}) %collective-permute-start.1) | collective-permute-done | bytes 196640 | tf_op jit(solution)/shard_map/ppermute | solution.py:35
  9.8 0.0 collective-permute-done
  9.9 0.0 copy-done
  9.9 3.7 %fold.1 = (f32[3,12,64,128]{3,2,1,0:T(8,128)S(1)}, f32[3,12,2,128]{3,2,1,0:T(2,128)S(1)}) custom-call(f32[3,8,64,128]{3,2,1,0:T(8,128)S(1)} %copy-done, f32[3,2,64,128]{3,2,1,0:T(8,128)S(1)} %get-tuple-element.17.below_ref, f32[3,2,64,128]{3,2,1,0:T(8,128)S(1)} %get-tuple-element.16.above_ref), custom_call_target="tpu_custom_call" | custom-call | tf_op jit(solution)/shard_map/fold/pallas_call | solution.py:243
  13.6 5.2 %collective-permute-start.3 = (f32[3,12,2,128]{3,2,1,0:T(2,128)S(1)}, f32[3,12,2,128]{3,2,1,0:T(2,128)S(1)}, u32[]{:S(2)}, u32[]{:S(2)}) collective-permute-start(f32[3,12,2,128]{3,2,1,0:T(2,128)S(1)} %get-tuple-element.9), channel_id=1, source_target_pairs={{0,3},{1,2},{2,1},{3,0},{4,7},{5,6},{6,5},{7,4},{8,11},{9,10},{10,... | collective-permute-start | bytes 110600 | tf_op jit(solution)/shard_map/ppermute | solution.py:35
  18.7 0.0 collective-permute-start.2
  18.7 1.9 %collective-permute-done.3 = f32[3,12,2,128]{3,2,1,0:T(2,128)S(1)} collective-permute-done((f32[3,12,2,128]{3,2,1,0:T(2,128)S(1)}, f32[3,12,2,128]{3,2,1,0:T(2,128)S(1)}, u32[]{:S(2)}, u32[]{:S(2)}) %collective-permute-start.3) | collective-permute-done | bytes 36896 | tf_op jit(solution)/shard_map/ppermute | solution.py:35
  20.7 2.0 %collective-permute-done.2 = f32[3,12,2,128]{3,2,1,0:T(2,128)S(1)} collective-permute-done((f32[3,12,2,128]{3,2,1,0:T(2,128)S(1)}, f32[3,12,2,128]{3,2,1,0:T(2,128)S(1)}, u32[]{:S(2)}, u32[]{:S(2)}) %collective-permute-start.2) | collective-permute-done | bytes 36896 | tf_op jit(solution)/shard_map/ppermute | solution.py:36
  22.7 6.5 %model.1 = (f32[8,64,128]{2,1,0:T(8,128)S(1)}, f32[32,128]{1,0:T(8,128)S(1)}) custom-call(f32[3,12,64,128]{3,2,1,0:T(8,128)S(1)} %get-tuple-element.8.u_ref, f32[3,12,2,128]{3,2,1,0:T(2,128)S(1)} %bitcast.10, f32[3,12,2,128]{3,2,1,0:T(2,128)S(1)} %bitcast.9), custom_call_target="tpu_custom_call" | custom-call | tf_op jit(solution)/shard_map/model/pallas_call | solution.py:258
  29.2 10.2 %all_to_all.11 = f32[32,1,128]{2,1,0:T(1,128)S(1)} all-to-all(f32[32,1,128]{2,1,0:T(1,128)S(1)} %bitcast.12), channel_id=1, replica_groups=mesh['gx'=8,'gz'=4] {'gx','gz'}, dimensions={0} | all-to-all | bytes 32768 | tf_op jit(solution)/shard_map/all_to_all | solution.py:277
  39.4 0.9 %finish.1 = (f32[1,64]{1,0:T(1,128)}, f32[8,64,128]{2,1,0:T(8,128)}) custom-call(f32[32,128]{1,0:T(8,128)S(1)} %bitcast.11, f32[8,64,128]{2,1,0:T(8,128)S(1)} %get-tuple-element.11.mag_ref), custom_call_target="tpu_custom_call" | custom-call | tf_op jit(solution)/shard_map/finish/pallas_call | solution.py:279
  (2 shorter events, 0.0 us)
Async XLA Ops:
  0.6 9.2 %copy-start = (f32[3,8,64,128]{3,2,1,0:T(8,128)S(1)}, f32[3,8,64,128]{3,2,1,0:T(8,128)}, u32[]{:S(2)}) copy-start(f32[3,8,64,128]{3,2,1,0:T(8,128)} %vel_ref.1) | copy-start | bytes 2359300
  1.8 8.0 %collective-permute-start.1 = (f32[3,2,64,128]{3,2,1,0:T(8,128)S(1)}, f32[3,2,64,128]{3,2,1,0:T(8,128)S(1)}, u32[]{:S(2)}, u32[]{:S(2)}) collective-permute-start(f32[3,2,64,128]{3,2,1,0:T(8,128)S(1)} %get-tuple-element.14), channel_id=1, source_target_pairs={{0,28},{4,8},{8,4},{12,16},{16,12},{20,24},{24,20},{28,0},{1,29},{... | collective-permute-start | bytes 589832 | tf_op jit(solution)/shard_map/ppermute | solution.py:35
  5.2 4.6 %collective-permute-start = (f32[3,2,64,128]{3,2,1,0:T(8,128)S(1)}, f32[3,2,64,128]{3,2,1,0:T(8,128)S(1)}, u32[]{:S(2)}, u32[]{:S(2)}) collective-permute-start(f32[3,2,64,128]{3,2,1,0:T(8,128)S(1)} %get-tuple-element.15), channel_id=1, source_target_pairs={{0,4},{4,0},{8,12},{12,8},{16,20},{20,16},{24,28},{28,24},{1,5},{5... | collective-permute-start | bytes 589832 | tf_op jit(solution)/shard_map/ppermute | solution.py:36
  13.6 7.1 %collective-permute-start.3 = (f32[3,12,2,128]{3,2,1,0:T(2,128)S(1)}, f32[3,12,2,128]{3,2,1,0:T(2,128)S(1)}, u32[]{:S(2)}, u32[]{:S(2)}) collective-permute-start(f32[3,12,2,128]{3,2,1,0:T(2,128)S(1)} %get-tuple-element.9), channel_id=1, source_target_pairs={{0,3},{1,2},{2,1},{3,0},{4,7},{5,6},{6,5},{7,4},{8,11},{9,10},{10,... | collective-permute-start | bytes 110600 | tf_op jit(solution)/shard_map/ppermute | solution.py:35
  18.7 4.0 %collective-permute-start.2 = (f32[3,12,2,128]{3,2,1,0:T(2,128)S(1)}, f32[3,12,2,128]{3,2,1,0:T(2,128)S(1)}, u32[]{:S(2)}, u32[]{:S(2)}) collective-permute-start(f32[3,12,2,128]{3,2,1,0:T(2,128)S(1)} %get-tuple-element.9), channel_id=1, source_target_pairs={{0,1},{1,0},{2,3},{3,2},{4,5},{5,4},{6,7},{7,6},{8,9},{9,8},{10,11... | collective-permute-start | bytes 110600 | tf_op jit(solution)/shard_map/ppermute | solution.py:36

commit v3 on v0

v3 whole, which is shorter than its diff:
```python
import functools

import jax
import jax.numpy as jnp
from jax import lax
from jax.experimental import pallas as pl
from jax.experimental.pallas import tpu as pltpu
from jax.sharding import PartitionSpec as P

WIDTH = 2
ROWS = 8
index_pairs = ((0, 0), (1, 1), (2, 2), (0, 1), (0, 2), (1, 2))
TOP = 9
SHARED = pltpu.CompilerParams(vmem_limit_bytes=8 * 1024 * 1024)

VMEM = pl.BlockSpec(memory_space=pltpu.VMEM)


def swap_pairs(count):
    far = [(i, (i + 1 if i % 2 else i - 1) % count) for i in range(count)]
    near = [(i, i ^ 1) for i in range(count)]
    return far, near


def swap_edges(for_below, for_above, axis):
    count = lax.axis_size(axis)
    if count % 2:
        forward = [(i, (i + 1) % count) for i in range(count)]
        backward = [(target, source) for source, target in forward]
        return (
            lax.ppermute(for_above, axis, forward),
            lax.ppermute(for_below, axis, backward),
        )
    far_pairs, near_pairs = swap_pairs(count)
    if for_below is for_above:
        near_send = far_send = for_below
    else:
        odd = lax.axis_index(axis) % 2 == 1
        far_send = jnp.where(odd, for_above, for_below)
        near_send = jnp.where(odd, for_below, for_above)
    far = lax.ppermute(far_send, axis, far_pairs)
    near = lax.ppermute(near_send, axis, near_pairs)
    return near, far


def below_is_first(axis):
    if lax.axis_size(axis) % 2:
        return True
    return lax.rem(lax.axis_index(axis), 2) == 1


def mirrored(plane):
    lanes = plane.shape[1]
    lane = lax.broadcasted_iota(jnp.int32, plane.shape, 1)
    return jnp.take_along_axis(plane, lanes - 1 - lane, axis=1)


def to_folded(plane):
    half = plane.shape[1] // 2
    return jnp.concatenate([plane[:, :half], mirrored(plane)[:, :half]], axis=0).T


def from_folded(folded):
    half, lanes = folded.shape
    ny = lanes // 2
    turned = folded.T
    both = jnp.concatenate([turned[:ny], turned[ny:]], axis=1)
    lane = lax.broadcasted_iota(jnp.int32, both.shape, 1)
    return jnp.take_along_axis(both, jnp.where(lane < half, lane, 3 * half - 1 - lane), axis=1)


class Lanes:
    def __init__(self, lanes):
        self.zero = jnp.minimum(lax.axis_index("gx"), 0)
        lane = lax.broadcasted_iota(jnp.int32, (ROWS, lanes), 1)
        row_y = lax.rem(lane, lanes // 2)
        self.first, self.last = row_y == 0, row_y == lanes // 2 - 1
        self.scale = jnp.where(self.first | self.last, 2.0, 1.0).astype(jnp.float32)
        self.sign = jnp.where(lane < lanes // 2, 1.0, -1.0).astype(jnp.float32)

    def rows(self, start, count=ROWS):
        return pl.ds(self.zero + start, count)

    def slope_y(self, field):
        lanes = field.shape[1]
        up = jnp.where(self.last, field, pltpu.roll(field, lanes - 1, 1))
        down = jnp.where(self.first, field, pltpu.roll(field, 1, 1))
        return (up - down) * self.scale

    def slope_z(self, after, before):
        return (after - before) * self.sign


def window(k):
    return pl.ds(ROWS * k, ROWS)


def store_plane(ln, u_ref, comp, slot, plane):
    folded = to_folded(plane)
    half, lanes = folded.shape
    for k in range(half // ROWS):
        u_ref[comp, slot, ln.rows(TOP + ROWS * k)] = folded[ROWS * k : ROWS * (k + 1)]
    inner = pltpu.roll(folded[half - ROWS :], lanes // 2, 1)
    for layer in range(WIDTH):
        u_ref[comp, slot, ln.rows(TOP + half + layer, 1)] = inner[ROWS - 1 - layer : ROWS - layer]


def rates(slopes):
    rate = [
        slopes[i][i] if i == j else slopes[i][j] + slopes[j][i] for i, j in index_pairs
    ]
    squares = [r * r for r in rate]
    straight = squares[0] + squares[1] + squares[2]
    crossed = squares[3] + squares[4] + squares[5]
    return rate, 0.5 * jnp.sqrt((straight + straight) + crossed)


def weighted(low, mid, high):
    return (low + high) + (mid + mid)


def filter_z(ln, u_ref, hz_ref, slot, k):
    at = ROWS * (k + 1)
    for comp in range(3):
        hz_ref[comp, slot, window(k)] = weighted(
            *[u_ref[comp, slot, ln.rows(at + step)] for step in (-1, 0, 1)]
        )


def strain(ln, u_ref, mag_ref, tmp_ref, keep_ref, slot, i, k):
    at = ROWS * (k + 1)
    mid = [u_ref[comp, i + 1, ln.rows(at)] for comp in range(3)]
    slopes = [
        (
            u_ref[comp, i + 2, ln.rows(at)] - u_ref[comp, i, ln.rows(at)],
            ln.slope_y(mid[comp]),
            ln.slope_z(u_ref[comp, i + 1, ln.rows(at + 1)], u_ref[comp, i + 1, ln.rows(at - 1)]),
        )
        for comp in range(3)
    ]
    rate, size = rates(slopes)
    mag_ref[i, window(k)] = size
    scaled = size * 0.0625
    quarter = [0.25 * m for m in mid]
    for n, (a, b) in enumerate(index_pairs):
        for at, value in ((n, scaled * rate[n]), (6 + n, quarter[a] * quarter[b])):
            tmp_ref[at, slot, window(k)] = value
            if k == 1:
                keep_ref[at, i] = value


def filter_products(ln, tmp_ref, fz_ref, slot, i, k):
    for n in range(12):
        fz_ref[n, i, window(k)] = weighted(
            *[tmp_ref[n, slot, ln.rows(ROWS * k + step)] for step in (0, 1, 2)]
        )


def filter_x(hz_ref, hu_ref, i, k):
    for comp in range(3):
        hu_ref[comp, i, window(k)] = 0.0625 * weighted(
            *[hz_ref[comp, i + step, window(k)] for step in (0, 1, 2)]
        )


def add_sums(ln, hu_ref, fz_ref, x, k, carry):
    numer, denom = carry
    at = 1 + ROWS * k
    mid = [hu_ref[comp, x + 1, ln.rows(at)] for comp in range(3)]
    slopes = [
        (
            hu_ref[comp, x + 2, ln.rows(at)] - hu_ref[comp, x, ln.rows(at)],
            ln.slope_y(mid[comp]),
            ln.slope_z(
                hu_ref[comp, x + 1, ln.rows(at + 1)], hu_ref[comp, x + 1, ln.rows(at - 1)]
            ),
        )
        for comp in range(3)
    ]
    rate, size = rates(slopes)
    size = 4.0 * size
    top, straight, crossed = [], [], []
    for n, (a, b) in enumerate(index_pairs):
        stress = weighted(*[fz_ref[n, x + step, window(k)] for step in (0, 1, 2)])
        product = weighted(*[fz_ref[6 + n, x + step, window(k)] for step in (0, 1, 2)])
        model = stress - size * rate[n]
        leonard = product - mid[a] * mid[b]
        top.append(leonard * model)
        (straight if a == b else crossed).append(model * model)
    numer = numer + ((top[0] + top[1]) + (top[2] + top[3]) + (top[4] + top[5]))
    denom = denom + (
        (straight[0] + straight[1] + straight[2])
        + 0.5 * (crossed[0] + crossed[1] + crossed[2])
    )
    return numer, denom


def strain_planes(ln, u_ref, mag_ref, tmp_ref, keep_ref, fz_ref, start, stop):
    windows = mag_ref.shape[1] // ROWS

    def plane(i):
        for k in range(1, windows):
            strain(ln, u_ref, mag_ref, tmp_ref, keep_ref, lax.rem(i, 2), i, k)

    def products(i):
        for k in range(1, windows - 1):
            filter_products(ln, tmp_ref, fz_ref, lax.rem(i, 2), i, k)

    def step(i, carry):
        products(i - 1)
        plane(i)
        return carry

    plane(start)
    lax.fori_loop(start + 1, stop, step, 0)
    products(stop - 1)


def sum_planes(ln, hu_ref, fz_ref, acc_ref, start, stop):
    def step(x, carry):
        for k in range(1, fz_ref.shape[2] // ROWS):
            carry = add_sums(ln, hu_ref, fz_ref, x, k, carry)
        return carry

    acc_ref[0], acc_ref[1] = lax.fori_loop(start, stop, step, (acc_ref[0], acc_ref[1]))


def interior_kernel(
    vel_ref, u_ref, keep_ref, fz_ref, hz_ref, hu_ref, mag_ref, acc_ref, tmp_ref
):
    nx = vel_ref.shape[1]
    windows = mag_ref.shape[1] // ROWS
    ln = Lanes(u_ref.shape[3])

    def fold(x, carry):
        for comp in range(3):
            store_plane(ln, u_ref, comp, WIDTH + x, vel_ref[comp, x])
        return carry

    lax.fori_loop(0, nx, fold, 0, unroll=2)

    def hat_z(x, carry):
        for k in range(1, windows):
            filter_z(ln, u_ref, hz_ref, WIDTH + x, k)
        return carry

    lax.fori_loop(0, nx, hat_z, 0)

    def hat_x(i, carry):
        for k in range(1, windows):
            filter_x(hz_ref, hu_ref, i, k)
        return carry

    lax.fori_loop(2, nx, hat_x, 0)
    strain_planes(ln, u_ref, mag_ref, tmp_ref, keep_ref, fz_ref, 2, nx)
    acc_ref[...] = jnp.zeros_like(acc_ref)
    sum_planes(ln, hu_ref, fz_ref, acc_ref, 2, nx - 2)


def fold_kernel(first_ref, second_ref, _, u_ref, edge_ref):
    planes = u_ref.shape[1]
    ln = Lanes(u_ref.shape[3])
    ordered = below_is_first("gx")
    for comp in range(3):
        for layer in range(WIDTH):
            first, second = first_ref[comp, layer], second_ref[comp, layer]
            below, above = jnp.where(ordered, first, second), jnp.where(ordered, second, first)
            store_plane(ln, u_ref, comp, layer, below)
            store_plane(ln, u_ref, comp, planes - WIDTH + layer, above)
    for comp in range(3):
        for slot in range(planes):
            for layer in range(WIDTH):
                to = WIDTH * (comp * planes + slot) + WIDTH - 1 - layer
                edge_ref[to : to + 1] = u_ref[comp, slot, ln.rows(TOP + layer, 1)]


def sides_kernel(
    u_ref, _1, _2, _3, _4, _5, _6,
    keep_ref, fz_ref, hz_ref, hu_ref, mag_ref, acc_ref, tmp_ref,
):
    planes = u_ref.shape[1]
    nx = planes - 2 * WIDTH
    windows = mag_ref.shape[1] // ROWS
    ln = Lanes(u_ref.shape[3])
    for start, stop in ((0, WIDTH), (planes - WIDTH, planes)):
        for slot in range(start, stop):
            for k in range(1, windows):
                filter_z(ln, u_ref, hz_ref, slot, k)
    for start, stop in ((0, 2), (nx, nx + 2)):
        for i in range(start, stop):
            for k in range(1, windows):
                filter_x(hz_ref, hu_ref, i, k)
        strain_planes(ln, u_ref, mag_ref, tmp_ref, keep_ref, fz_ref, start, stop)
    sum_planes(ln, hu_ref, fz_ref, acc_ref, 0, 2)
    sum_planes(ln, hu_ref, fz_ref, acc_ref, nx - 2, nx)


def rim_kernel(
    u_ref, first_ref, second_ref, keep_in, hu_in, mag_in, acc_in,
    mag_ref, sums_ref, near, turned, tmp, fz, hz, hu, mag,
):
    planes, _, lanes = u_ref.shape[1:]
    nx = planes - 2 * WIDTH
    ny = lanes // 2
    ln = Lanes(lanes)
    upper = lax.broadcasted_iota(jnp.int32, first_ref.shape, 1) >= ny
    take_first = jnp.logical_not(jnp.logical_xor(upper, below_is_first("gz")))
    turned[...] = pltpu.roll(jnp.where(take_first, first_ref[...], second_ref[...]), ny, 1)
    for comp in range(3):
        for slot in range(planes):
            at = WIDTH * (comp * planes + slot)
            near[comp, slot, ln.rows(TOP - WIDTH, WIDTH)] = turned[at : at + WIDTH]
            near[comp, slot, ln.rows(TOP)] = u_ref[comp, slot, ln.rows(TOP)]
    for slot in range(planes):
        filter_z(ln, near, hz, slot, 0)
    for i in range(nx + 2):
        strain(ln, near, mag, tmp, None, i, i, 0)
        for n in range(12):
            tmp[n, i, window(1)] = keep_in[n, i]
    for i in range(nx + 2):
        filter_x(hz, hu, i, 0)
        for comp in range(3):
            hu[comp, i, window(1)] = hu_in[comp, i, window(1)]
        filter_products(ln, tmp, fz, i, i, 0)
    carry = acc_in[0], acc_in[1]
    for x in range(nx):
        carry = add_sums(ln, hu, fz, x, 0, carry)
    numer, denom = [jnp.sum(part, axis=0, keepdims=True) for part in carry]
    numer = numer + pltpu.roll(numer, ny, 1)
    denom = denom + pltpu.roll(denom, ny, 1)
    both = jnp.where(lax.broadcasted_iota(jnp.int32, (1, lanes), 1) < ny, numer, denom)
    sums_ref[...] = jnp.broadcast_to(both, sums_ref.shape)
    half = mag_ref.shape[2] // 2
    for x in range(nx):
        mag[x + 1, window(1)] = mag_in[x + 1, window(1)]
        folded = jnp.concatenate(
            [mag[x + 1, ln.rows(1)]]
            + [mag_in[x + 1, ln.rows(1 + ROWS * k)] for k in range(1, half // ROWS)],
            axis=0,
        )
        mag_ref[x] = from_folded(folded)


def finish_kernel(cells, parts_ref, mag_ref, coefficient_ref, eddy_ref):
    lanes = parts_ref.shape[1]
    ny = lanes // 2
    sums = jnp.sum(parts_ref[...], axis=0, keepdims=True)
    numer = sums[:, :ny]
    denom = pltpu.roll(sums, ny, 1)[:, :ny]
    coefficient = numer / cells / (denom / cells + 1e-06)
    coefficient_ref[...] = coefficient
    column = jnp.broadcast_to(coefficient, (mag_ref.shape[2], ny)).T
    for x in range(mag_ref.shape[0]):
        eddy_ref[x] = column * mag_ref[x]


def call(kernel, name, shapes, operands, cycles, aliases=None, scratch=()):
    return pl.pallas_call(
        kernel,
        out_shape=tuple(jax.ShapeDtypeStruct(shape, jnp.float32) for shape in shapes),
        in_specs=[VMEM] * len(operands),
        out_specs=tuple(VMEM for _ in shapes),
        scratch_shapes=[pltpu.VMEM(shape, jnp.float32) for shape in scratch],
        input_output_aliases=aliases or {},
        compiler_params=SHARED,
        cost_estimate=pl.CostEstimate(
            flops=cycles * 4096, bytes_accessed=0, transcendentals=0
        ),
        name=name,
    )(*operands)


def on_device(velocity):
    nx, ny, nz = velocity.shape[1:]
    half, lanes = nz // 2, 2 * ny
    planes = nx + 2 * WIDTH
    tall, windowed = half + 3 * ROWS, half + ROWS
    u_shape = (3, planes, tall, lanes)
    work = (
        (12, nx + 2, ROWS, lanes),
        (12, nx + 2, half, lanes),
        (3, planes, windowed, lanes),
        (3, nx + 2, windowed, lanes),
        (nx + 2, windowed, lanes),
        (2, ROWS, lanes),
    )
    window_pair = ((12, 2, windowed, lanes),)
    sent = velocity[:, :WIDTH], velocity[:, nx - WIDTH :]
    first, second = swap_edges(*sent, "gx")
    u, *fields = call(
        interior_kernel, "interior", (u_shape, *work), (velocity,), 6000, scratch=window_pair
    )
    edge_shape = (3 * planes * WIDTH, lanes)
    u, edges = call(
        fold_kernel, "fold", (u_shape, edge_shape), (first, second, u), 800, {2: 0}
    )
    first, second = swap_edges(edges, edges, "gz")
    keep, _, _, hu, mag, acc = call(
        sides_kernel,
        "sides",
        work,
        (u, *fields),
        4000,
        {1 + n: n for n in range(6)},
        window_pair,
    )
    count = lax.axis_size("gx") * lax.axis_size("gz")
    magnitude, sums = call(
        rim_kernel,
        "rim",
        ((nx, ny, nz), (count, lanes)),
        (u, first, second, keep, hu, mag, acc),
        1000,
        scratch=(
            (3, planes, 3 * ROWS, lanes),
            edge_shape,
            (12, nx + 2, 2 * ROWS, lanes),
            (12, nx + 2, ROWS, lanes),
            (3, planes, ROWS, lanes),
            (3, nx + 2, 2 * ROWS, lanes),
            (nx + 2, 2 * ROWS, lanes),
        ),
    )
    parts = lax.all_to_all(sums, ("gx", "gz"), 0, 0, tiled=True)
    cells = nx * lax.axis_size("gx") * nz * lax.axis_size("gz")
    coefficient, eddy_viscosity = call(
        functools.partial(finish_kernel, cells),
        "finish",
        ((1, ny), (nx, ny, nz)),
        (parts, magnitude),
        500,
    )
    return (coefficient[0], eddy_viscosity)


def solution(mesh):
    in_specs = (P(None, "gx", None, "gz"),)
    out_specs = (P(), P("gx", None, "gz"))
    return jax.shard_map(
        on_device, mesh=mesh, in_specs=in_specs, out_specs=out_specs, check_vma=False
    )
```

time: 66.9 us -> 32.4 us (0.48)
  other arithmetic: 18.2 us -> 1.06 us
  waiting for transfers between devices: 16.3 us -> 2.26 us
  blocking collectives: 20.2 us -> 10.2 us
  Pallas kernels: 0 us -> 9.18 us
  local copies, waits for them, and re-layouts: 4.06 us -> 1.13 us
    psum x2 -> x0, blocking collectives: 20.2 us -> none  [the longest x1 11.8 us: on_device(): numer, denom = lax.psum((numer, denom), 'gx')]
    ppermute x4, waiting for transfers between devices: 16.3 us -> 2.26 us  [the longest x2 2.02 us: swap_edges(): near = lax.ppermute(near_send, axis, near_pairs)]
    all_to_all x0 -> x1, blocking collectives: none -> 10.2 us  [on_device(): parts = lax.all_to_all(sums, ('gx', 'gz'), 0, 0, tiled=True)]
    mul x14 -> x0, other arithmetic: 9.9 us -> none  [the longest x2 2.25 us: along_y(): middle = 0.5 * (inside[..., 2:, :] - inside[..., :-2, :])]
    pallas_call x0 -> x5, Pallas kernels: none -> 9.18 us  [call(): pl.pallas_call(kernel, out_shape=tuple((jax.ShapeDtypeStruct(shape, jnp.f...]
    sub x2 -> x0, other arithmetic: 4.1 us -> none  [along_y(): bottom = inside[..., 1:2, :] - inside[..., 0:1, :]]
    unnamed x10 -> x2, local copies, waits for them, and re-layouts: 4.01 us -> 1.13 us
    reduce_sum x3 -> x0, other arithmetic: 2.17 us -> none  [the longest x2 1.15 us: strain(): jnp.sum(weights * strain_rate * strain_rate, axis=0)]
  transfers between devices with their start and end apart: 4 -> 4, of which waited for: 4 -> 2; matrix products, arithmetic and copies ran while one was open for 0% -> 0% of each run, Pallas kernels for 0% -> 18%
where the time goes in v3:
time: 32.4 us; the launch traced here: 32.3 us
  blocking collectives  10.2 us (31%)
  Pallas kernels  9.18 us (28%)
  starting transfers between devices  7.71 us (24%)
  waiting for transfers between devices  2.26 us (7%)
  local copies, waits for them, and re-layouts  1.13 us (3%)
  other arithmetic  1.06 us (3%)
  between operations  0.69 us (2%)
    all_to_all x1, blocking collectives, on_device(): parts = lax.all_to_all(sums, ('gx', 'gz'), 0, 0, tiled=True)  10.2 us
    pallas_call x5, Pallas kernels, call(): pl.pallas_call(kernel, out_shape=tuple((jax.ShapeDtypeStruct(shape, jnp.f...  9.18 us
    ppermute x2, starting transfers between devices, swap_edges(): far = lax.ppermute(far_send, axis, far_pairs)  7.71 us
    ppermute x2, waiting for transfers between devices, swap_edges(): near = lax.ppermute(near_send, axis, near_pairs)  2.02 us
    unnamed x2, local copies, waits for them, and re-layouts  1.13 us
    select_n x1, other arithmetic, swap_edges(): far_send = jnp.where(odd, for_above, for_below)  1.06 us
  transfers between devices with their start and end apart: 4, of which 2 were waited for; matrix products, arithmetic and copies ran while one was open for 0% of the time, Pallas kernels for 18%

profile of v3, /device:TPU:0, one launch (start us, length us, event | category | flops | bytes accessed | tf_op | source)
XLA Modules:
  0.0 32.3 jit_solution(5877565508666171464)
XLA Ops:
  0.6 1.1 %slice_select_fusion = (f32[3,2,64,128]{3,2,1,0:T(8,128)S(1)}, f32[3,2,64,128]{3,2,1,0:T(8,128)S(1)}) fusion(f32[3,8,64,128]{3,2,1,0:T(8,128)} %vel_ref.1, pred[]{:T(512)S(6)} %eq.5), kind=kLoop, calls=%fused_computation | loop fusion | flops 98304 | bytes 786433 | tf_op jit(solution)/shard_map/jit(_where)/select_n | solution.py:39
  1.7 3.4 %collective-permute-start.1 = (f32[3,2,64,128]{3,2,1,0:T(8,128)S(1)}, f32[3,2,64,128]{3,2,1,0:T(8,128)S(1)}, u32[]{:S(2)}, u32[]{:S(2)}) collective-permute-start(f32[3,2,64,128]{3,2,1,0:T(8,128)S(1)} %get-tuple-element.36), channel_id=1, source_target_pairs={{0,28},{4,8},{8,4},{12,16},{16,12},{20,24},{24,20},{28,0},{1,29},{... | collective-permute-start | bytes 589832 | tf_op jit(solution)/shard_map/ppermute | solution.py:41
  5.1 0.0 collective-permute-start
  5.1 0.0 copy-start
  5.1 1.1 %copy-done = f32[3,8,64,128]{3,2,1,0:T(8,128)S(1)} copy-done((f32[3,8,64,128]{3,2,1,0:T(8,128)S(1)}, f32[3,8,64,128]{3,2,1,0:T(8,128)}, u32[]{:S(2)}) %copy-start) | copy-done | bytes 786456
  6.3 4.3 %interior.1 = (f32[3,12,88,128]{3,2,1,0:T(8,128)S(1)}, f32[12,10,8,128]{3,2,1,0:T(8,128)S(1)}, f32[12,10,64,128]{3,2,1,0:T(8,128)S(1)}, f32[3,12,72,128]{3,2,1,0...) custom-call(f32[3,8,64,128]{3,2,1,0:T(8,128)S(1)} %copy-done), custom_call_target="tpu_custom_call" | custom-call | flops 24576000 | tf_op jit(solution)/shard_map/interior/pallas_call | solution.py:358
  10.6 0.0 collective-permute-done.1.second_ref
  10.6 0.0 collective-permute-done.first_ref
  10.6 1.3 %fold.1 = (f32[3,12,88,128]{3,2,1,0:T(8,128)S(1)}, f32[72,128]{1,0:T(8,128)S(1)}) custom-call(f32[3,2,64,128]{3,2,1,0:T(8,128)S(1)} %collective-permute-done.first_ref, f32[3,2,64,128]{3,2,1,0:T(8,128)S(1)} %collective-permute-done.1.second_ref, f32[3,12,88,128]{3,2,1,0:T(8,128)S(1)} %get-tuple-element.19._), custom_call_target="tpu_custom_call", output_to_operand_aliasing={{0}: (2, {})} | custom-call | flops 3276800 | tf_op jit(solution)/shard_map/fold/pallas_call | solution.py:358
  11.9 4.3 %collective-permute-start.3 = (f32[72,128]{1,0:T(8,128)S(1)}, f32[72,128]{1,0:T(8,128)S(1)}, u32[]{:S(2)}, u32[]{:S(2)}) collective-permute-start(f32[72,128]{1,0:T(8,128)S(1)} %get-tuple-element.21), channel_id=1, source_target_pairs={{0,3},{1,2},{2,1},{3,0},{4,7},{5,6},{6,5},{7,4},{8,11},{9,10},{10,... | collective-permute-start | bytes 110600 | tf_op jit(solution)/shard_map/ppermute | solution.py:41
  16.2 0.0 collective-permute-start.2
  16.2 1.7 %sides.1 = (f32[12,10,8,128]{3,2,1,0:T(8,128)S(1)}, f32[12,10,64,128]{3,2,1,0:T(8,128)S(1)}, f32[3,12,72,128]{3,2,1,0:T(8,128)S(1)}, f32[3,10,72,128]{3,2,1,0:T(...) custom-call(f32[3,12,88,128]{3,2,1,0:T(8,128)S(1)} %get-tuple-elemen, ...), custom_call_target="tpu_custom_call", output_to_operand_aliasing={{0}: (1, {}), {1}: (2, {}), {2}: (3, {}), {3}: (4, {}), {4}... | custom-call | flops 16384000 | tf_op jit(solution)/shard_map/sides/pallas_call | solution.py:358
  17.9 0.2 collective-permute-done.3.second_ref
  18.1 2.0 %collective-permute-done.2.first_ref = f32[72,128]{1,0:T(8,128)S(1)} collective-permute-done((f32[72,128]{1,0:T(8,128)S(1)}, f32[72,128]{1,0:T(8,128)S(1)}, u32[]{:S(2)}, u32[]{:S(2)}) %collective-permute-start.2) | collective-permute-done | bytes 36896 | tf_op jit(solution)/shard_map/ppermute | solution.py:42
  20.1 1.0 %rim.1 = (f32[8,64,128]{2,1,0:T(8,128)S(1)}, f32[32,128]{1,0:T(8,128)S(1)}) custom-call(f32[3,12,88,128]{3,2,1,0:T(8,128)S(1)} %get-tuple-element.20.u_ref, f32[72,128]{1,0:T(8,128)S(1)} %collective-permute-done.2.first_ref, f32[72,128]{1,0:T(8,128)S(1)} %collective-permute-done.3.second_ref, f32[12,10,8,128]{3,2,1,0:T(8,128)S(1)} %get-tuple-element.28.keep_in, ...), custom_call_target="tpu_custom_call" | custom-call | flops 4096000 | tf_op jit(solution)/shard_map/rim/pallas_call | solution.py:358
  21.2 10.2 %all_to_all.11 = f32[32,1,128]{2,1,0:T(1,128)S(1)} all-to-all(f32[32,1,128]{2,1,0:T(1,128)S(1)} %bitcast.6), channel_id=1, replica_groups=mesh['gx'=8,'gz'=4] {'gx','gz'}, dimensions={0} | all-to-all | bytes 32768 | tf_op jit(solution)/shard_map/all_to_all | solution.py:424
  31.4 0.9 %finish.1 = (f32[1,64]{1,0:T(1,128)}, f32[8,64,128]{2,1,0:T(8,128)}) custom-call(f32[32,128]{1,0:T(8,128)S(1)} %bitcast.5, f32[8,64,128]{2,1,0:T(8,128)S(1)} %get-tuple-element.33.mag_ref), custom_call_target="tpu_custom_call" | custom-call | flops 2048000 | tf_op jit(solution)/shard_map/finish/pallas_call | solution.py:358
Async XLA Ops:
  1.7 8.9 %collective-permute-start.1 = (f32[3,2,64,128]{3,2,1,0:T(8,128)S(1)}, f32[3,2,64,128]{3,2,1,0:T(8,128)S(1)}, u32[]{:S(2)}, u32[]{:S(2)}) collective-permute-start(f32[3,2,64,128]{3,2,1,0:T(8,128)S(1)} %get-tuple-element.36), channel_id=1, source_target_pairs={{0,28},{4,8},{8,4},{12,16},{16,12},{20,24},{24,20},{28,0},{1,29},{... | collective-permute-start | bytes 589832 | tf_op jit(solution)/shard_map/ppermute | solution.py:41
  5.1 5.4 %collective-permute-start = (f32[3,2,64,128]{3,2,1,0:T(8,128)S(1)}, f32[3,2,64,128]{3,2,1,0:T(8,128)S(1)}, u32[]{:S(2)}, u32[]{:S(2)}) collective-permute-start(f32[3,2,64,128]{3,2,1,0:T(8,128)S(1)} %get-tuple-element.37), channel_id=1, source_target_pairs={{0,4},{4,0},{8,12},{12,8},{16,20},{20,16},{24,28},{28,24},{1,5},{5... | collective-permute-start | bytes 589832 | tf_op jit(solution)/shard_map/ppermute | solution.py:42
  5.1 1.1 %copy-start = (f32[3,8,64,128]{3,2,1,0:T(8,128)S(1)}, f32[3,8,64,128]{3,2,1,0:T(8,128)}, u32[]{:S(2)}) copy-start(f32[3,8,64,128]{3,2,1,0:T(8,128)} %vel_ref.1) | copy-start | bytes 2359300
  11.9 6.2 %collective-permute-start.3 = (f32[72,128]{1,0:T(8,128)S(1)}, f32[72,128]{1,0:T(8,128)S(1)}, u32[]{:S(2)}, u32[]{:S(2)}) collective-permute-start(f32[72,128]{1,0:T(8,128)S(1)} %get-tuple-element.21), channel_id=1, source_target_pairs={{0,3},{1,2},{2,1},{3,0},{4,7},{5,6},{6,5},{7,4},{8,11},{9,10},{10,... | collective-permute-start | bytes 110600 | tf_op jit(solution)/shard_map/ppermute | solution.py:41
  16.2 4.0 %collective-permute-start.2 = (f32[72,128]{1,0:T(8,128)S(1)}, f32[72,128]{1,0:T(8,128)S(1)}, u32[]{:S(2)}, u32[]{:S(2)}) collective-permute-start(f32[72,128]{1,0:T(8,128)S(1)} %get-tuple-element.21), channel_id=1, source_target_pairs={{0,1},{1,0},{2,3},{3,2},{4,5},{5,4},{6,7},{7,6},{8,9},{9,8},{10,11... | collective-permute-start | bytes 110600 | tf_op jit(solution)/shard_map/ppermute | solution.py:42

commit v4 on v3

--- a/solution.py
+++ b/solution.py
@@ -11,7 +11,6 @@
 ROWS = 8
 index_pairs = ((0, 0), (1, 1), (2, 2), (0, 1), (0, 2), (1, 2))
 TOP = 9
-SHARED = pltpu.CompilerParams(vmem_limit_bytes=8 * 1024 * 1024)
 
 VMEM = pl.BlockSpec(memory_space=pltpu.VMEM)
 
@@ -22,25 +21,15 @@
     return far, near
 
 
-def swap_edges(for_below, for_above, axis):
+def swap_edges(first, second, axis):
     count = lax.axis_size(axis)
     if count % 2:
         forward = [(i, (i + 1) % count) for i in range(count)]
         backward = [(target, source) for source, target in forward]
-        return (
-            lax.ppermute(for_above, axis, forward),
-            lax.ppermute(for_below, axis, backward),
-        )
+        return lax.ppermute(first, axis, forward), lax.ppermute(second, axis, backward)
     far_pairs, near_pairs = swap_pairs(count)
-    if for_below is for_above:
-        near_send = far_send = for_below
-    else:
-        odd = lax.axis_index(axis) % 2 == 1
-        far_send = jnp.where(odd, for_above, for_below)
-        near_send = jnp.where(odd, for_below, for_above)
-    far = lax.ppermute(far_send, axis, far_pairs)
-    near = lax.ppermute(near_send, axis, near_pairs)
-    return near, far
+    far = lax.ppermute(second, axis, far_pairs)
+    return lax.ppermute(first, axis, near_pairs), far
 
 
 def below_is_first(axis):
@@ -49,15 +38,20 @@
     return lax.rem(lax.axis_index(axis), 2) == 1
 
 
+def first_goes_below(axis):
+    if lax.axis_size(axis) % 2:
+        return False
+    return below_is_first(axis)
+
+
 def mirrored(plane):
     lanes = plane.shape[1]
     lane = lax.broadcasted_iota(jnp.int32, plane.shape, 1)
     return jnp.take_along_axis(plane, lanes - 1 - lane, axis=1)
 
 
-def to_folded(plane):
-    half = plane.shape[1] // 2
-    return jnp.concatenate([plane[:, :half], mirrored(plane)[:, :half]], axis=0).T
+def to_folded(plane, rows):
+    return jnp.concatenate([plane[:, :rows], mirrored(plane)[:, :rows]], axis=0).T
 
 
 def from_folded(folded):
@@ -96,13 +90,10 @@
 
 
 def store_plane(ln, u_ref, comp, slot, plane):
-    folded = to_folded(plane)
-    half, lanes = folded.shape
-    for k in range(half // ROWS):
+    count = plane.shape[1] // 2 + ROWS
+    folded = to_folded(plane, count)
+    for k in range(count // ROWS):
         u_ref[comp, slot, ln.rows(TOP + ROWS * k)] = folded[ROWS * k : ROWS * (k + 1)]
-    inner = pltpu.roll(folded[half - ROWS :], lanes // 2, 1)
-    for layer in range(WIDTH):
-        u_ref[comp, slot, ln.rows(TOP + half + layer, 1)] = inner[ROWS - 1 - layer : ROWS - layer]
 
 
 def rates(slopes):
@@ -146,7 +137,7 @@
         for at, value in ((n, scaled * rate[n]), (6 + n, quarter[a] * quarter[b])):
             tmp_ref[at, slot, window(k)] = value
             if k == 1:
-                keep_ref[at, i] = value
+                keep_ref[at, i, window(1)] = value
 
 
 def filter_products(ln, tmp_ref, fz_ref, slot, i, k):
@@ -267,11 +258,20 @@
             below, above = jnp.where(ordered, first, second), jnp.where(ordered, second, first)
             store_plane(ln, u_ref, comp, layer, below)
             store_plane(ln, u_ref, comp, planes - WIDTH + layer, above)
+    edges = []
     for comp in range(3):
         for slot in range(planes):
+            edges.append((comp, slot))
+    row = lax.broadcasted_iota(jnp.int32, (ROWS, edge_ref.shape[1]), 0)
+    per_window = ROWS // WIDTH
+    for at in range(0, len(edges), per_window):
+        packed = None
+        for n, (comp, slot) in enumerate(edges[at : at + per_window]):
             for layer in range(WIDTH):
-                to = WIDTH * (comp * planes + slot) + WIDTH - 1 - layer
-                edge_ref[to : to + 1] = u_ref[comp, slot, ln.rows(TOP + layer, 1)]
+                to = WIDTH * n + WIDTH - 1 - layer
+                rows = u_ref[comp, slot, ln.rows(TOP + layer - to)]
+                packed = rows if packed is None else jnp.where(row == to, rows, packed)
+        edge_ref[window(at // per_window)] = packed
 
 
 def sides_kernel(
@@ -296,49 +296,42 @@
 
 
 def rim_kernel(
-    u_ref, first_ref, second_ref, keep_in, hu_in, mag_in, acc_in,
-    mag_ref, sums_ref, near, turned, tmp, fz, hz, hu, mag,
+    first_ref, second_ref, _1, _2, _3, _4, acc_ref, u_ref, tmp_ref, hu_ref, mag_ref,
+    plain_ref, sums_ref, turned, fz, hz,
 ):
     planes, _, lanes = u_ref.shape[1:]
     nx = planes - 2 * WIDTH
     ny = lanes // 2
+    half = plain_ref.shape[2] // 2
     ln = Lanes(lanes)
+    count = first_ref.shape[0]
     upper = lax.broadcasted_iota(jnp.int32, first_ref.shape, 1) >= ny
     take_first = jnp.logical_not(jnp.logical_xor(upper, below_is_first("gz")))
-    turned[...] = pltpu.roll(jnp.where(take_first, first_ref[...], second_ref[...]), ny, 1)
+    turned[ROWS : ROWS + count] = pltpu.roll(
+        jnp.where(take_first, first_ref[...], second_ref[...]), ny, 1
+    )
     for comp in range(3):
         for slot in range(planes):
-            at = WIDTH * (comp * planes + slot)
-            near[comp, slot, ln.rows(TOP - WIDTH, WIDTH)] = turned[at : at + WIDTH]
-            near[comp, slot, ln.rows(TOP)] = u_ref[comp, slot, ln.rows(TOP)]
+            at = WIDTH * (comp * planes + slot + 1)
+            u_ref[comp, slot, ln.rows(TOP - ROWS)] = turned[ln.rows(at)]
     for slot in range(planes):
-        filter_z(ln, near, hz, slot, 0)
+        filter_z(ln, u_ref, hz, slot, 0)
     for i in range(nx + 2):
-        strain(ln, near, mag, tmp, None, i, i, 0)
-        for n in range(12):
-            tmp[n, i, window(1)] = keep_in[n, i]
+        filter_x(hz, hu_ref, i, 0)
     for i in range(nx + 2):
-        filter_x(hz, hu, i, 0)
-        for comp in range(3):
-            hu[comp, i, window(1)] = hu_in[comp, i, window(1)]
-        filter_products(ln, tmp, fz, i, i, 0)
-    carry = acc_in[0], acc_in[1]
+        strain(ln, u_ref, mag_ref, tmp_ref, None, i, i, 0)
+    for i in range(nx + 2):
+        filter_products(ln, tmp_ref, fz, i, i, 0)
+    carry = acc_ref[0], acc_ref[1]
     for x in range(nx):
-        carry = add_sums(ln, hu, fz, x, 0, carry)
+        carry = add_sums(ln, hu_ref, fz, x, 0, carry)
     numer, denom = [jnp.sum(part, axis=0, keepdims=True) for part in carry]
     numer = numer + pltpu.roll(numer, ny, 1)
     denom = denom + pltpu.roll(denom, ny, 1)
     both = jnp.where(lax.broadcasted_iota(jnp.int32, (1, lanes), 1) < ny, numer, denom)
     sums_ref[...] = jnp.broadcast_to(both, sums_ref.shape)
-    half = mag_ref.shape[2] // 2
     for x in range(nx):
-        mag[x + 1, window(1)] = mag_in[x + 1, window(1)]
-        folded = jnp.concatenate(
-            [mag[x + 1, ln.rows(1)]]
-            + [mag_in[x + 1, ln.rows(1 + ROWS * k)] for k in range(1, half // ROWS)],
-            axis=0,
-        )
-        mag_ref[x] = from_folded(folded)
+        plain_ref[x] = from_folded(mag_ref[x + 1, ln.rows(1, half)])
 
 
 def finish_kernel(cells, parts_ref, mag_ref, coefficient_ref, eddy_ref):
@@ -354,15 +347,19 @@
         eddy_ref[x] = column * mag_ref[x]
 
 
-def call(kernel, name, shapes, operands, cycles, aliases=None, scratch=()):
+def call(
+    kernel, name, shapes, operands, cycles, aliases=None, scratch=()
+):
     return pl.pallas_call(
         kernel,
         out_shape=tuple(jax.ShapeDtypeStruct(shape, jnp.float32) for shape in shapes),
         in_specs=[VMEM] * len(operands),
         out_specs=tuple(VMEM for _ in shapes),
-        scratch_shapes=[pltpu.VMEM(shape, jnp.float32) for shape in scratch],
+        scratch_shapes=[
+            pltpu.VMEM(item, jnp.float32) if isinstance(item, tuple) else item for item in scratch
+        ],
         input_output_aliases=aliases or {},
-        compiler_params=SHARED,
+        compiler_params=pltpu.CompilerParams(vmem_limit_bytes=8 * 1024 * 1024),
         cost_estimate=pl.CostEstimate(
             flops=cycles * 4096, bytes_accessed=0, transcendentals=0
         ),
@@ -377,7 +374,7 @@
     tall, windowed = half + 3 * ROWS, half + ROWS
     u_shape = (3, planes, tall, lanes)
     work = (
-        (12, nx + 2, ROWS, lanes),
+        (12, nx + 2, 2 * ROWS, lanes),
         (12, nx + 2, half, lanes),
         (3, planes, windowed, lanes),
         (3, nx + 2, windowed, lanes),
@@ -385,8 +382,10 @@
         (2, ROWS, lanes),
     )
     window_pair = ((12, 2, windowed, lanes),)
-    sent = velocity[:, :WIDTH], velocity[:, nx - WIDTH :]
-    first, second = swap_edges(*sent, "gx")
+    low, high = velocity[:, :WIDTH], velocity[:, nx - WIDTH :]
+    flag = first_goes_below("gx")
+    first, second = jnp.where(flag, low, high), jnp.where(flag, high, low)
+    first, second = swap_edges(first, second, "gx")
     u, *fields = call(
         interior_kernel, "interior", (u_shape, *work), (velocity,), 6000, scratch=window_pair
     )
@@ -405,20 +404,17 @@
         window_pair,
     )
     count = lax.axis_size("gx") * lax.axis_size("gz")
-    magnitude, sums = call(
+    *_, magnitude, sums = call(
         rim_kernel,
         "rim",
-        ((nx, ny, nz), (count, lanes)),
-        (u, first, second, keep, hu, mag, acc),
+        (u_shape, work[0], work[3], work[4], (nx, ny, nz), (count, lanes)),
+        (first, second, u, keep, hu, mag, acc),
         1000,
+        {2 + n: n for n in range(4)},
         scratch=(
-            (3, planes, 3 * ROWS, lanes),
-            edge_shape,
-            (12, nx + 2, 2 * ROWS, lanes),
+            (ROWS + edge_shape[0], lanes),
             (12, nx + 2, ROWS, lanes),
             (3, planes, ROWS, lanes),
-            (3, nx + 2, 2 * ROWS, lanes),
-            (nx + 2, 2 * ROWS, lanes),
         ),
     )
     parts = lax.all_to_all(sums, ("gx", "gz"), 0, 0, tiled=True)

time: 32.4 us -> 31.5 us (0.972)
  Pallas kernels: 9.18 us -> 6.93 us
  starting transfers between devices: 7.71 us -> 8.6 us
  waiting for transfers between devices: 2.26 us -> 2.72 us
    pallas_call x5, Pallas kernels: 9.18 us -> 6.93 us  [call(): pl.pallas_call(kernel, out_shape=tuple((jax.ShapeDtypeStruct(shape, jnp.f...]
    ppermute x4, starting transfers between devices: 7.71 us -> 8.6 us  [the longest x2 8.6 us: swap_edges(): far = lax.ppermute(second, axis, far_pairs)]
    ppermute x4, waiting for transfers between devices: 2.26 us -> 2.72 us  [the longest x2 2.02 us: swap_edges(): return (lax.ppermute(first, axis, near_pairs), far)]
  transfers between devices with their start and end apart: 4 -> 4, of which waited for: 2 -> 3; matrix products, arithmetic and copies ran while one was open for 0% -> 0% of each run, Pallas kernels for 18% -> 15%
where the time goes in v4:
time: 31.5 us; the launch traced here: 31.3 us
  blocking collectives  10.2 us (32%)
  starting transfers between devices  8.6 us (27%)
  Pallas kernels  6.93 us (22%)
  waiting for transfers between devices  2.72 us (9%)
  local copies, waits for them, and re-layouts  1.13 us (4%)
  other arithmetic  1.06 us (3%)
  between operations  0.67 us (2%)
    all_to_all x1, blocking collectives, on_device(): parts = lax.all_to_all(sums, ('gx', 'gz'), 0, 0, tiled=True)  10.2 us
    ppermute x2, starting transfers between devices, swap_edges(): far = lax.ppermute(second, axis, far_pairs)  8.6 us
    pallas_call x5, Pallas kernels, call(): pl.pallas_call(kernel, out_shape=tuple((jax.ShapeDtypeStruct(shape, jnp.f...  6.93 us
    ppermute x2, waiting for transfers between devices, swap_edges(): return (lax.ppermute(first, axis, near_pairs), far)  2.02 us
    unnamed x2, local copies, waits for them, and re-layouts  1.13 us
    select_n x1, other arithmetic, on_device(): first, second = (jnp.where(flag, low, high), jnp.where(flag, high, low))  1.06 us
    ppermute x2, waiting for transfers between devices, swap_edges(): far = lax.ppermute(second, axis, far_pairs)  0.7 us
  transfers between devices with their start and end apart: 4, of which 3 were waited for; matrix products, arithmetic and copies ran while one was open for 0% of the time, Pallas kernels for 15%

profile of v4, /device:TPU:0, one launch (start us, length us, event | category | flops | bytes accessed | tf_op | source)
XLA Modules:
  0.0 31.3 jit_solution(230490048112019610)
XLA Ops:
  0.6 1.1 %slice_select_fusion = (f32[3,2,64,128]{3,2,1,0:T(8,128)S(1)}, f32[3,2,64,128]{3,2,1,0:T(8,128)S(1)}) fusion(f32[3,8,64,128]{3,2,1,0:T(8,128)} %vel_ref.1, pred[]{:T(512)S(6)} %eq.3), kind=kLoop, calls=%fused_computation | loop fusion | flops 98304 | bytes 786433 | tf_op jit(solution)/shard_map/jit(_where)/select_n | solution.py:387
  1.7 3.4 %collective-permute-start.1 = (f32[3,2,64,128]{3,2,1,0:T(8,128)S(1)}, f32[3,2,64,128]{3,2,1,0:T(8,128)S(1)}, u32[]{:S(2)}, u32[]{:S(2)}) collective-permute-start(f32[3,2,64,128]{3,2,1,0:T(8,128)S(1)} %get-tuple-element.36), channel_id=1, source_target_pairs={{0,28},{4,8},{8,4},{12,16},{16,12},{20,24},{24,20},{28,0},{1,29},{... | collective-permute-start | bytes 589832 | tf_op jit(solution)/shard_map/ppermute | solution.py:31
  5.1 0.0 collective-permute-start
  5.1 0.0 copy-start
  5.1 1.1 %copy-done = f32[3,8,64,128]{3,2,1,0:T(8,128)S(1)} copy-done((f32[3,8,64,128]{3,2,1,0:T(8,128)S(1)}, f32[3,8,64,128]{3,2,1,0:T(8,128)}, u32[]{:S(2)}) %copy-start) | copy-done | bytes 786456
  6.3 3.0 %interior.1 = (f32[3,12,88,128]{3,2,1,0:T(8,128)S(1)}, f32[12,10,16,128]{3,2,1,0:T(8,128)S(1)}, f32[12,10,64,128]{3,2,1,0:T(8,128)S(1)}, f32[3,12,72,128]{3,2,1,...) custom-call(f32[3,8,64,128]{3,2,1,0:T(8,128)S(1)} %copy-done), custom_call_target="tpu_custom_call" | custom-call | flops 24576000 | tf_op jit(solution)/shard_map/interior/pallas_call | solution.py:353
  9.3 0.5 %collective-permute-done.1.second_ref = f32[3,2,64,128]{3,2,1,0:T(8,128)S(1)} collective-permute-done((f32[3,2,64,128]{3,2,1,0:T(8,128)S(1)}, f32[3,2,64,128]{3,2,1,0:T(8,128)S(1)}, u32[]{:S(2)}, u32[]{:S(2)}) %collective-permute-start.1) | collective-permute-done | bytes 196640 | tf_op jit(solution)/shard_map/ppermute | solution.py:31
  9.7 0.0 collective-permute-done.first_ref
  9.7 0.4 %fold.1 = (f32[3,12,88,128]{3,2,1,0:T(8,128)S(1)}, f32[72,128]{1,0:T(8,128)S(1)}) custom-call(f32[3,2,64,128]{3,2,1,0:T(8,128)S(1)} %collective-permute-done.first_ref, f32[3,2,64,128]{3,2,1,0:T(8,128)S(1)} %collective-permute-done.1.second_ref, f32[3,12,88,128]{3,2,1,0:T(8,128)S(1)} %get-tuple-element.19._), custom_call_target="tpu_custom_call", output_to_operand_aliasing={{0}: (2, {})} | custom-call | flops 3276800 | tf_op jit(solution)/shard_map/fold/pallas_call | solution.py:353
  10.1 5.2 %collective-permute-start.3 = (f32[72,128]{1,0:T(8,128)S(1)}, f32[72,128]{1,0:T(8,128)S(1)}, u32[]{:S(2)}, u32[]{:S(2)}) collective-permute-start(f32[72,128]{1,0:T(8,128)S(1)} %get-tuple-element.20), channel_id=1, source_target_pairs={{0,3},{1,2},{2,1},{3,0},{4,7},{5,6},{6,5},{7,4},{8,11},{9,10},{10,... | collective-permute-start | bytes 110600 | tf_op jit(solution)/shard_map/ppermute | solution.py:31
  15.3 0.0 collective-permute-start.2
  15.3 1.7 %sides.1 = (f32[12,10,16,128]{3,2,1,0:T(8,128)S(1)}, f32[12,10,64,128]{3,2,1,0:T(8,128)S(1)}, f32[3,12,72,128]{3,2,1,0:T(8,128)S(1)}, f32[3,10,72,128]{3,2,1,0:T...) custom-call(f32[3,12,88,128]{3,2,1,0:T(8,128)S(1)} %get-tuple-elemen, ...), custom_call_target="tpu_custom_call", output_to_operand_aliasing={{0}: (1, {}), {1}: (2, {}), {2}: (3, {}), {3}: (4, {}), {4}... | custom-call | flops 16384000 | tf_op jit(solution)/shard_map/sides/pallas_call | solution.py:353
  17.0 0.2 collective-permute-done.3.second_ref
  17.2 2.0 %collective-permute-done.2.first_ref = f32[72,128]{1,0:T(8,128)S(1)} collective-permute-done((f32[72,128]{1,0:T(8,128)S(1)}, f32[72,128]{1,0:T(8,128)S(1)}, u32[]{:S(2)}, u32[]{:S(2)}) %collective-permute-start.2) | collective-permute-done | bytes 36896 | tf_op jit(solution)/shard_map/ppermute | solution.py:32
  19.3 1.0 %rim.1 = (f32[3,12,88,128]{3,2,1,0:T(8,128)S(1)}, f32[12,10,16,128]{3,2,1,0:T(8,128)S(1)}, f32[3,10,72,128]{3,2,1,0:T(8,128)S(1)}, f32[10,72,128]{2,1,0:T(8,128)...) custom-call(f32[72,128]{1,0:T(8,128)S(1)} %collective-permute-done.2, ...), custom_call_target="tpu_custom_call", output_to_operand_aliasing={{0}: (2, {}), {1}: (3, {}), {2}: (4, {}), {3}: (5, {})} | custom-call | flops 4096000 | tf_op jit(solution)/shard_map/rim/pallas_call | solution.py:353
  20.2 10.2 %all_to_all.11 = f32[32,1,128]{2,1,0:T(1,128)S(1)} all-to-all(f32[32,1,128]{2,1,0:T(1,128)S(1)} %bitcast.6), channel_id=1, replica_groups=mesh['gx'=8,'gz'=4] {'gx','gz'}, dimensions={0} | all-to-all | bytes 32768 | tf_op jit(solution)/shard_map/all_to_all | solution.py:420
  30.5 0.9 %finish.1 = (f32[1,64]{1,0:T(1,128)}, f32[8,64,128]{2,1,0:T(8,128)}) custom-call(f32[32,128]{1,0:T(8,128)S(1)} %bitcast.5, f32[8,64,128]{2,1,0:T(8,128)S(1)} %get-tuple-element.33.mag_ref), custom_call_target="tpu_custom_call" | custom-call | flops 2048000 | tf_op jit(solution)/shard_map/finish/pallas_call | solution.py:353
Async XLA Ops:
  1.7 8.0 %collective-permute-start.1 = (f32[3,2,64,128]{3,2,1,0:T(8,128)S(1)}, f32[3,2,64,128]{3,2,1,0:T(8,128)S(1)}, u32[]{:S(2)}, u32[]{:S(2)}) collective-permute-start(f32[3,2,64,128]{3,2,1,0:T(8,128)S(1)} %get-tuple-element.36), channel_id=1, source_target_pairs={{0,28},{4,8},{8,4},{12,16},{16,12},{20,24},{24,20},{28,0},{1,29},{... | collective-permute-start | bytes 589832 | tf_op jit(solution)/shard_map/ppermute | solution.py:31
  5.1 4.6 %collective-permute-start = (f32[3,2,64,128]{3,2,1,0:T(8,128)S(1)}, f32[3,2,64,128]{3,2,1,0:T(8,128)S(1)}, u32[]{:S(2)}, u32[]{:S(2)}) collective-permute-start(f32[3,2,64,128]{3,2,1,0:T(8,128)S(1)} %get-tuple-element.37), channel_id=1, source_target_pairs={{0,4},{4,0},{8,12},{12,8},{16,20},{20,16},{24,28},{28,24},{1,5},{5... | collective-permute-start | bytes 589832 | tf_op jit(solution)/shard_map/ppermute | solution.py:32
  5.1 1.1 %copy-start = (f32[3,8,64,128]{3,2,1,0:T(8,128)S(1)}, f32[3,8,64,128]{3,2,1,0:T(8,128)}, u32[]{:S(2)}) copy-start(f32[3,8,64,128]{3,2,1,0:T(8,128)} %vel_ref.1) | copy-start | bytes 2359300
  10.1 7.1 %collective-permute-start.3 = (f32[72,128]{1,0:T(8,128)S(1)}, f32[72,128]{1,0:T(8,128)S(1)}, u32[]{:S(2)}, u32[]{:S(2)}) collective-permute-start(f32[72,128]{1,0:T(8,128)S(1)} %get-tuple-element.20), channel_id=1, source_target_pairs={{0,3},{1,2},{2,1},{3,0},{4,7},{5,6},{6,5},{7,4},{8,11},{9,10},{10,... | collective-permute-start | bytes 110600 | tf_op jit(solution)/shard_map/ppermute | solution.py:31
  15.3 4.0 %collective-permute-start.2 = (f32[72,128]{1,0:T(8,128)S(1)}, f32[72,128]{1,0:T(8,128)S(1)}, u32[]{:S(2)}, u32[]{:S(2)}) collective-permute-start(f32[72,128]{1,0:T(8,128)S(1)} %get-tuple-element.20), channel_id=1, source_target_pairs={{0,1},{1,0},{2,3},{3,2},{4,5},{5,4},{6,7},{7,6},{8,9},{9,8},{10,11... | collective-permute-start | bytes 110600 | tf_op jit(solution)/shard_map/ppermute | solution.py:32

commit v5 on v4

--- a/solution.py
+++ b/solution.py
@@ -7,29 +7,23 @@
 from jax.experimental.pallas import tpu as pltpu
 from jax.sharding import PartitionSpec as P
 
+
 WIDTH = 2
 ROWS = 8
 index_pairs = ((0, 0), (1, 1), (2, 2), (0, 1), (0, 2), (1, 2))
+STRIP = 16
 TOP = 9
 
 VMEM = pl.BlockSpec(memory_space=pltpu.VMEM)
 
 
-def swap_pairs(count):
-    far = [(i, (i + 1 if i % 2 else i - 1) % count) for i in range(count)]
-    near = [(i, i ^ 1) for i in range(count)]
-    return far, near
-
-
-def swap_edges(first, second, axis):
+def swap_axes(axis):
     count = lax.axis_size(axis)
     if count % 2:
         forward = [(i, (i + 1) % count) for i in range(count)]
-        backward = [(target, source) for source, target in forward]
-        return lax.ppermute(first, axis, forward), lax.ppermute(second, axis, backward)
-    far_pairs, near_pairs = swap_pairs(count)
-    far = lax.ppermute(second, axis, far_pairs)
-    return lax.ppermute(first, axis, near_pairs), far
+        return forward, [(target, source) for source, target in forward]
+    far = [(i, (i + 1 if i % 2 else i - 1) % count) for i in range(count)]
+    return [(i, i ^ 1) for i in range(count)], far
 
 
 def below_is_first(axis):
@@ -216,83 +210,110 @@
     acc_ref[0], acc_ref[1] = lax.fori_loop(start, stop, step, (acc_ref[0], acc_ref[1]))
 
 
-def interior_kernel(
-    vel_ref, u_ref, keep_ref, fz_ref, hz_ref, hu_ref, mag_ref, acc_ref, tmp_ref
-):
+def pack_edges(ln, u_ref, entries):
+    packed = None
+    for n, (comp, slot) in enumerate(entries):
+        for layer in range(WIDTH):
+            to = WIDTH * n + WIDTH - 1 - layer
+            rows = u_ref[comp, slot, ln.rows(TOP + layer - to)]
+            row = lax.broadcasted_iota(jnp.int32, rows.shape, 0)
+            packed = rows if packed is None else jnp.where(row == to, rows, packed)
+    return packed
+
+
+def pack_all(ln, u_ref, entries, edge_ref, start):
+    for at in range(0, len(entries), ROWS // WIDTH):
+        to = start + WIDTH * at
+        edge_ref[to : to + ROWS] = pack_edges(ln, u_ref, entries[at : at + ROWS // WIDTH])
+
+
+def load_kernel(vel_ref, first_ref, second_ref, strip_ref, top_ref):
     nx = vel_ref.shape[1]
-    windows = mag_ref.shape[1] // ROWS
+    ln = Lanes(strip_ref.shape[1])
+    flag = first_goes_below("gx")
+    entries = [(comp, layer) for comp in range(3) for layer in range(WIDTH)]
+    for comp, layer in entries:
+        low, high = vel_ref[comp, layer], vel_ref[comp, nx - WIDTH + layer]
+        first_ref[comp, layer] = jnp.where(flag, low, high)
+        second = jnp.where(flag, high, low)
+        second_ref[comp, layer] = second
+        top_ref[comp, layer, ln.rows(TOP)] = to_folded(second, ROWS)
+    pack_all(ln, top_ref, entries, strip_ref, 0)
+
+
+def near_slots(nx):
+    flag = below_is_first("gx")
+    return jnp.where(flag, 0, WIDTH), jnp.where(flag, nx + WIDTH, 0)
+
+
+def fold_kernel(vel_ref, first_ref, strip_ref, u_ref, edge_ref):
+    nx = vel_ref.shape[1]
     ln = Lanes(u_ref.shape[3])
+    start, _ = near_slots(nx)
+    first_slot = jnp.where(below_is_first("gx"), 0, nx + WIDTH)
+    for layer in range(WIDTH):
+        for comp in range(3):
+            store_plane(ln, u_ref, comp, first_slot + layer, first_ref[comp, layer])
 
     def fold(x, carry):
         for comp in range(3):
             store_plane(ln, u_ref, comp, WIDTH + x, vel_ref[comp, x])
         return carry
 
-    lax.fori_loop(0, nx, fold, 0, unroll=2)
-
-    def hat_z(x, carry):
+    lax.fori_loop(0, nx, fold, 0, unroll=4)
+    entries = [(comp, start + n) for comp in range(3) for n in range(nx + WIDTH)]
+    count = strip_ref.shape[0]
+    edge_ref[:count] = strip_ref[...]
+    pack_all(ln, u_ref, entries, edge_ref, count)
+
+
+def interior_kernel(
+    u_ref, keep_ref, fz_ref, hz_ref, hu_ref, mag_ref, acc_ref, tmp_ref
+):
+    nx = u_ref.shape[1] - 2 * WIDTH
+    windows = mag_ref.shape[1] // ROWS
+    ln = Lanes(u_ref.shape[3])
+    start, _ = near_slots(nx)
+
+    def hat_z(slot, carry):
         for k in range(1, windows):
-            filter_z(ln, u_ref, hz_ref, WIDTH + x, k)
+            filter_z(ln, u_ref, hz_ref, slot, k)
         return carry
 
-    lax.fori_loop(0, nx, hat_z, 0)
+    lax.fori_loop(start, start + nx + WIDTH, hat_z, 0)
 
     def hat_x(i, carry):
         for k in range(1, windows):
             filter_x(hz_ref, hu_ref, i, k)
         return carry
 
-    lax.fori_loop(2, nx, hat_x, 0)
-    strain_planes(ln, u_ref, mag_ref, tmp_ref, keep_ref, fz_ref, 2, nx)
+    lax.fori_loop(start, start + nx, hat_x, 0)
+    strain_planes(ln, u_ref, mag_ref, tmp_ref, keep_ref, fz_ref, start, start + nx)
     acc_ref[...] = jnp.zeros_like(acc_ref)
-    sum_planes(ln, hu_ref, fz_ref, acc_ref, 2, nx - 2)
-
-
-def fold_kernel(first_ref, second_ref, _, u_ref, edge_ref):
-    planes = u_ref.shape[1]
-    ln = Lanes(u_ref.shape[3])
-    ordered = below_is_first("gx")
-    for comp in range(3):
-        for layer in range(WIDTH):
-            first, second = first_ref[comp, layer], second_ref[comp, layer]
-            below, above = jnp.where(ordered, first, second), jnp.where(ordered, second, first)
-            store_plane(ln, u_ref, comp, layer, below)
-            store_plane(ln, u_ref, comp, planes - WIDTH + layer, above)
-    edges = []
-    for comp in range(3):
-        for slot in range(planes):
-            edges.append((comp, slot))
-    row = lax.broadcasted_iota(jnp.int32, (ROWS, edge_ref.shape[1]), 0)
-    per_window = ROWS // WIDTH
-    for at in range(0, len(edges), per_window):
-        packed = None
-        for n, (comp, slot) in enumerate(edges[at : at + per_window]):
-            for layer in range(WIDTH):
-                to = WIDTH * n + WIDTH - 1 - layer
-                rows = u_ref[comp, slot, ln.rows(TOP + layer - to)]
-                packed = rows if packed is None else jnp.where(row == to, rows, packed)
-        edge_ref[window(at // per_window)] = packed
+    sum_planes(ln, hu_ref, fz_ref, acc_ref, start, start + nx - WIDTH)
 
 
 def sides_kernel(
-    u_ref, _1, _2, _3, _4, _5, _6,
-    keep_ref, fz_ref, hz_ref, hu_ref, mag_ref, acc_ref, tmp_ref,
+    second_ref, _0, _1, _2, _3, _4, _5, _6,
+    u_ref, keep_ref, fz_ref, hz_ref, hu_ref, mag_ref, acc_ref, tmp_ref,
 ):
-    planes = u_ref.shape[1]
-    nx = planes - 2 * WIDTH
+    nx = u_ref.shape[1] - 2 * WIDTH
     windows = mag_ref.shape[1] // ROWS
     ln = Lanes(u_ref.shape[3])
-    for start, stop in ((0, WIDTH), (planes - WIDTH, planes)):
-        for slot in range(start, stop):
-            for k in range(1, windows):
-                filter_z(ln, u_ref, hz_ref, slot, k)
-    for start, stop in ((0, 2), (nx, nx + 2)):
-        for i in range(start, stop):
-            for k in range(1, windows):
-                filter_x(hz_ref, hu_ref, i, k)
-        strain_planes(ln, u_ref, mag_ref, tmp_ref, keep_ref, fz_ref, start, stop)
-    sum_planes(ln, hu_ref, fz_ref, acc_ref, 0, 2)
-    sum_planes(ln, hu_ref, fz_ref, acc_ref, nx - 2, nx)
+    _, slot = near_slots(nx)
+    plane = jnp.where(below_is_first("gx"), nx, 0)
+    inner = jnp.where(below_is_first("gx"), nx - WIDTH, 0)
+    for layer in range(WIDTH):
+        for comp in range(3):
+            store_plane(ln, u_ref, comp, slot + layer, second_ref[comp, layer])
+    for layer in range(WIDTH):
+        for k in range(1, windows):
+            filter_z(ln, u_ref, hz_ref, slot + layer, k)
+    for layer in range(WIDTH):
+        for k in range(1, windows):
+            filter_x(hz_ref, hu_ref, plane + layer, k)
+    strain_planes(ln, u_ref, mag_ref, tmp_ref, keep_ref, fz_ref, plane, plane + WIDTH)
+    sum_planes(ln, hu_ref, fz_ref, acc_ref, inner, inner + WIDTH)
 
 
 def rim_kernel(
@@ -310,9 +331,12 @@
     turned[ROWS : ROWS + count] = pltpu.roll(
         jnp.where(take_first, first_ref[...], second_ref[...]), ny, 1
     )
-    for comp in range(3):
-        for slot in range(planes):
-            at = WIDTH * (comp * planes + slot + 1)
+    start, far = near_slots(nx)
+    places = [(comp, far + n) for comp in range(3) for n in range(WIDTH)]
+    rest = [(comp, start + n) for comp in range(3) for n in range(nx + WIDTH)]
+    for first_row, entries in ((0, places), (STRIP, rest)):
+        for n, (comp, slot) in enumerate(entries):
+            at = first_row + WIDTH * (n + 1)
             u_ref[comp, slot, ln.rows(TOP - ROWS)] = turned[ln.rows(at)]
     for slot in range(planes):
         filter_z(ln, u_ref, hz, slot, 0)
@@ -347,9 +371,7 @@
         eddy_ref[x] = column * mag_ref[x]
 
 
-def call(
-    kernel, name, shapes, operands, cycles, aliases=None, scratch=()
-):
+def call(kernel, shapes, operands, cycles, aliases=None, scratch=()):
     return pl.pallas_call(
         kernel,
         out_shape=tuple(jax.ShapeDtypeStruct(shape, jnp.float32) for shape in shapes),
@@ -363,7 +385,6 @@
         cost_estimate=pl.CostEstimate(
             flops=cycles * 4096, bytes_accessed=0, transcendentals=0
         ),
-        name=name,
     )(*operands)
 
 
@@ -382,37 +403,42 @@
         (2, ROWS, lanes),
     )
     window_pair = ((12, 2, windowed, lanes),)
-    low, high = velocity[:, :WIDTH], velocity[:, nx - WIDTH :]
-    flag = first_goes_below("gx")
-    first, second = jnp.where(flag, low, high), jnp.where(flag, high, low)
-    first, second = swap_edges(first, second, "gx")
-    u, *fields = call(
-        interior_kernel, "interior", (u_shape, *work), (velocity,), 6000, scratch=window_pair
-    )
-    edge_shape = (3 * planes * WIDTH, lanes)
-    u, edges = call(
-        fold_kernel, "fold", (u_shape, edge_shape), (first, second, u), 800, {2: 0}
-    )
-    first, second = swap_edges(edges, edges, "gz")
-    keep, _, _, hu, mag, acc = call(
+    halo = (3, WIDTH, ny, nz)
+    strip_shape = (STRIP, lanes)
+    first, second, strip = call(
+        load_kernel,
+        (halo, halo, strip_shape),
+        (velocity,),
+        500,
+        scratch=((3, WIDTH, 3 * ROWS, lanes),),
+    )
+    to_first, to_second = swap_axes("gx")
+    strip = lax.ppermute(strip, "gx", to_second)
+    first = lax.ppermute(first, "gx", to_first)
+    second = lax.ppermute(second, "gx", to_second)
+    edge_rows = STRIP + -(-3 * (nx + WIDTH) * WIDTH // ROWS) * ROWS
+    u, edges = call(fold_kernel, (u_shape, (edge_rows, lanes)), (velocity, first, strip), 1500)
+    to_first, to_second = swap_axes("gz")
+    low = lax.ppermute(edges, "gz", to_second)
+    high = lax.ppermute(edges, "gz", to_first)
+    fields = call(interior_kernel, work, (u,), 6000, scratch=window_pair)
+    u, keep, _, _, hu, mag, acc = call(
         sides_kernel,
-        "sides",
-        work,
-        (u, *fields),
-        4000,
-        {1 + n: n for n in range(6)},
+        (u_shape, *work),
+        (second, u, *fields),
+        2000,
+        {1 + n: n for n in range(7)},
         window_pair,
     )
     count = lax.axis_size("gx") * lax.axis_size("gz")
     *_, magnitude, sums = call(
         rim_kernel,
-        "rim",
         (u_shape, work[0], work[3], work[4], (nx, ny, nz), (count, lanes)),
-        (first, second, u, keep, hu, mag, acc),
+        (high, low, u, keep, hu, mag, acc),
         1000,
         {2 + n: n for n in range(4)},
         scratch=(
-            (ROWS + edge_shape[0], lanes),
+            (ROWS + edge_rows, lanes),
             (12, nx + 2, ROWS, lanes),
             (3, planes, ROWS, lanes),
         ),
@@ -420,11 +446,7 @@
     parts = lax.all_to_all(sums, ("gx", "gz"), 0, 0, tiled=True)
     cells = nx * lax.axis_size("gx") * nz * lax.axis_size("gz")
     coefficient, eddy_viscosity = call(
-        functools.partial(finish_kernel, cells),
-        "finish",
-        ((1, ny), (nx, ny, nz)),
-        (parts, magnitude),
-        500,
+        functools.partial(finish_kernel, cells), ((1, ny), (nx, ny, nz)), (parts, magnitude), 500
     )
     return (coefficient[0], eddy_viscosity)
 

time: 31.5 us -> 32.8 us (1.041)
  waiting for transfers between devices: 2.72 us -> 4.78 us
  other arithmetic: 1.06 us -> 0 us
    ppermute x4 -> x5, waiting for transfers between devices: 2.72 us -> 4.78 us  [the longest x1 4.77 us: on_device(): strip = lax.ppermute(strip, 'gx', to_second)]
    select_n x1 -> x0, other arithmetic: 1.06 us -> none  [on_device(): first, second = (jnp.where(flag, low, high), jnp.where(flag, high, low))]
    pallas_call x5 -> x6, Pallas kernels: 6.93 us -> 7.02 us  [call(): pl.pallas_call(kernel, out_shape=tuple((jax.ShapeDtypeStruct(shape, jnp.f...]
    ppermute x4 -> x5, starting transfers between devices: 8.6 us -> 8.56 us  [the longest x1 3.54 us: on_device(): second = lax.ppermute(second, 'gx', to_second)]
  transfers between devices with their start and end apart: 4 -> 5, of which waited for: 3 -> 1; matrix products, arithmetic and copies ran while one was open for 0% -> 0% of each run, Pallas kernels for 15% -> 15%
where the time goes in v5:
time: 32.8 us; the launch traced here: 32.7 us
  blocking collectives  10.5 us (32%)
  starting transfers between devices  8.56 us (26%)
  Pallas kernels  7.02 us (21%)
  waiting for transfers between devices  4.78 us (15%)
  local copies, waits for them, and re-layouts  1.13 us (3%)
  between operations  0.69 us (2%)
    all_to_all x1, blocking collectives, on_device(): parts = lax.all_to_all(sums, ('gx', 'gz'), 0, 0, tiled=True)  10.5 us
    pallas_call x6, Pallas kernels, call(): pl.pallas_call(kernel, out_shape=tuple((jax.ShapeDtypeStruct(shape, jnp.f...  7.02 us
    ppermute x1, waiting for transfers between devices, on_device(): strip = lax.ppermute(strip, 'gx', to_second)  4.77 us
    ppermute x1, starting transfers between devices, on_device(): second = lax.ppermute(second, 'gx', to_second)  3.54 us
    ppermute x1, starting transfers between devices, on_device(): low = lax.ppermute(edges, 'gz', to_second)  2.47 us
    ppermute x1, starting transfers between devices, on_device(): high = lax.ppermute(edges, 'gz', to_first)  1.96 us
    unnamed x2, local copies, waits for them, and re-layouts  1.13 us
  transfers between devices with their start and end apart: 5, of which 1 were waited for; matrix products, arithmetic and copies ran while one was open for 0% of the time, Pallas kernels for 15%

profile of v5, /device:TPU:0, one launch (start us, length us, event | category | flops | bytes accessed | tf_op | source)
XLA Modules:
  0.0 32.7 jit_solution(16592517933385512530)
XLA Ops:
  0.6 0.0 copy-start
  0.6 1.1 %copy-done = f32[3,8,64,128]{3,2,1,0:T(8,128)S(1)} copy-done((f32[3,8,64,128]{3,2,1,0:T(8,128)S(1)}, f32[3,8,64,128]{3,2,1,0:T(8,128)}, u32[]{:S(2)}) %copy-start) | copy-done | bytes 786456
  1.8 0.2 shard_map.30
  2.0 0.5 %collective-permute-start = (f32[3,2,64,128]{3,2,1,0:T(8,128)S(1)}, f32[3,2,64,128]{3,2,1,0:T(8,128)S(1)}, u32[]{:S(2)}, u32[]{:S(2)}) collective-permute-start(f32[3,2,64,128]{3,2,1,0:T(8,128)S(1)} %get-tuple-element.22), channel_id=1, source_target_pairs={{0,4},{4,0},{8,12},{12,8},{16,20},{20,16},{24,28},{28,24},{1,5},{5... | collective-permute-start | bytes 589832 | tf_op jit(solution)/shard_map/ppermute | solution.py:417
  2.5 3.5 %collective-permute-start.4 = (f32[3,2,64,128]{3,2,1,0:T(8,128)S(1)}, f32[3,2,64,128]{3,2,1,0:T(8,128)S(1)}, u32[]{:S(2)}, u32[]{:S(2)}) collective-permute-start(f32[3,2,64,128]{3,2,1,0:T(8,128)S(1)} %get-tuple-element.25), channel_id=1, source_target_pairs={{0,28},{4,8},{8,4},{12,16},{16,12},{20,24},{24,20},{28,0},{1,29},{... | collective-permute-start | bytes 589832 | tf_op jit(solution)/shard_map/ppermute | solution.py:418
  6.1 0.0 collective-permute-start.1
  6.1 4.8 %collective-permute-done.1.strip_ref = f32[16,128]{1,0:T(8,128)S(1)} collective-permute-done((f32[16,128]{1,0:T(8,128)S(1)}, f32[16,128]{1,0:T(8,128)S(1)}, u32[]{:S(2)}, u32[]{:S(2)}) %collective-permute-start.1) | collective-permute-done | bytes 8224 | tf_op jit(solution)/shard_map/ppermute | solution.py:416
  10.9 0.0 collective-permute-done.first_ref
  10.9 1.0 %shard_map.31 = (f32[3,12,88,128]{3,2,1,0:T(8,128)S(1)}, f32[80,128]{1,0:T(8,128)S(1)}) custom-call(f32[3,8,64,128]{3,2,1,0:T(8,128)S(1)} %copy-done, f32[3,2,64,128]{3,2,1,0:T(8,128)S(1)} %collective-permute-done.first_ref, f32[16,128]{1,0:T(8,128)S(1)} %collective-permute-done.1.strip_ref), custom_call_target="tpu_custom_call" | custom-call | flops 6144000 | tf_op jit(solution)/shard_map/pallas_call | solution.py:375
  11.9 2.0 %collective-permute-start.2 = (f32[80,128]{1,0:T(8,128)S(1)}, f32[80,128]{1,0:T(8,128)S(1)}, u32[]{:S(2)}, u32[]{:S(2)}) collective-permute-start(f32[80,128]{1,0:T(8,128)S(1)} %get-tuple-element.24), channel_id=1, source_target_pairs={{0,1},{1,0},{2,3},{3,2},{4,5},{5,4},{6,7},{7,6},{8,9},{9,8},{10,11... | collective-permute-start | bytes 122888 | tf_op jit(solution)/shard_map/ppermute | solution.py:423
  13.9 2.5 %collective-permute-start.3 = (f32[80,128]{1,0:T(8,128)S(1)}, f32[80,128]{1,0:T(8,128)S(1)}, u32[]{:S(2)}, u32[]{:S(2)}) collective-permute-start(f32[80,128]{1,0:T(8,128)S(1)} %get-tuple-element.24), channel_id=1, source_target_pairs={{0,3},{1,2},{2,1},{3,0},{4,7},{5,6},{6,5},{7,4},{8,11},{9,10},{10,... | collective-permute-start | bytes 122888 | tf_op jit(solution)/shard_map/ppermute | solution.py:422
  16.3 2.8 %shard_map.32 = (f32[12,10,16,128]{3,2,1,0:T(8,128)S(1)}, f32[12,10,64,128]{3,2,1,0:T(8,128)S(1)}, f32[3,12,72,128]{3,2,1,0:T(8,128)S(1)}, f32[3,10,72,128]{3,2,...) custom-call(f32[3,12,88,128]{3,2,1,0:T(8,128)S(1)} %get-tuple-element.26.u_ref._0), custom_call_target="tpu_custom_call" | custom-call | flops 24576000 | tf_op jit(solution)/shard_map/pallas_call | solution.py:375
  19.2 0.0 collective-permute-done.4.second_ref
  19.2 1.1 %shard_map.33 = (f32[3,12,88,128]{3,2,1,0:T(8,128)S(1)}, f32[12,10,16,128]{3,2,1,0:T(8,128)S(1)}, f32[12,10,64,128]{3,2,1,0:T(8,128)S(1)}, f32[3,12,72,128]{3,2,...) custom-call(f32[3,2,64,128]{3,2,1,0:T(8,128)S(1)} %collective-permut, ...), custom_call_target="tpu_custom_call", output_to_operand_aliasing={{0}: (1, {}), {1}: (2, {}), {2}: (3, {}), {3}: (4, {}), {4}... | custom-call | flops 8192000 | tf_op jit(solution)/shard_map/pallas_call | solution.py:375
  20.3 0.0 collective-permute-done.2.first_ref
  20.3 0.0 collective-permute-done.3.second_ref
  20.3 1.0 %shard_map.34 = (f32[3,12,88,128]{3,2,1,0:T(8,128)S(1)}, f32[12,10,16,128]{3,2,1,0:T(8,128)S(1)}, f32[3,10,72,128]{3,2,1,0:T(8,128)S(1)}, f32[10,72,128]{2,1,0:T...) custom-call(f32[80,128]{1,0:T(8,128)S(1)} %collective-permute-done.2, ...), custom_call_target="tpu_custom_call", output_to_operand_aliasing={{0}: (2, {}), {1}: (3, {}), {2}: (4, {}), {3}: (5, {})} | custom-call | flops 4096000 | tf_op jit(solution)/shard_map/pallas_call | solution.py:375
  21.3 10.5 %all_to_all.11 = f32[32,1,128]{2,1,0:T(1,128)S(1)} all-to-all(f32[32,1,128]{2,1,0:T(1,128)S(1)} %bitcast.6), channel_id=1, replica_groups=mesh['gx'=8,'gz'=4] {'gx','gz'}, dimensions={0} | all-to-all | bytes 32768 | tf_op jit(solution)/shard_map/all_to_all | solution.py:446
  31.8 0.9 %shard_map.35 = (f32[1,64]{1,0:T(1,128)}, f32[8,64,128]{2,1,0:T(8,128)}) custom-call(f32[32,128]{1,0:T(8,128)S(1)} %bitcast.5, f32[8,64,128]{2,1,0:T(8,128)S(1)} %get-tuple-element.39.mag_ref), custom_call_target="tpu_custom_call" | custom-call | flops 2048000 | tf_op jit(solution)/shard_map/pallas_call | solution.py:375
Async XLA Ops:
  0.6 1.1 %copy-start = (f32[3,8,64,128]{3,2,1,0:T(8,128)S(1)}, f32[3,8,64,128]{3,2,1,0:T(8,128)}, u32[]{:S(2)}) copy-start(f32[3,8,64,128]{3,2,1,0:T(8,128)} %vel_ref.3) | copy-start | bytes 2359300
  2.0 8.9 %collective-permute-start = (f32[3,2,64,128]{3,2,1,0:T(8,128)S(1)}, f32[3,2,64,128]{3,2,1,0:T(8,128)S(1)}, u32[]{:S(2)}, u32[]{:S(2)}) collective-permute-start(f32[3,2,64,128]{3,2,1,0:T(8,128)S(1)} %get-tuple-element.22), channel_id=1, source_target_pairs={{0,4},{4,0},{8,12},{12,8},{16,20},{20,16},{24,28},{28,24},{1,5},{5... | collective-permute-start | bytes 589832 | tf_op jit(solution)/shard_map/ppermute | solution.py:417
  2.5 16.6 %collective-permute-start.4 = (f32[3,2,64,128]{3,2,1,0:T(8,128)S(1)}, f32[3,2,64,128]{3,2,1,0:T(8,128)S(1)}, u32[]{:S(2)}, u32[]{:S(2)}) collective-permute-start(f32[3,2,64,128]{3,2,1,0:T(8,128)S(1)} %get-tuple-element.25), channel_id=1, source_target_pairs={{0,28},{4,8},{8,4},{12,16},{16,12},{20,24},{24,20},{28,0},{1,29},{... | collective-permute-start | bytes 589832 | tf_op jit(solution)/shard_map/ppermute | solution.py:418
  6.1 4.8 %collective-permute-start.1 = (f32[16,128]{1,0:T(8,128)S(1)}, f32[16,128]{1,0:T(8,128)S(1)}, u32[]{:S(2)}, u32[]{:S(2)}) collective-permute-start(f32[16,128]{1,0:T(8,128)S(1)} %get-tuple-element.23), channel_id=1, source_target_pairs={{0,28},{4,8},{8,4},{12,16},{16,12},{20,24},{24,20},{28,0},{1,29},{... | collective-permute-start | bytes 24584 | tf_op jit(solution)/shard_map/ppermute | solution.py:416
  11.9 8.4 %collective-permute-start.2 = (f32[80,128]{1,0:T(8,128)S(1)}, f32[80,128]{1,0:T(8,128)S(1)}, u32[]{:S(2)}, u32[]{:S(2)}) collective-permute-start(f32[80,128]{1,0:T(8,128)S(1)} %get-tuple-element.24), channel_id=1, source_target_pairs={{0,1},{1,0},{2,3},{3,2},{4,5},{5,4},{6,7},{7,6},{8,9},{9,8},{10,11... | collective-permute-start | bytes 122888 | tf_op jit(solution)/shard_map/ppermute | solution.py:423
  13.9 6.4 %collective-permute-start.3 = (f32[80,128]{1,0:T(8,128)S(1)}, f32[80,128]{1,0:T(8,128)S(1)}, u32[]{:S(2)}, u32[]{:S(2)}) collective-permute-start(f32[80,128]{1,0:T(8,128)S(1)} %get-tuple-element.24), channel_id=1, source_target_pairs={{0,3},{1,2},{2,1},{3,0},{4,7},{5,6},{6,5},{7,4},{8,11},{9,10},{10,... | collective-permute-start | bytes 122888 | tf_op jit(solution)/shard_map/ppermute | solution.py:422

commit v6 on v5

--- a/solution.py
+++ b/solution.py
@@ -132,6 +132,25 @@
             tmp_ref[at, slot, window(k)] = value
             if k == 1:
                 keep_ref[at, i, window(1)] = value
+
+
+def outer_size(ln, u_ref, mag_ref, i):
+    at = TOP + 1
+    slopes = [
+        (
+            u_ref[comp, i + 2, ln.rows(at)] - u_ref[comp, i, ln.rows(at)],
+            ln.slope_y(u_ref[comp, i + 1, ln.rows(at)]),
+            ln.slope_z(u_ref[comp, i + 1, ln.rows(at + 1)], u_ref[comp, i + 1, ln.rows(at - 1)]),
+        )
+        for comp in range(3)
+    ]
+    mag_ref[i, ln.rows(2)] = rates(slopes)[1]
+
+
+def unfold_planes(ln, mag_ref, plain_ref, start, count):
+    half = plain_ref.shape[2] // 2
+    for n in range(count):
+        plain_ref[start + n] = from_folded(mag_ref[start + n + 1, ln.rows(1, half)])
 
 
 def filter_products(ln, tmp_ref, fz_ref, slot, i, k):
@@ -246,14 +265,20 @@
     return jnp.where(flag, 0, WIDTH), jnp.where(flag, nx + WIDTH, 0)
 
 
-def fold_kernel(vel_ref, first_ref, strip_ref, u_ref, edge_ref):
+def edge_places(nx):
+    start, far = near_slots(nx)
+    near = jnp.where(below_is_first("gx"), start, nx + WIDTH)
+    block = [(comp, WIDTH + x) for comp in range(3) for x in range(nx)]
+    halos = [
+        [(comp, slot + layer) for comp in range(3) for layer in range(WIDTH)]
+        for slot in (far, near)
+    ]
+    return ((0, halos[0]), (STRIP, block), (STRIP + WIDTH * len(block), halos[1]))
+
+
+def fold_kernel(vel_ref, u_ref, edge_ref):
     nx = vel_ref.shape[1]
     ln = Lanes(u_ref.shape[3])
-    start, _ = near_slots(nx)
-    first_slot = jnp.where(below_is_first("gx"), 0, nx + WIDTH)
-    for layer in range(WIDTH):
-        for comp in range(3):
-            store_plane(ln, u_ref, comp, first_slot + layer, first_ref[comp, layer])
 
     def fold(x, carry):
         for comp in range(3):
@@ -261,14 +286,25 @@
         return carry
 
     lax.fori_loop(0, nx, fold, 0, unroll=4)
-    entries = [(comp, start + n) for comp in range(3) for n in range(nx + WIDTH)]
-    count = strip_ref.shape[0]
-    edge_ref[:count] = strip_ref[...]
-    pack_all(ln, u_ref, entries, edge_ref, count)
+    row, entries = edge_places(nx)[1]
+    pack_all(ln, u_ref, entries, edge_ref, row)
+
+
+def near_kernel(first_ref, _0, _1, u_ref, edge_ref):
+    nx = u_ref.shape[1] - 2 * WIDTH
+    ln = Lanes(u_ref.shape[3])
+    row, entries = edge_places(nx)[2]
+    for n, (comp, slot) in enumerate(entries):
+        store_plane(ln, u_ref, comp, slot, first_ref[comp, n % WIDTH])
+    pack_all(ln, u_ref, entries, edge_ref, row)
+
+
+def edge_kernel(strip_ref, _, edge_ref):
+    edge_ref[:STRIP] = strip_ref[...]
 
 
 def interior_kernel(
-    u_ref, keep_ref, fz_ref, hz_ref, hu_ref, mag_ref, acc_ref, tmp_ref
+    u_ref, keep_ref, fz_ref, hz_ref, hu_ref, mag_ref, acc_ref, plain_ref, tmp_ref
 ):
     nx = u_ref.shape[1] - 2 * WIDTH
     windows = mag_ref.shape[1] // ROWS
@@ -291,6 +327,10 @@
     strain_planes(ln, u_ref, mag_ref, tmp_ref, keep_ref, fz_ref, start, start + nx)
     acc_ref[...] = jnp.zeros_like(acc_ref)
     sum_planes(ln, hu_ref, fz_ref, acc_ref, start, start + nx - WIDTH)
+    inner = jnp.maximum(start - 1, 0)
+    for n in range(nx - 1):
+        outer_size(ln, u_ref, mag_ref, inner + n + 1)
+    unfold_planes(ln, mag_ref, plain_ref, inner, nx - 1)
 
 
 def sides_kernel(
@@ -317,13 +357,12 @@
 
 
 def rim_kernel(
-    first_ref, second_ref, _1, _2, _3, _4, acc_ref, u_ref, tmp_ref, hu_ref, mag_ref,
-    plain_ref, sums_ref, turned, fz, hz,
+    first_ref, second_ref, _1, _2, _3, _4, _5, acc_ref, u_ref, tmp_ref, hu_ref, mag_ref,
+    plain_ref, outer_ref, sums_ref, turned, fz, hz,
 ):
     planes, _, lanes = u_ref.shape[1:]
     nx = planes - 2 * WIDTH
     ny = lanes // 2
-    half = plain_ref.shape[2] // 2
     ln = Lanes(lanes)
     count = first_ref.shape[0]
     upper = lax.broadcasted_iota(jnp.int32, first_ref.shape, 1) >= ny
@@ -331,10 +370,7 @@
     turned[ROWS : ROWS + count] = pltpu.roll(
         jnp.where(take_first, first_ref[...], second_ref[...]), ny, 1
     )
-    start, far = near_slots(nx)
-    places = [(comp, far + n) for comp in range(3) for n in range(WIDTH)]
-    rest = [(comp, start + n) for comp in range(3) for n in range(nx + WIDTH)]
-    for first_row, entries in ((0, places), (STRIP, rest)):
+    for first_row, entries in edge_places(nx):
         for n, (comp, slot) in enumerate(entries):
             at = first_row + WIDTH * (n + 1)
             u_ref[comp, slot, ln.rows(TOP - ROWS)] = turned[ln.rows(at)]
@@ -355,10 +391,11 @@
     both = jnp.where(lax.broadcasted_iota(jnp.int32, (1, lanes), 1) < ny, numer, denom)
     sums_ref[...] = jnp.broadcast_to(both, sums_ref.shape)
     for x in range(nx):
-        plain_ref[x] = from_folded(mag_ref[x + 1, ln.rows(1, half)])
-
-
-def finish_kernel(cells, parts_ref, mag_ref, coefficient_ref, eddy_ref):
+        outer_ref[x : x + 1] = mag_ref[x + 1, 1:2]
+    unfold_planes(ln, mag_ref, plain_ref, jnp.where(below_is_first("gx"), nx - 1, 0), 1)
+
+
+def finish_kernel(cells, parts_ref, mag_ref, outer_ref, coefficient_ref, eddy_ref):
     lanes = parts_ref.shape[1]
     ny = lanes // 2
     sums = jnp.sum(parts_ref[...], axis=0, keepdims=True)
@@ -367,8 +404,12 @@
     coefficient = numer / cells / (denom / cells + 1e-06)
     coefficient_ref[...] = coefficient
     column = jnp.broadcast_to(coefficient, (mag_ref.shape[2], ny)).T
+    outer = outer_ref[...].T
+    lane = lax.broadcasted_iota(jnp.int32, column.shape, 1)
     for x in range(mag_ref.shape[0]):
-        eddy_ref[x] = column * mag_ref[x]
+        low, high = outer[:ny, x : x + 1], outer[ny:, x : x + 1]
+        plane = jnp.where(lane == 0, low, mag_ref[x])
+        eddy_ref[x] = column * jnp.where(lane == lane.shape[1] - 1, high, plane)
 
 
 def call(kernel, shapes, operands, cycles, aliases=None, scratch=()):
@@ -416,12 +457,15 @@
     strip = lax.ppermute(strip, "gx", to_second)
     first = lax.ppermute(first, "gx", to_first)
     second = lax.ppermute(second, "gx", to_second)
-    edge_rows = STRIP + -(-3 * (nx + WIDTH) * WIDTH // ROWS) * ROWS
-    u, edges = call(fold_kernel, (u_shape, (edge_rows, lanes)), (velocity, first, strip), 1500)
+    edge_rows = STRIP + WIDTH * 3 * nx + STRIP
+    edge_shape = (edge_rows, lanes)
+    u, edges = call(fold_kernel, (u_shape, edge_shape), (velocity,), 1200)
+    u, edges = call(near_kernel, (u_shape, edge_shape), (first, u, edges), 400, {1: 0, 2: 1})
+    (edges,) = call(edge_kernel, (edge_shape,), (strip, edges), 50, {1: 0})
     to_first, to_second = swap_axes("gz")
     low = lax.ppermute(edges, "gz", to_second)
     high = lax.ppermute(edges, "gz", to_first)
-    fields = call(interior_kernel, work, (u,), 6000, scratch=window_pair)
+    *fields, plain = call(interior_kernel, (*work, (nx, ny, nz)), (u,), 6000, scratch=window_pair)
     u, keep, _, _, hu, mag, acc = call(
         sides_kernel,
         (u_shape, *work),
@@ -431,12 +475,12 @@
         window_pair,
     )
     count = lax.axis_size("gx") * lax.axis_size("gz")
-    *_, magnitude, sums = call(
+    *_, plain, outer, sums = call(
         rim_kernel,
-        (u_shape, work[0], work[3], work[4], (nx, ny, nz), (count, lanes)),
-        (high, low, u, keep, hu, mag, acc),
+        (u_shape, work[0], work[3], work[4], (nx, ny, nz), (nx, lanes), (count, lanes)),
+        (high, low, u, keep, hu, mag, plain, acc),
         1000,
-        {2 + n: n for n in range(4)},
+        {2 + n: n for n in range(5)},
         scratch=(
             (ROWS + edge_rows, lanes),
             (12, nx + 2, ROWS, lanes),
@@ -446,7 +490,7 @@
     parts = lax.all_to_all(sums, ("gx", "gz"), 0, 0, tiled=True)
     cells = nx * lax.axis_size("gx") * nz * lax.axis_size("gz")
     coefficient, eddy_viscosity = call(
-        functools.partial(finish_kernel, cells), ((1, ny), (nx, ny, nz)), (parts, magnitude), 500
+        functools.partial(finish_kernel, cells), ((1, ny), (nx, ny, nz)), (parts, plain, outer), 500
     )
     return (coefficient[0], eddy_viscosity)
 

time: 32.8 us -> 31.7 us (0.966)
  waiting for transfers between devices: 4.78 us -> 3.75 us
  blocking collectives: 10.5 us -> 10 us
  Pallas kernels: 7.02 us -> 7.42 us
    ppermute x1, waiting for transfers between devices: 4.77 us -> 3.74 us  [on_device(): strip = lax.ppermute(strip, 'gx', to_second)]
    all_to_all x1, blocking collectives: 10.5 us -> 10 us  [on_device(): parts = lax.all_to_all(sums, ('gx', 'gz'), 0, 0, tiled=True)]
    pallas_call x6 -> x8, Pallas kernels: 7.02 us -> 7.42 us  [call(): pl.pallas_call(kernel, out_shape=tuple((jax.ShapeDtypeStruct(shape, jnp.f...]
  transfers between devices with their start and end apart: 5 -> 5, of which waited for: 1 -> 1; matrix products, arithmetic and copies ran while one was open for 0% -> 0% of each run, Pallas kernels for 15% -> 18%
where the time goes in v6:
time: 31.7 us; the launch traced here: 31.5 us
  blocking collectives  10 us (32%)
  starting transfers between devices  8.5 us (27%)
  Pallas kernels  7.42 us (23%)
  waiting for transfers between devices  3.75 us (12%)
  local copies, waits for them, and re-layouts  1.13 us (4%)
  between operations  0.69 us (2%)
    all_to_all x1, blocking collectives, on_device(): parts = lax.all_to_all(sums, ('gx', 'gz'), 0, 0, tiled=True)  10 us
    pallas_call x8, Pallas kernels, call(): pl.pallas_call(kernel, out_shape=tuple((jax.ShapeDtypeStruct(shape, jnp.f...  7.42 us
    ppermute x1, waiting for transfers between devices, on_device(): strip = lax.ppermute(strip, 'gx', to_second)  3.74 us
    ppermute x1, starting transfers between devices, on_device(): second = lax.ppermute(second, 'gx', to_second)  3.54 us
    ppermute x1, starting transfers between devices, on_device(): low = lax.ppermute(edges, 'gz', to_second)  2.47 us
    ppermute x1, starting transfers between devices, on_device(): high = lax.ppermute(edges, 'gz', to_first)  1.89 us
    unnamed x2, local copies, waits for them, and re-layouts  1.13 us
  transfers between devices with their start and end apart: 5, of which 1 were waited for; matrix products, arithmetic and copies ran while one was open for 0% of the time, Pallas kernels for 18%

profile of v6, /device:TPU:0, one launch (start us, length us, event | category | flops | bytes accessed | tf_op | source)
XLA Modules:
  0.0 31.5 jit_solution(7014372856387950367)
XLA Ops:
  0.6 0.0 copy-start
  0.6 1.1 %copy-done = f32[3,8,64,128]{3,2,1,0:T(8,128)S(1)} copy-done((f32[3,8,64,128]{3,2,1,0:T(8,128)S(1)}, f32[3,8,64,128]{3,2,1,0:T(8,128)}, u32[]{:S(2)}) %copy-start) | copy-done | bytes 786456
  1.8 0.2 shard_map.30
  2.0 0.5 %collective-permute-start.1 = (f32[3,2,64,128]{3,2,1,0:T(8,128)S(1)}, f32[3,2,64,128]{3,2,1,0:T(8,128)S(1)}, u32[]{:S(2)}, u32[]{:S(2)}) collective-permute-start(f32[3,2,64,128]{3,2,1,0:T(8,128)S(1)} %get-tuple-element.27), channel_id=1, source_target_pairs={{0,4},{4,0},{8,12},{12,8},{16,20},{20,16},{24,28},{28,24},{1,5},{5... | collective-permute-start | bytes 589832 | tf_op jit(solution)/shard_map/ppermute | solution.py:458
  2.5 3.5 %collective-permute-start.4 = (f32[3,2,64,128]{3,2,1,0:T(8,128)S(1)}, f32[3,2,64,128]{3,2,1,0:T(8,128)S(1)}, u32[]{:S(2)}, u32[]{:S(2)}) collective-permute-start(f32[3,2,64,128]{3,2,1,0:T(8,128)S(1)} %get-tuple-element.31), channel_id=1, source_target_pairs={{0,28},{4,8},{8,4},{12,16},{16,12},{20,24},{24,20},{28,0},{1,29},{... | collective-permute-start | bytes 589832 | tf_op jit(solution)/shard_map/ppermute | solution.py:459
  6.1 0.0 collective-permute-start
  6.1 0.8 %shard_map.31 = (f32[3,12,88,128]{3,2,1,0:T(8,128)S(1)}, f32[80,128]{1,0:T(8,128)S(1)}) custom-call(f32[3,8,64,128]{3,2,1,0:T(8,128)S(1)} %copy-done), custom_call_target="tpu_custom_call" | custom-call | flops 4915200 | tf_op jit(solution)/shard_map/pallas_call | solution.py:416
  6.9 0.0 collective-permute-done.1.first_ref
  6.9 0.2 shard_map.32
  7.1 3.7 %collective-permute-done.strip_ref = f32[16,128]{1,0:T(8,128)S(1)} collective-permute-done((f32[16,128]{1,0:T(8,128)S(1)}, f32[16,128]{1,0:T(8,128)S(1)}, u32[]{:S(2)}, u32[]{:S(2)}) %collective-permute-start) | collective-permute-done | bytes 8224 | tf_op jit(solution)/shard_map/ppermute | solution.py:457
  10.9 1.9 %collective-permute-start.2 = (f32[80,128]{1,0:T(8,128)S(1)}, f32[80,128]{1,0:T(8,128)S(1)}, u32[]{:S(2)}, u32[]{:S(2)}) collective-permute-start(f32[80,128]{1,0:T(8,128)S(1)} %shard_map.33), channel_id=1, source_target_pairs={{0,1},{1,0},{2,3},{3,2},{4,5},{5,4},{6,7},{7,6},{8,9},{9,8},{10,11... | collective-permute-start | bytes 122888 | tf_op jit(solution)/shard_map/ppermute | solution.py:467
  12.8 2.5 %collective-permute-start.3 = (f32[80,128]{1,0:T(8,128)S(1)}, f32[80,128]{1,0:T(8,128)S(1)}, u32[]{:S(2)}, u32[]{:S(2)}) collective-permute-start(f32[80,128]{1,0:T(8,128)S(1)} %shard_map.33), channel_id=1, source_target_pairs={{0,3},{1,2},{2,1},{3,0},{4,7},{5,6},{6,5},{7,4},{8,11},{9,10},{10,... | collective-permute-start | bytes 122888 | tf_op jit(solution)/shard_map/ppermute | solution.py:466
  15.3 3.5 %shard_map.34 = (f32[12,10,16,128]{3,2,1,0:T(8,128)S(1)}, f32[12,10,64,128]{3,2,1,0:T(8,128)S(1)}, f32[3,12,72,128]{3,2,1,0:T(8,128)S(1)}, f32[3,10,72,128]{3,2,...) custom-call(f32[3,12,88,128]{3,2,1,0:T(8,128)S(1)} %get-tuple-element.32.u_ref._0), custom_call_target="tpu_custom_call" | custom-call | flops 24576000 | tf_op jit(solution)/shard_map/pallas_call | solution.py:416
  18.7 0.0 collective-permute-done.4.second_ref
  18.7 1.1 %shard_map.35 = (f32[3,12,88,128]{3,2,1,0:T(8,128)S(1)}, f32[12,10,16,128]{3,2,1,0:T(8,128)S(1)}, f32[12,10,64,128]{3,2,1,0:T(8,128)S(1)}, f32[3,12,72,128]{3,2,...) custom-call(f32[3,2,64,128]{3,2,1,0:T(8,128)S(1)} %collective-permut, ...), custom_call_target="tpu_custom_call", output_to_operand_aliasing={{0}: (1, {}), {1}: (2, {}), {2}: (3, {}), {3}: (4, {}), {4}... | custom-call | flops 8192000 | tf_op jit(solution)/shard_map/pallas_call | solution.py:416
  19.8 0.0 collective-permute-done.2.first_ref
  19.8 0.0 collective-permute-done.3.second_ref
  19.8 0.6 %shard_map.36 = (f32[3,12,88,128]{3,2,1,0:T(8,128)S(1)}, f32[12,10,16,128]{3,2,1,0:T(8,128)S(1)}, f32[3,10,72,128]{3,2,1,0:T(8,128)S(1)}, f32[10,72,128]{2,1,0:T...) custom-call(f32[80,128]{1,0:T(8,128)S(1)} %collective-permute-done.2, ...), custom_call_target="tpu_custom_call", output_to_operand_aliasing={{0}: (2, {}), {1}: (3, {}), {2}: (4, {}), {3}: (5, {}), {4}... | custom-call | flops 4096000 | tf_op jit(solution)/shard_map/pallas_call | solution.py:416
  20.4 10.0 %all_to_all.11 = f32[32,1,128]{2,1,0:T(1,128)S(1)} all-to-all(f32[32,1,128]{2,1,0:T(1,128)S(1)} %bitcast.6), channel_id=1, replica_groups=mesh['gx'=8,'gz'=4] {'gx','gz'}, dimensions={0} | all-to-all | bytes 32768 | tf_op jit(solution)/shard_map/all_to_all | solution.py:490
  30.4 1.1 %shard_map.37 = (f32[1,64]{1,0:T(1,128)}, f32[8,64,128]{2,1,0:T(8,128)}) custom-call(f32[32,128]{1,0:T(8,128)S(1)} %bitcast.5, f32[8,64,128]{2,1,0:T(8,128)S(1)} %get-tuple-element.46.mag_ref, f32[8,128]{1,0:T(8,128)S(1)} %get-tuple-element.47.outer_ref), custom_call_target="tpu_custom_call" | custom-call | flops 2048000 | tf_op jit(solution)/shard_map/pallas_call | solution.py:416
  (1 shorter events, 0.0 us)
Async XLA Ops:
  0.6 1.1 %copy-start = (f32[3,8,64,128]{3,2,1,0:T(8,128)S(1)}, f32[3,8,64,128]{3,2,1,0:T(8,128)}, u32[]{:S(2)}) copy-start(f32[3,8,64,128]{3,2,1,0:T(8,128)} %vel_ref.3) | copy-start | bytes 2359300
  2.0 4.9 %collective-permute-start.1 = (f32[3,2,64,128]{3,2,1,0:T(8,128)S(1)}, f32[3,2,64,128]{3,2,1,0:T(8,128)S(1)}, u32[]{:S(2)}, u32[]{:S(2)}) collective-permute-start(f32[3,2,64,128]{3,2,1,0:T(8,128)S(1)} %get-tuple-element.27), channel_id=1, source_target_pairs={{0,4},{4,0},{8,12},{12,8},{16,20},{20,16},{24,28},{28,24},{1,5},{5... | collective-permute-start | bytes 589832 | tf_op jit(solution)/shard_map/ppermute | solution.py:458
  2.5 16.2 %collective-permute-start.4 = (f32[3,2,64,128]{3,2,1,0:T(8,128)S(1)}, f32[3,2,64,128]{3,2,1,0:T(8,128)S(1)}, u32[]{:S(2)}, u32[]{:S(2)}) collective-permute-start(f32[3,2,64,128]{3,2,1,0:T(8,128)S(1)} %get-tuple-element.31), channel_id=1, source_target_pairs={{0,28},{4,8},{8,4},{12,16},{16,12},{20,24},{24,20},{28,0},{1,29},{... | collective-permute-start | bytes 589832 | tf_op jit(solution)/shard_map/ppermute | solution.py:459
  6.1 4.8 %collective-permute-start = (f32[16,128]{1,0:T(8,128)S(1)}, f32[16,128]{1,0:T(8,128)S(1)}, u32[]{:S(2)}, u32[]{:S(2)}) collective-permute-start(f32[16,128]{1,0:T(8,128)S(1)} %get-tuple-element.26), channel_id=1, source_target_pairs={{0,28},{4,8},{8,4},{12,16},{16,12},{20,24},{24,20},{28,0},{1,29},{... | collective-permute-start | bytes 24584 | tf_op jit(solution)/shard_map/ppermute | solution.py:457
  10.9 8.9 %collective-permute-start.2 = (f32[80,128]{1,0:T(8,128)S(1)}, f32[80,128]{1,0:T(8,128)S(1)}, u32[]{:S(2)}, u32[]{:S(2)}) collective-permute-start(f32[80,128]{1,0:T(8,128)S(1)} %shard_map.33), channel_id=1, source_target_pairs={{0,1},{1,0},{2,3},{3,2},{4,5},{5,4},{6,7},{7,6},{8,9},{9,8},{10,11... | collective-permute-start | bytes 122888 | tf_op jit(solution)/shard_map/ppermute | solution.py:467
  12.8 7.0 %collective-permute-start.3 = (f32[80,128]{1,0:T(8,128)S(1)}, f32[80,128]{1,0:T(8,128)S(1)}, u32[]{:S(2)}, u32[]{:S(2)}) collective-permute-start(f32[80,128]{1,0:T(8,128)S(1)} %shard_map.33), channel_id=1, source_target_pairs={{0,3},{1,2},{2,1},{3,0},{4,7},{5,6},{6,5},{7,4},{8,11},{9,10},{10,... | collective-permute-start | bytes 122888 | tf_op jit(solution)/shard_map/ppermute | solution.py:466

commit v7 on v6

--- a/solution.py
+++ b/solution.py
@@ -199,10 +199,14 @@
     return numer, denom
 
 
-def strain_planes(ln, u_ref, mag_ref, tmp_ref, keep_ref, fz_ref, start, stop):
+def strain_planes(
+    ln, u_ref, mag_ref, tmp_ref, keep_ref, fz_ref, start, stop, with_outer=False
+):
     windows = mag_ref.shape[1] // ROWS
 
     def plane(i):
+        if with_outer:
+            outer_size(ln, u_ref, mag_ref, i)
         for k in range(1, windows):
             strain(ln, u_ref, mag_ref, tmp_ref, keep_ref, lax.rem(i, 2), i, k)
 
@@ -220,8 +224,10 @@
     products(stop - 1)
 
 
-def sum_planes(ln, hu_ref, fz_ref, acc_ref, start, stop):
+def sum_planes(ln, hu_ref, fz_ref, acc_ref, start, stop, beside=None):
     def step(x, carry):
+        if beside is not None:
+            beside(x)
         for k in range(1, fz_ref.shape[2] // ROWS):
             carry = add_sums(ln, hu_ref, fz_ref, x, k, carry)
         return carry
@@ -324,13 +330,15 @@
         return carry
 
     lax.fori_loop(start, start + nx, hat_x, 0)
-    strain_planes(ln, u_ref, mag_ref, tmp_ref, keep_ref, fz_ref, start, start + nx)
+    strain_planes(ln, u_ref, mag_ref, tmp_ref, keep_ref, fz_ref, start, start + nx, True)
     acc_ref[...] = jnp.zeros_like(acc_ref)
-    sum_planes(ln, hu_ref, fz_ref, acc_ref, start, start + nx - WIDTH)
     inner = jnp.maximum(start - 1, 0)
-    for n in range(nx - 1):
-        outer_size(ln, u_ref, mag_ref, inner + n + 1)
-    unfold_planes(ln, mag_ref, plain_ref, inner, nx - 1)
+
+    def unfold(x):
+        unfold_planes(ln, mag_ref, plain_ref, inner + x - start, 1)
+
+    sum_planes(ln, hu_ref, fz_ref, acc_ref, start, start + nx - WIDTH, unfold)
+    unfold_planes(ln, mag_ref, plain_ref, inner + nx - WIDTH, 1)
 
 
 def sides_kernel(

time: 31.7 us -> 31.8 us (level)
  no operation moved by 1% of the time
where the time goes in v7:
time: 31.8 us; the launch traced here: 31.6 us
  blocking collectives  10 us (31%)
  starting transfers between devices  8.5 us (27%)
  Pallas kernels  7.5 us (24%)
  waiting for transfers between devices  3.75 us (12%)
  local copies, waits for them, and re-layouts  1.13 us (4%)
  between operations  0.69 us (2%)
    all_to_all x1, blocking collectives, on_device(): parts = lax.all_to_all(sums, ('gx', 'gz'), 0, 0, tiled=True)  10 us
    pallas_call x8, Pallas kernels, call(): pl.pallas_call(kernel, out_shape=tuple((jax.ShapeDtypeStruct(shape, jnp.f...  7.5 us
    ppermute x1, waiting for transfers between devices, on_device(): strip = lax.ppermute(strip, 'gx', to_second)  3.74 us
    ppermute x1, starting transfers between devices, on_device(): second = lax.ppermute(second, 'gx', to_second)  3.54 us
    ppermute x1, starting transfers between devices, on_device(): low = lax.ppermute(edges, 'gz', to_second)  2.47 us
    ppermute x1, starting transfers between devices, on_device(): high = lax.ppermute(edges, 'gz', to_first)  1.89 us
    unnamed x2, local copies, waits for them, and re-layouts  1.13 us
  transfers between devices with their start and end apart: 5, of which 1 were waited for; matrix products, arithmetic and copies ran while one was open for 0% of the time, Pallas kernels for 18%

profile of v7, /device:TPU:0, one launch (start us, length us, event | category | flops | bytes accessed | tf_op | source)
XLA Modules:
  0.0 31.6 jit_solution(2698895505415620864)
XLA Ops:
  0.6 0.0 copy-start
  0.6 1.1 %copy-done = f32[3,8,64,128]{3,2,1,0:T(8,128)S(1)} copy-done((f32[3,8,64,128]{3,2,1,0:T(8,128)S(1)}, f32[3,8,64,128]{3,2,1,0:T(8,128)}, u32[]{:S(2)}) %copy-start) | copy-done | bytes 786456
  1.8 0.2 shard_map.30
  2.0 0.5 %collective-permute-start.1 = (f32[3,2,64,128]{3,2,1,0:T(8,128)S(1)}, f32[3,2,64,128]{3,2,1,0:T(8,128)S(1)}, u32[]{:S(2)}, u32[]{:S(2)}) collective-permute-start(f32[3,2,64,128]{3,2,1,0:T(8,128)S(1)} %get-tuple-element.27), channel_id=1, source_target_pairs={{0,4},{4,0},{8,12},{12,8},{16,20},{20,16},{24,28},{28,24},{1,5},{5... | collective-permute-start | bytes 589832 | tf_op jit(solution)/shard_map/ppermute | solution.py:466
  2.5 3.5 %collective-permute-start.4 = (f32[3,2,64,128]{3,2,1,0:T(8,128)S(1)}, f32[3,2,64,128]{3,2,1,0:T(8,128)S(1)}, u32[]{:S(2)}, u32[]{:S(2)}) collective-permute-start(f32[3,2,64,128]{3,2,1,0:T(8,128)S(1)} %get-tuple-element.31), channel_id=1, source_target_pairs={{0,28},{4,8},{8,4},{12,16},{16,12},{20,24},{24,20},{28,0},{1,29},{... | collective-permute-start | bytes 589832 | tf_op jit(solution)/shard_map/ppermute | solution.py:467
  6.1 0.0 collective-permute-start
  6.1 0.8 %shard_map.31 = (f32[3,12,88,128]{3,2,1,0:T(8,128)S(1)}, f32[80,128]{1,0:T(8,128)S(1)}) custom-call(f32[3,8,64,128]{3,2,1,0:T(8,128)S(1)} %copy-done), custom_call_target="tpu_custom_call" | custom-call | flops 4915200 | tf_op jit(solution)/shard_map/pallas_call | solution.py:424
  6.9 0.0 collective-permute-done.1.first_ref
  6.9 0.2 shard_map.32
  7.1 3.7 %collective-permute-done.strip_ref = f32[16,128]{1,0:T(8,128)S(1)} collective-permute-done((f32[16,128]{1,0:T(8,128)S(1)}, f32[16,128]{1,0:T(8,128)S(1)}, u32[]{:S(2)}, u32[]{:S(2)}) %collective-permute-start) | collective-permute-done | bytes 8224 | tf_op jit(solution)/shard_map/ppermute | solution.py:465
  10.9 1.9 %collective-permute-start.2 = (f32[80,128]{1,0:T(8,128)S(1)}, f32[80,128]{1,0:T(8,128)S(1)}, u32[]{:S(2)}, u32[]{:S(2)}) collective-permute-start(f32[80,128]{1,0:T(8,128)S(1)} %shard_map.33), channel_id=1, source_target_pairs={{0,1},{1,0},{2,3},{3,2},{4,5},{5,4},{6,7},{7,6},{8,9},{9,8},{10,11... | collective-permute-start | bytes 122888 | tf_op jit(solution)/shard_map/ppermute | solution.py:475
  12.8 2.5 %collective-permute-start.3 = (f32[80,128]{1,0:T(8,128)S(1)}, f32[80,128]{1,0:T(8,128)S(1)}, u32[]{:S(2)}, u32[]{:S(2)}) collective-permute-start(f32[80,128]{1,0:T(8,128)S(1)} %shard_map.33), channel_id=1, source_target_pairs={{0,3},{1,2},{2,1},{3,0},{4,7},{5,6},{6,5},{7,4},{8,11},{9,10},{10,... | collective-permute-start | bytes 122888 | tf_op jit(solution)/shard_map/ppermute | solution.py:474
  15.3 3.5 %shard_map.34 = (f32[12,10,16,128]{3,2,1,0:T(8,128)S(1)}, f32[12,10,64,128]{3,2,1,0:T(8,128)S(1)}, f32[3,12,72,128]{3,2,1,0:T(8,128)S(1)}, f32[3,10,72,128]{3,2,...) custom-call(f32[3,12,88,128]{3,2,1,0:T(8,128)S(1)} %get-tuple-element.32.u_ref._0), custom_call_target="tpu_custom_call" | custom-call | flops 24576000 | tf_op jit(solution)/shard_map/pallas_call | solution.py:424
  18.8 0.0 collective-permute-done.4.second_ref
  18.8 1.1 %shard_map.35 = (f32[3,12,88,128]{3,2,1,0:T(8,128)S(1)}, f32[12,10,16,128]{3,2,1,0:T(8,128)S(1)}, f32[12,10,64,128]{3,2,1,0:T(8,128)S(1)}, f32[3,12,72,128]{3,2,...) custom-call(f32[3,2,64,128]{3,2,1,0:T(8,128)S(1)} %collective-permut, ...), custom_call_target="tpu_custom_call", output_to_operand_aliasing={{0}: (1, {}), {1}: (2, {}), {2}: (3, {}), {3}: (4, {}), {4}... | custom-call | flops 8192000 | tf_op jit(solution)/shard_map/pallas_call | solution.py:424
  19.9 0.0 collective-permute-done.2.first_ref
  19.9 0.0 collective-permute-done.3.second_ref
  19.9 0.6 %shard_map.36 = (f32[3,12,88,128]{3,2,1,0:T(8,128)S(1)}, f32[12,10,16,128]{3,2,1,0:T(8,128)S(1)}, f32[3,10,72,128]{3,2,1,0:T(8,128)S(1)}, f32[10,72,128]{2,1,0:T...) custom-call(f32[80,128]{1,0:T(8,128)S(1)} %collective-permute-done.2, ...), custom_call_target="tpu_custom_call", output_to_operand_aliasing={{0}: (2, {}), {1}: (3, {}), {2}: (4, {}), {3}: (5, {}), {4}... | custom-call | flops 4096000 | tf_op jit(solution)/shard_map/pallas_call | solution.py:424
  20.5 10.0 %all_to_all.11 = f32[32,1,128]{2,1,0:T(1,128)S(1)} all-to-all(f32[32,1,128]{2,1,0:T(1,128)S(1)} %bitcast.6), channel_id=1, replica_groups=mesh['gx'=8,'gz'=4] {'gx','gz'}, dimensions={0} | all-to-all | bytes 32768 | tf_op jit(solution)/shard_map/all_to_all | solution.py:498
  30.5 1.1 %shard_map.37 = (f32[1,64]{1,0:T(1,128)}, f32[8,64,128]{2,1,0:T(8,128)}) custom-call(f32[32,128]{1,0:T(8,128)S(1)} %bitcast.5, f32[8,64,128]{2,1,0:T(8,128)S(1)} %get-tuple-element.46.mag_ref, f32[8,128]{1,0:T(8,128)S(1)} %get-tuple-element.47.outer_ref), custom_call_target="tpu_custom_call" | custom-call | flops 2048000 | tf_op jit(solution)/shard_map/pallas_call | solution.py:424
  (1 shorter events, 0.0 us)
Async XLA Ops:
  0.6 1.1 %copy-start = (f32[3,8,64,128]{3,2,1,0:T(8,128)S(1)}, f32[3,8,64,128]{3,2,1,0:T(8,128)}, u32[]{:S(2)}) copy-start(f32[3,8,64,128]{3,2,1,0:T(8,128)} %vel_ref.3) | copy-start | bytes 2359300
  2.0 4.9 %collective-permute-start.1 = (f32[3,2,64,128]{3,2,1,0:T(8,128)S(1)}, f32[3,2,64,128]{3,2,1,0:T(8,128)S(1)}, u32[]{:S(2)}, u32[]{:S(2)}) collective-permute-start(f32[3,2,64,128]{3,2,1,0:T(8,128)S(1)} %get-tuple-element.27), channel_id=1, source_target_pairs={{0,4},{4,0},{8,12},{12,8},{16,20},{20,16},{24,28},{28,24},{1,5},{5... | collective-permute-start | bytes 589832 | tf_op jit(solution)/shard_map/ppermute | solution.py:466
  2.5 16.3 %collective-permute-start.4 = (f32[3,2,64,128]{3,2,1,0:T(8,128)S(1)}, f32[3,2,64,128]{3,2,1,0:T(8,128)S(1)}, u32[]{:S(2)}, u32[]{:S(2)}) collective-permute-start(f32[3,2,64,128]{3,2,1,0:T(8,128)S(1)} %get-tuple-element.31), channel_id=1, source_target_pairs={{0,28},{4,8},{8,4},{12,16},{16,12},{20,24},{24,20},{28,0},{1,29},{... | collective-permute-start | bytes 589832 | tf_op jit(solution)/shard_map/ppermute | solution.py:467
  6.1 4.8 %collective-permute-start = (f32[16,128]{1,0:T(8,128)S(1)}, f32[16,128]{1,0:T(8,128)S(1)}, u32[]{:S(2)}, u32[]{:S(2)}) collective-permute-start(f32[16,128]{1,0:T(8,128)S(1)} %get-tuple-element.26), channel_id=1, source_target_pairs={{0,28},{4,8},{8,4},{12,16},{16,12},{20,24},{24,20},{28,0},{1,29},{... | collective-permute-start | bytes 24584 | tf_op jit(solution)/shard_map/ppermute | solution.py:465
  10.9 9.0 %collective-permute-start.2 = (f32[80,128]{1,0:T(8,128)S(1)}, f32[80,128]{1,0:T(8,128)S(1)}, u32[]{:S(2)}, u32[]{:S(2)}) collective-permute-start(f32[80,128]{1,0:T(8,128)S(1)} %shard_map.33), channel_id=1, source_target_pairs={{0,1},{1,0},{2,3},{3,2},{4,5},{5,4},{6,7},{7,6},{8,9},{9,8},{10,11... | collective-permute-start | bytes 122888 | tf_op jit(solution)/shard_map/ppermute | solution.py:475
  12.8 7.1 %collective-permute-start.3 = (f32[80,128]{1,0:T(8,128)S(1)}, f32[80,128]{1,0:T(8,128)S(1)}, u32[]{:S(2)}, u32[]{:S(2)}) collective-permute-start(f32[80,128]{1,0:T(8,128)S(1)} %shard_map.33), channel_id=1, source_target_pairs={{0,3},{1,2},{2,1},{3,0},{4,7},{5,6},{6,5},{7,4},{8,11},{9,10},{10,... | collective-permute-start | bytes 122888 | tf_op jit(solution)/shard_map/ppermute | solution.py:474

commit v8 on v7

--- a/solution.py
+++ b/solution.py
@@ -112,17 +112,22 @@
         )
 
 
-def strain(ln, u_ref, mag_ref, tmp_ref, keep_ref, slot, i, k):
+def strain(ln, u_ref, mag_ref, tmp_ref, keep_ref, slot, i, k, hz_ref=None):
     at = ROWS * (k + 1)
-    mid = [u_ref[comp, i + 1, ln.rows(at)] for comp in range(3)]
+    before, mid, after = [
+        [u_ref[comp, i + 1, ln.rows(at + step)] for comp in range(3)] for step in (-1, 0, 1)
+    ]
     slopes = [
         (
             u_ref[comp, i + 2, ln.rows(at)] - u_ref[comp, i, ln.rows(at)],
             ln.slope_y(mid[comp]),
-            ln.slope_z(u_ref[comp, i + 1, ln.rows(at + 1)], u_ref[comp, i + 1, ln.rows(at - 1)]),
+            ln.slope_z(after[comp], before[comp]),
         )
         for comp in range(3)
     ]
+    if hz_ref is not None:
+        for comp in range(3):
+            hz_ref[comp, i + 1, window(k)] = weighted(before[comp], mid[comp], after[comp])
     rate, size = rates(slopes)
     mag_ref[i, window(k)] = size
     scaled = size * 0.0625
@@ -200,15 +205,15 @@
 
 
 def strain_planes(
-    ln, u_ref, mag_ref, tmp_ref, keep_ref, fz_ref, start, stop, with_outer=False
+    ln, u_ref, mag_ref, tmp_ref, keep_ref, fz_ref, start, stop, hz_ref=None
 ):
     windows = mag_ref.shape[1] // ROWS
 
     def plane(i):
-        if with_outer:
+        if hz_ref is not None:
             outer_size(ln, u_ref, mag_ref, i)
         for k in range(1, windows):
-            strain(ln, u_ref, mag_ref, tmp_ref, keep_ref, lax.rem(i, 2), i, k)
+            strain(ln, u_ref, mag_ref, tmp_ref, keep_ref, lax.rem(i, 2), i, k, hz_ref)
 
     def products(i):
         for k in range(1, windows - 1):
@@ -317,12 +322,10 @@
     ln = Lanes(u_ref.shape[3])
     start, _ = near_slots(nx)
 
-    def hat_z(slot, carry):
+    for slot in (start, start + nx + 1):
         for k in range(1, windows):
             filter_z(ln, u_ref, hz_ref, slot, k)
-        return carry
-
-    lax.fori_loop(start, start + nx + WIDTH, hat_z, 0)
+    strain_planes(ln, u_ref, mag_ref, tmp_ref, keep_ref, fz_ref, start, start + nx, hz_ref)
 
     def hat_x(i, carry):
         for k in range(1, windows):
@@ -330,7 +333,6 @@
         return carry
 
     lax.fori_loop(start, start + nx, hat_x, 0)
-    strain_planes(ln, u_ref, mag_ref, tmp_ref, keep_ref, fz_ref, start, start + nx, True)
     acc_ref[...] = jnp.zeros_like(acc_ref)
     inner = jnp.maximum(start - 1, 0)
 

time: 31.8 us -> 31.7 us (level)
  no operation moved by 1% of the time
where the time goes in v8:
time: 31.7 us; the launch traced here: 31.5 us
  blocking collectives  10 us (32%)
  starting transfers between devices  8.5 us (27%)
  Pallas kernels  7.44 us (23%)
  waiting for transfers between devices  3.75 us (12%)
  local copies, waits for them, and re-layouts  1.13 us (4%)
  between operations  0.69 us (2%)
    all_to_all x1, blocking collectives, on_device(): parts = lax.all_to_all(sums, ('gx', 'gz'), 0, 0, tiled=True)  10 us
    pallas_call x8, Pallas kernels, call(): pl.pallas_call(kernel, out_shape=tuple((jax.ShapeDtypeStruct(shape, jnp.f...  7.44 us
    ppermute x1, waiting for transfers between devices, on_device(): strip = lax.ppermute(strip, 'gx', to_second)  3.74 us
    ppermute x1, starting transfers between devices, on_device(): second = lax.ppermute(second, 'gx', to_second)  3.54 us
    ppermute x1, starting transfers between devices, on_device(): low = lax.ppermute(edges, 'gz', to_second)  2.47 us
    ppermute x1, starting transfers between devices, on_device(): high = lax.ppermute(edges, 'gz', to_first)  1.89 us
    unnamed x2, local copies, waits for them, and re-layouts  1.13 us
  transfers between devices with their start and end apart: 5, of which 1 were waited for; matrix products, arithmetic and copies ran while one was open for 0% of the time, Pallas kernels for 18%

profile of v8, /device:TPU:0, one launch (start us, length us, event | category | flops | bytes accessed | tf_op | source)
XLA Modules:
  0.0 31.5 jit_solution(8855937056784467153)
XLA Ops:
  0.6 0.0 copy-start
  0.6 1.1 %copy-done = f32[3,8,64,128]{3,2,1,0:T(8,128)S(1)} copy-done((f32[3,8,64,128]{3,2,1,0:T(8,128)S(1)}, f32[3,8,64,128]{3,2,1,0:T(8,128)}, u32[]{:S(2)}) %copy-start) | copy-done | bytes 786456
  1.8 0.2 shard_map.30
  2.0 0.5 %collective-permute-start.1 = (f32[3,2,64,128]{3,2,1,0:T(8,128)S(1)}, f32[3,2,64,128]{3,2,1,0:T(8,128)S(1)}, u32[]{:S(2)}, u32[]{:S(2)}) collective-permute-start(f32[3,2,64,128]{3,2,1,0:T(8,128)S(1)} %get-tuple-element.27), channel_id=1, source_target_pairs={{0,4},{4,0},{8,12},{12,8},{16,20},{20,16},{24,28},{28,24},{1,5},{5... | collective-permute-start | bytes 589832 | tf_op jit(solution)/shard_map/ppermute | solution.py:468
  2.5 3.5 %collective-permute-start.4 = (f32[3,2,64,128]{3,2,1,0:T(8,128)S(1)}, f32[3,2,64,128]{3,2,1,0:T(8,128)S(1)}, u32[]{:S(2)}, u32[]{:S(2)}) collective-permute-start(f32[3,2,64,128]{3,2,1,0:T(8,128)S(1)} %get-tuple-element.31), channel_id=1, source_target_pairs={{0,28},{4,8},{8,4},{12,16},{16,12},{20,24},{24,20},{28,0},{1,29},{... | collective-permute-start | bytes 589832 | tf_op jit(solution)/shard_map/ppermute | solution.py:469
  6.1 0.0 collective-permute-start
  6.1 0.8 %shard_map.31 = (f32[3,12,88,128]{3,2,1,0:T(8,128)S(1)}, f32[80,128]{1,0:T(8,128)S(1)}) custom-call(f32[3,8,64,128]{3,2,1,0:T(8,128)S(1)} %copy-done), custom_call_target="tpu_custom_call" | custom-call | flops 4915200 | tf_op jit(solution)/shard_map/pallas_call | solution.py:426
  6.9 0.0 collective-permute-done.1.first_ref
  6.9 0.2 shard_map.32
  7.1 3.7 %collective-permute-done.strip_ref = f32[16,128]{1,0:T(8,128)S(1)} collective-permute-done((f32[16,128]{1,0:T(8,128)S(1)}, f32[16,128]{1,0:T(8,128)S(1)}, u32[]{:S(2)}, u32[]{:S(2)}) %collective-permute-start) | collective-permute-done | bytes 8224 | tf_op jit(solution)/shard_map/ppermute | solution.py:467
  10.9 1.9 %collective-permute-start.2 = (f32[80,128]{1,0:T(8,128)S(1)}, f32[80,128]{1,0:T(8,128)S(1)}, u32[]{:S(2)}, u32[]{:S(2)}) collective-permute-start(f32[80,128]{1,0:T(8,128)S(1)} %shard_map.33), channel_id=1, source_target_pairs={{0,1},{1,0},{2,3},{3,2},{4,5},{5,4},{6,7},{7,6},{8,9},{9,8},{10,11... | collective-permute-start | bytes 122888 | tf_op jit(solution)/shard_map/ppermute | solution.py:477
  12.8 2.5 %collective-permute-start.3 = (f32[80,128]{1,0:T(8,128)S(1)}, f32[80,128]{1,0:T(8,128)S(1)}, u32[]{:S(2)}, u32[]{:S(2)}) collective-permute-start(f32[80,128]{1,0:T(8,128)S(1)} %shard_map.33), channel_id=1, source_target_pairs={{0,3},{1,2},{2,1},{3,0},{4,7},{5,6},{6,5},{7,4},{8,11},{9,10},{10,... | collective-permute-start | bytes 122888 | tf_op jit(solution)/shard_map/ppermute | solution.py:476
  15.3 3.5 %shard_map.34 = (f32[12,10,16,128]{3,2,1,0:T(8,128)S(1)}, f32[12,10,64,128]{3,2,1,0:T(8,128)S(1)}, f32[3,12,72,128]{3,2,1,0:T(8,128)S(1)}, f32[3,10,72,128]{3,2,...) custom-call(f32[3,12,88,128]{3,2,1,0:T(8,128)S(1)} %get-tuple-element.32.u_ref._0), custom_call_target="tpu_custom_call" | custom-call | flops 24576000 | tf_op jit(solution)/shard_map/pallas_call | solution.py:426
  18.7 0.0 collective-permute-done.4.second_ref
  18.7 1.1 %shard_map.35 = (f32[3,12,88,128]{3,2,1,0:T(8,128)S(1)}, f32[12,10,16,128]{3,2,1,0:T(8,128)S(1)}, f32[12,10,64,128]{3,2,1,0:T(8,128)S(1)}, f32[3,12,72,128]{3,2,...) custom-call(f32[3,2,64,128]{3,2,1,0:T(8,128)S(1)} %collective-permut, ...), custom_call_target="tpu_custom_call", output_to_operand_aliasing={{0}: (1, {}), {1}: (2, {}), {2}: (3, {}), {3}: (4, {}), {4}... | custom-call | flops 8192000 | tf_op jit(solution)/shard_map/pallas_call | solution.py:426
  19.8 0.0 collective-permute-done.2.first_ref
  19.8 0.0 collective-permute-done.3.second_ref
  19.8 0.6 %shard_map.36 = (f32[3,12,88,128]{3,2,1,0:T(8,128)S(1)}, f32[12,10,16,128]{3,2,1,0:T(8,128)S(1)}, f32[3,10,72,128]{3,2,1,0:T(8,128)S(1)}, f32[10,72,128]{2,1,0:T...) custom-call(f32[80,128]{1,0:T(8,128)S(1)} %collective-permute-done.2, ...), custom_call_target="tpu_custom_call", output_to_operand_aliasing={{0}: (2, {}), {1}: (3, {}), {2}: (4, {}), {3}: (5, {}), {4}... | custom-call | flops 4096000 | tf_op jit(solution)/shard_map/pallas_call | solution.py:426
  20.5 10.0 %all_to_all.11 = f32[32,1,128]{2,1,0:T(1,128)S(1)} all-to-all(f32[32,1,128]{2,1,0:T(1,128)S(1)} %bitcast.6), channel_id=1, replica_groups=mesh['gx'=8,'gz'=4] {'gx','gz'}, dimensions={0} | all-to-all | bytes 32768 | tf_op jit(solution)/shard_map/all_to_all | solution.py:500
  30.5 1.1 %shard_map.37 = (f32[1,64]{1,0:T(1,128)}, f32[8,64,128]{2,1,0:T(8,128)}) custom-call(f32[32,128]{1,0:T(8,128)S(1)} %bitcast.5, f32[8,64,128]{2,1,0:T(8,128)S(1)} %get-tuple-element.46.mag_ref, f32[8,128]{1,0:T(8,128)S(1)} %get-tuple-element.47.outer_ref), custom_call_target="tpu_custom_call" | custom-call | flops 2048000 | tf_op jit(solution)/shard_map/pallas_call | solution.py:426
  (1 shorter events, 0.0 us)
Async XLA Ops:
  0.6 1.1 %copy-start = (f32[3,8,64,128]{3,2,1,0:T(8,128)S(1)}, f32[3,8,64,128]{3,2,1,0:T(8,128)}, u32[]{:S(2)}) copy-start(f32[3,8,64,128]{3,2,1,0:T(8,128)} %vel_ref.3) | copy-start | bytes 2359300
  2.0 4.9 %collective-permute-start.1 = (f32[3,2,64,128]{3,2,1,0:T(8,128)S(1)}, f32[3,2,64,128]{3,2,1,0:T(8,128)S(1)}, u32[]{:S(2)}, u32[]{:S(2)}) collective-permute-start(f32[3,2,64,128]{3,2,1,0:T(8,128)S(1)} %get-tuple-element.27), channel_id=1, source_target_pairs={{0,4},{4,0},{8,12},{12,8},{16,20},{20,16},{24,28},{28,24},{1,5},{5... | collective-permute-start | bytes 589832 | tf_op jit(solution)/shard_map/ppermute | solution.py:468
  2.5 16.2 %collective-permute-start.4 = (f32[3,2,64,128]{3,2,1,0:T(8,128)S(1)}, f32[3,2,64,128]{3,2,1,0:T(8,128)S(1)}, u32[]{:S(2)}, u32[]{:S(2)}) collective-permute-start(f32[3,2,64,128]{3,2,1,0:T(8,128)S(1)} %get-tuple-element.31), channel_id=1, source_target_pairs={{0,28},{4,8},{8,4},{12,16},{16,12},{20,24},{24,20},{28,0},{1,29},{... | collective-permute-start | bytes 589832 | tf_op jit(solution)/shard_map/ppermute | solution.py:469
  6.1 4.8 %collective-permute-start = (f32[16,128]{1,0:T(8,128)S(1)}, f32[16,128]{1,0:T(8,128)S(1)}, u32[]{:S(2)}, u32[]{:S(2)}) collective-permute-start(f32[16,128]{1,0:T(8,128)S(1)} %get-tuple-element.26), channel_id=1, source_target_pairs={{0,28},{4,8},{8,4},{12,16},{16,12},{20,24},{24,20},{28,0},{1,29},{... | collective-permute-start | bytes 24584 | tf_op jit(solution)/shard_map/ppermute | solution.py:467
  10.9 8.9 %collective-permute-start.2 = (f32[80,128]{1,0:T(8,128)S(1)}, f32[80,128]{1,0:T(8,128)S(1)}, u32[]{:S(2)}, u32[]{:S(2)}) collective-permute-start(f32[80,128]{1,0:T(8,128)S(1)} %shard_map.33), channel_id=1, source_target_pairs={{0,1},{1,0},{2,3},{3,2},{4,5},{5,4},{6,7},{7,6},{8,9},{9,8},{10,11... | collective-permute-start | bytes 122888 | tf_op jit(solution)/shard_map/ppermute | solution.py:477
  12.8 7.1 %collective-permute-start.3 = (f32[80,128]{1,0:T(8,128)S(1)}, f32[80,128]{1,0:T(8,128)S(1)}, u32[]{:S(2)}, u32[]{:S(2)}) collective-permute-start(f32[80,128]{1,0:T(8,128)S(1)} %shard_map.33), channel_id=1, source_target_pairs={{0,3},{1,2},{2,1},{3,0},{4,7},{5,6},{6,5},{7,4},{8,11},{9,10},{10,... | collective-permute-start | bytes 122888 | tf_op jit(solution)/shard_map/ppermute | solution.py:476

commit v9 on v8

--- a/solution.py
+++ b/solution.py
@@ -368,7 +368,7 @@
 
 def rim_kernel(
     first_ref, second_ref, _1, _2, _3, _4, _5, acc_ref, u_ref, tmp_ref, hu_ref, mag_ref,
-    plain_ref, outer_ref, sums_ref, turned, fz, hz,
+    plain_ref, sums_ref, turned, fz, hz, outer_ref,
 ):
     planes, _, lanes = u_ref.shape[1:]
     nx = planes - 2 * WIDTH
@@ -390,6 +390,15 @@
         filter_x(hz, hu_ref, i, 0)
     for i in range(nx + 2):
         strain(ln, u_ref, mag_ref, tmp_ref, None, i, i, 0)
+    for x in range(nx):
+        outer_ref[x : x + 1] = mag_ref[x + 1, 1:2]
+    unfold_planes(ln, mag_ref, plain_ref, jnp.where(below_is_first("gx"), nx - 1, 0), 1)
+    outer = outer_ref[...].T
+    depth = lax.broadcasted_iota(jnp.int32, plain_ref.shape[1:], 1)
+    for x in range(nx):
+        low, high = outer[:ny, x : x + 1], outer[ny:, x : x + 1]
+        plane = jnp.where(depth == 0, low, plain_ref[x])
+        plain_ref[x] = jnp.where(depth == depth.shape[1] - 1, high, plane)
     for i in range(nx + 2):
         filter_products(ln, tmp_ref, fz, i, i, 0)
     carry = acc_ref[0], acc_ref[1]
@@ -400,12 +409,9 @@
     denom = denom + pltpu.roll(denom, ny, 1)
     both = jnp.where(lax.broadcasted_iota(jnp.int32, (1, lanes), 1) < ny, numer, denom)
     sums_ref[...] = jnp.broadcast_to(both, sums_ref.shape)
-    for x in range(nx):
-        outer_ref[x : x + 1] = mag_ref[x + 1, 1:2]
-    unfold_planes(ln, mag_ref, plain_ref, jnp.where(below_is_first("gx"), nx - 1, 0), 1)
-
-
-def finish_kernel(cells, parts_ref, mag_ref, outer_ref, coefficient_ref, eddy_ref):
+
+
+def finish_kernel(cells, parts_ref, mag_ref, coefficient_ref, eddy_ref):
     lanes = parts_ref.shape[1]
     ny = lanes // 2
     sums = jnp.sum(parts_ref[...], axis=0, keepdims=True)
@@ -414,12 +420,8 @@
     coefficient = numer / cells / (denom / cells + 1e-06)
     coefficient_ref[...] = coefficient
     column = jnp.broadcast_to(coefficient, (mag_ref.shape[2], ny)).T
-    outer = outer_ref[...].T
-    lane = lax.broadcasted_iota(jnp.int32, column.shape, 1)
     for x in range(mag_ref.shape[0]):
-        low, high = outer[:ny, x : x + 1], outer[ny:, x : x + 1]
-        plane = jnp.where(lane == 0, low, mag_ref[x])
-        eddy_ref[x] = column * jnp.where(lane == lane.shape[1] - 1, high, plane)
+        eddy_ref[x] = column * mag_ref[x]
 
 
 def call(kernel, shapes, operands, cycles, aliases=None, scratch=()):
@@ -485,9 +487,9 @@
         window_pair,
     )
     count = lax.axis_size("gx") * lax.axis_size("gz")
-    *_, plain, outer, sums = call(
+    *_, plain, sums = call(
         rim_kernel,
-        (u_shape, work[0], work[3], work[4], (nx, ny, nz), (nx, lanes), (count, lanes)),
+        (u_shape, work[0], work[3], work[4], (nx, ny, nz), (count, lanes)),
         (high, low, u, keep, hu, mag, plain, acc),
         1000,
         {2 + n: n for n in range(5)},
@@ -495,12 +497,13 @@
             (ROWS + edge_rows, lanes),
             (12, nx + 2, ROWS, lanes),
             (3, planes, ROWS, lanes),
+            (nx, lanes),
         ),
     )
     parts = lax.all_to_all(sums, ("gx", "gz"), 0, 0, tiled=True)
     cells = nx * lax.axis_size("gx") * nz * lax.axis_size("gz")
     coefficient, eddy_viscosity = call(
-        functools.partial(finish_kernel, cells), ((1, ny), (nx, ny, nz)), (parts, plain, outer), 500
+        functools.partial(finish_kernel, cells), ((1, ny), (nx, ny, nz)), (parts, plain), 500
     )
     return (coefficient[0], eddy_viscosity)
 

time: 31.7 us -> 31.7 us (level)
  no operation moved by 1% of the time
where the time goes in v9:
time: 31.7 us; the launch traced here: 31.5 us
  blocking collectives  10 us (32%)
  starting transfers between devices  8.5 us (27%)
  Pallas kernels  7.47 us (24%)
  waiting for transfers between devices  3.75 us (12%)
  local copies, waits for them, and re-layouts  1.13 us (4%)
  between operations  0.69 us (2%)
    all_to_all x1, blocking collectives, on_device(): parts = lax.all_to_all(sums, ('gx', 'gz'), 0, 0, tiled=True)  10 us
    pallas_call x8, Pallas kernels, call(): pl.pallas_call(kernel, out_shape=tuple((jax.ShapeDtypeStruct(shape, jnp.f...  7.47 us
    ppermute x1, waiting for transfers between devices, on_device(): strip = lax.ppermute(strip, 'gx', to_second)  3.74 us
    ppermute x1, starting transfers between devices, on_device(): second = lax.ppermute(second, 'gx', to_second)  3.54 us
    ppermute x1, starting transfers between devices, on_device(): low = lax.ppermute(edges, 'gz', to_second)  2.47 us
    ppermute x1, starting transfers between devices, on_device(): high = lax.ppermute(edges, 'gz', to_first)  1.89 us
    unnamed x2, local copies, waits for them, and re-layouts  1.13 us
  transfers between devices with their start and end apart: 5, of which 1 were waited for; matrix products, arithmetic and copies ran while one was open for 0% of the time, Pallas kernels for 18%

profile of v9, /device:TPU:0, one launch (start us, length us, event | category | flops | bytes accessed | tf_op | source)
XLA Modules:
  0.0 31.5 jit_solution(16551798888174219700)
XLA Ops:
  0.6 0.0 copy-start
  0.6 1.1 %copy-done = f32[3,8,64,128]{3,2,1,0:T(8,128)S(1)} copy-done((f32[3,8,64,128]{3,2,1,0:T(8,128)S(1)}, f32[3,8,64,128]{3,2,1,0:T(8,128)}, u32[]{:S(2)}) %copy-start) | copy-done | bytes 786456
  1.8 0.2 shard_map.30
  2.0 0.5 %collective-permute-start.1 = (f32[3,2,64,128]{3,2,1,0:T(8,128)S(1)}, f32[3,2,64,128]{3,2,1,0:T(8,128)S(1)}, u32[]{:S(2)}, u32[]{:S(2)}) collective-permute-start(f32[3,2,64,128]{3,2,1,0:T(8,128)S(1)} %get-tuple-element.26), channel_id=1, source_target_pairs={{0,4},{4,0},{8,12},{12,8},{16,20},{20,16},{24,28},{28,24},{1,5},{5... | collective-permute-start | bytes 589832 | tf_op jit(solution)/shard_map/ppermute | solution.py:470
  2.5 3.5 %collective-permute-start.4 = (f32[3,2,64,128]{3,2,1,0:T(8,128)S(1)}, f32[3,2,64,128]{3,2,1,0:T(8,128)S(1)}, u32[]{:S(2)}, u32[]{:S(2)}) collective-permute-start(f32[3,2,64,128]{3,2,1,0:T(8,128)S(1)} %get-tuple-element.30), channel_id=1, source_target_pairs={{0,28},{4,8},{8,4},{12,16},{16,12},{20,24},{24,20},{28,0},{1,29},{... | collective-permute-start | bytes 589832 | tf_op jit(solution)/shard_map/ppermute | solution.py:471
  6.1 0.0 collective-permute-start
  6.1 0.8 %shard_map.31 = (f32[3,12,88,128]{3,2,1,0:T(8,128)S(1)}, f32[80,128]{1,0:T(8,128)S(1)}) custom-call(f32[3,8,64,128]{3,2,1,0:T(8,128)S(1)} %copy-done), custom_call_target="tpu_custom_call" | custom-call | flops 4915200 | tf_op jit(solution)/shard_map/pallas_call | solution.py:428
  6.9 0.0 collective-permute-done.1.first_ref
  6.9 0.2 shard_map.32
  7.1 3.7 %collective-permute-done.strip_ref = f32[16,128]{1,0:T(8,128)S(1)} collective-permute-done((f32[16,128]{1,0:T(8,128)S(1)}, f32[16,128]{1,0:T(8,128)S(1)}, u32[]{:S(2)}, u32[]{:S(2)}) %collective-permute-start) | collective-permute-done | bytes 8224 | tf_op jit(solution)/shard_map/ppermute | solution.py:469
  10.9 1.9 %collective-permute-start.2 = (f32[80,128]{1,0:T(8,128)S(1)}, f32[80,128]{1,0:T(8,128)S(1)}, u32[]{:S(2)}, u32[]{:S(2)}) collective-permute-start(f32[80,128]{1,0:T(8,128)S(1)} %shard_map.33), channel_id=1, source_target_pairs={{0,1},{1,0},{2,3},{3,2},{4,5},{5,4},{6,7},{7,6},{8,9},{9,8},{10,11... | collective-permute-start | bytes 122888 | tf_op jit(solution)/shard_map/ppermute | solution.py:479
  12.8 2.5 %collective-permute-start.3 = (f32[80,128]{1,0:T(8,128)S(1)}, f32[80,128]{1,0:T(8,128)S(1)}, u32[]{:S(2)}, u32[]{:S(2)}) collective-permute-start(f32[80,128]{1,0:T(8,128)S(1)} %shard_map.33), channel_id=1, source_target_pairs={{0,3},{1,2},{2,1},{3,0},{4,7},{5,6},{6,5},{7,4},{8,11},{9,10},{10,... | collective-permute-start | bytes 122888 | tf_op jit(solution)/shard_map/ppermute | solution.py:478
  15.3 3.5 %shard_map.34 = (f32[12,10,16,128]{3,2,1,0:T(8,128)S(1)}, f32[12,10,64,128]{3,2,1,0:T(8,128)S(1)}, f32[3,12,72,128]{3,2,1,0:T(8,128)S(1)}, f32[3,10,72,128]{3,2,...) custom-call(f32[3,12,88,128]{3,2,1,0:T(8,128)S(1)} %get-tuple-element.31.u_ref._0), custom_call_target="tpu_custom_call" | custom-call | flops 24576000 | tf_op jit(solution)/shard_map/pallas_call | solution.py:428
  18.7 0.0 collective-permute-done.4.second_ref
  18.7 1.1 %shard_map.35 = (f32[3,12,88,128]{3,2,1,0:T(8,128)S(1)}, f32[12,10,16,128]{3,2,1,0:T(8,128)S(1)}, f32[12,10,64,128]{3,2,1,0:T(8,128)S(1)}, f32[3,12,72,128]{3,2,...) custom-call(f32[3,2,64,128]{3,2,1,0:T(8,128)S(1)} %collective-permut, ...), custom_call_target="tpu_custom_call", output_to_operand_aliasing={{0}: (1, {}), {1}: (2, {}), {2}: (3, {}), {3}: (4, {}), {4}... | custom-call | flops 8192000 | tf_op jit(solution)/shard_map/pallas_call | solution.py:428
  19.8 0.0 collective-permute-done.2.first_ref
  19.8 0.0 collective-permute-done.3.second_ref
  19.8 0.8 %shard_map.36 = (f32[3,12,88,128]{3,2,1,0:T(8,128)S(1)}, f32[12,10,16,128]{3,2,1,0:T(8,128)S(1)}, f32[3,10,72,128]{3,2,1,0:T(8,128)S(1)}, f32[10,72,128]{2,1,0:T...) custom-call(f32[80,128]{1,0:T(8,128)S(1)} %collective-permute-done.2, ...), custom_call_target="tpu_custom_call", output_to_operand_aliasing={{0}: (2, {}), {1}: (3, {}), {2}: (4, {}), {3}: (5, {}), {4}... | custom-call | flops 4096000 | tf_op jit(solution)/shard_map/pallas_call | solution.py:428
  20.7 10.0 %all_to_all.11 = f32[32,1,128]{2,1,0:T(1,128)S(1)} all-to-all(f32[32,1,128]{2,1,0:T(1,128)S(1)} %bitcast.6), channel_id=1, replica_groups=mesh['gx'=8,'gz'=4] {'gx','gz'}, dimensions={0} | all-to-all | bytes 32768 | tf_op jit(solution)/shard_map/all_to_all | solution.py:503
  30.7 0.9 %shard_map.37 = (f32[1,64]{1,0:T(1,128)}, f32[8,64,128]{2,1,0:T(8,128)}) custom-call(f32[32,128]{1,0:T(8,128)S(1)} %bitcast.5, f32[8,64,128]{2,1,0:T(8,128)S(1)} %get-tuple-element.45.mag_ref), custom_call_target="tpu_custom_call" | custom-call | flops 2048000 | tf_op jit(solution)/shard_map/pallas_call | solution.py:428
  (1 shorter events, 0.0 us)
Async XLA Ops:
  0.6 1.1 %copy-start = (f32[3,8,64,128]{3,2,1,0:T(8,128)S(1)}, f32[3,8,64,128]{3,2,1,0:T(8,128)}, u32[]{:S(2)}) copy-start(f32[3,8,64,128]{3,2,1,0:T(8,128)} %vel_ref.3) | copy-start | bytes 2359300
  2.0 4.9 %collective-permute-start.1 = (f32[3,2,64,128]{3,2,1,0:T(8,128)S(1)}, f32[3,2,64,128]{3,2,1,0:T(8,128)S(1)}, u32[]{:S(2)}, u32[]{:S(2)}) collective-permute-start(f32[3,2,64,128]{3,2,1,0:T(8,128)S(1)} %get-tuple-element.26), channel_id=1, source_target_pairs={{0,4},{4,0},{8,12},{12,8},{16,20},{20,16},{24,28},{28,24},{1,5},{5... | collective-permute-start | bytes 589832 | tf_op jit(solution)/shard_map/ppermute | solution.py:470
  2.5 16.2 %collective-permute-start.4 = (f32[3,2,64,128]{3,2,1,0:T(8,128)S(1)}, f32[3,2,64,128]{3,2,1,0:T(8,128)S(1)}, u32[]{:S(2)}, u32[]{:S(2)}) collective-permute-start(f32[3,2,64,128]{3,2,1,0:T(8,128)S(1)} %get-tuple-element.30), channel_id=1, source_target_pairs={{0,28},{4,8},{8,4},{12,16},{16,12},{20,24},{24,20},{28,0},{1,29},{... | collective-permute-start | bytes 589832 | tf_op jit(solution)/shard_map/ppermute | solution.py:471
  6.1 4.8 %collective-permute-start = (f32[16,128]{1,0:T(8,128)S(1)}, f32[16,128]{1,0:T(8,128)S(1)}, u32[]{:S(2)}, u32[]{:S(2)}) collective-permute-start(f32[16,128]{1,0:T(8,128)S(1)} %get-tuple-element.25), channel_id=1, source_target_pairs={{0,28},{4,8},{8,4},{12,16},{16,12},{20,24},{24,20},{28,0},{1,29},{... | collective-permute-start | bytes 24584 | tf_op jit(solution)/shard_map/ppermute | solution.py:469
  10.9 8.9 %collective-permute-start.2 = (f32[80,128]{1,0:T(8,128)S(1)}, f32[80,128]{1,0:T(8,128)S(1)}, u32[]{:S(2)}, u32[]{:S(2)}) collective-permute-start(f32[80,128]{1,0:T(8,128)S(1)} %shard_map.33), channel_id=1, source_target_pairs={{0,1},{1,0},{2,3},{3,2},{4,5},{5,4},{6,7},{7,6},{8,9},{9,8},{10,11... | collective-permute-start | bytes 122888 | tf_op jit(solution)/shard_map/ppermute | solution.py:479
  12.8 7.1 %collective-permute-start.3 = (f32[80,128]{1,0:T(8,128)S(1)}, f32[80,128]{1,0:T(8,128)S(1)}, u32[]{:S(2)}, u32[]{:S(2)}) collective-permute-start(f32[80,128]{1,0:T(8,128)S(1)} %shard_map.33), channel_id=1, source_target_pairs={{0,3},{1,2},{2,1},{3,0},{4,7},{5,6},{6,5},{7,4},{8,11},{9,10},{10,... | collective-permute-start | bytes 122888 | tf_op jit(solution)/shard_map/ppermute | solution.py:478

commit v10 on v9

--- a/solution.py
+++ b/solution.py
@@ -405,18 +405,19 @@
     for x in range(nx):
         carry = add_sums(ln, hu_ref, fz, x, 0, carry)
     numer, denom = [jnp.sum(part, axis=0, keepdims=True) for part in carry]
-    numer = numer + pltpu.roll(numer, ny, 1)
-    denom = denom + pltpu.roll(denom, ny, 1)
-    both = jnp.where(lax.broadcasted_iota(jnp.int32, (1, lanes), 1) < ny, numer, denom)
-    sums_ref[...] = jnp.broadcast_to(both, sums_ref.shape)
+    row = lax.broadcasted_iota(jnp.int32, sums_ref.shape, 0)
+    sums_ref[...] = jnp.where(lax.rem(row, 2) == 0, numer, denom)
 
 
 def finish_kernel(cells, parts_ref, mag_ref, coefficient_ref, eddy_ref):
     lanes = parts_ref.shape[1]
     ny = lanes // 2
-    sums = jnp.sum(parts_ref[...], axis=0, keepdims=True)
-    numer = sums[:, :ny]
-    denom = pltpu.roll(sums, ny, 1)[:, :ny]
+    parts = parts_ref[...]
+    even = lax.rem(lax.broadcasted_iota(jnp.int32, parts.shape, 0), 2) == 0
+    numer = jnp.sum(jnp.where(even, parts, 0.0), axis=0, keepdims=True)
+    denom = jnp.sum(jnp.where(even, 0.0, parts), axis=0, keepdims=True)
+    numer = (numer + pltpu.roll(numer, ny, 1))[:, :ny]
+    denom = (denom + pltpu.roll(denom, ny, 1))[:, :ny]
     coefficient = numer / cells / (denom / cells + 1e-06)
     coefficient_ref[...] = coefficient
     column = jnp.broadcast_to(coefficient, (mag_ref.shape[2], ny)).T
@@ -489,7 +490,7 @@
     count = lax.axis_size("gx") * lax.axis_size("gz")
     *_, plain, sums = call(
         rim_kernel,
-        (u_shape, work[0], work[3], work[4], (nx, ny, nz), (count, lanes)),
+        (u_shape, work[0], work[3], work[4], (nx, ny, nz), (2 * count, lanes)),
         (high, low, u, keep, hu, mag, plain, acc),
         1000,
         {2 + n: n for n in range(5)},

time: 31.7 us -> 31.8 us (level)
  no operation moved by 1% of the time
where the time goes in v10:
time: 31.8 us; the launch traced here: 31.6 us
  blocking collectives  10.1 us (32%)
  starting transfers between devices  8.5 us (27%)
  Pallas kernels  7.43 us (23%)
  waiting for transfers between devices  3.75 us (12%)
  local copies, waits for them, and re-layouts  1.13 us (4%)
  between operations  0.69 us (2%)
    all_to_all x1, blocking collectives, on_device(): parts = lax.all_to_all(sums, ('gx', 'gz'), 0, 0, tiled=True)  10.1 us
    pallas_call x8, Pallas kernels, call(): pl.pallas_call(kernel, out_shape=tuple((jax.ShapeDtypeStruct(shape, jnp.f...  7.43 us
    ppermute x1, waiting for transfers between devices, on_device(): strip = lax.ppermute(strip, 'gx', to_second)  3.74 us
    ppermute x1, starting transfers between devices, on_device(): second = lax.ppermute(second, 'gx', to_second)  3.54 us
    ppermute x1, starting transfers between devices, on_device(): low = lax.ppermute(edges, 'gz', to_second)  2.47 us
    ppermute x1, starting transfers between devices, on_device(): high = lax.ppermute(edges, 'gz', to_first)  1.89 us
    unnamed x2, local copies, waits for them, and re-layouts  1.13 us
  transfers between devices with their start and end apart: 5, of which 1 were waited for; matrix products, arithmetic and copies ran while one was open for 0% of the time, Pallas kernels for 18%

profile of v10, /device:TPU:0, one launch (start us, length us, event | category | flops | bytes accessed | tf_op | source)
XLA Modules:
  0.0 31.6 jit_solution(2713351103859696658)
XLA Ops:
  0.6 0.0 copy-start
  0.6 1.1 %copy-done = f32[3,8,64,128]{3,2,1,0:T(8,128)S(1)} copy-done((f32[3,8,64,128]{3,2,1,0:T(8,128)S(1)}, f32[3,8,64,128]{3,2,1,0:T(8,128)}, u32[]{:S(2)}) %copy-start) | copy-done | bytes 786456
  1.8 0.2 shard_map.30
  2.0 0.5 %collective-permute-start.1 = (f32[3,2,64,128]{3,2,1,0:T(8,128)S(1)}, f32[3,2,64,128]{3,2,1,0:T(8,128)S(1)}, u32[]{:S(2)}, u32[]{:S(2)}) collective-permute-start(f32[3,2,64,128]{3,2,1,0:T(8,128)S(1)} %get-tuple-element.26), channel_id=1, source_target_pairs={{0,4},{4,0},{8,12},{12,8},{16,20},{20,16},{24,28},{28,24},{1,5},{5... | collective-permute-start | bytes 589832 | tf_op jit(solution)/shard_map/ppermute | solution.py:471
  2.5 3.5 %collective-permute-start.4 = (f32[3,2,64,128]{3,2,1,0:T(8,128)S(1)}, f32[3,2,64,128]{3,2,1,0:T(8,128)S(1)}, u32[]{:S(2)}, u32[]{:S(2)}) collective-permute-start(f32[3,2,64,128]{3,2,1,0:T(8,128)S(1)} %get-tuple-element.30), channel_id=1, source_target_pairs={{0,28},{4,8},{8,4},{12,16},{16,12},{20,24},{24,20},{28,0},{1,29},{... | collective-permute-start | bytes 589832 | tf_op jit(solution)/shard_map/ppermute | solution.py:472
  6.1 0.0 collective-permute-start
  6.1 0.8 %shard_map.31 = (f32[3,12,88,128]{3,2,1,0:T(8,128)S(1)}, f32[80,128]{1,0:T(8,128)S(1)}) custom-call(f32[3,8,64,128]{3,2,1,0:T(8,128)S(1)} %copy-done), custom_call_target="tpu_custom_call" | custom-call | flops 4915200 | tf_op jit(solution)/shard_map/pallas_call | solution.py:429
  6.9 0.0 collective-permute-done.1.first_ref
  6.9 0.2 shard_map.32
  7.1 3.7 %collective-permute-done.strip_ref = f32[16,128]{1,0:T(8,128)S(1)} collective-permute-done((f32[16,128]{1,0:T(8,128)S(1)}, f32[16,128]{1,0:T(8,128)S(1)}, u32[]{:S(2)}, u32[]{:S(2)}) %collective-permute-start) | collective-permute-done | bytes 8224 | tf_op jit(solution)/shard_map/ppermute | solution.py:470
  10.9 1.9 %collective-permute-start.2 = (f32[80,128]{1,0:T(8,128)S(1)}, f32[80,128]{1,0:T(8,128)S(1)}, u32[]{:S(2)}, u32[]{:S(2)}) collective-permute-start(f32[80,128]{1,0:T(8,128)S(1)} %shard_map.33), channel_id=1, source_target_pairs={{0,1},{1,0},{2,3},{3,2},{4,5},{5,4},{6,7},{7,6},{8,9},{9,8},{10,11... | collective-permute-start | bytes 122888 | tf_op jit(solution)/shard_map/ppermute | solution.py:480
  12.8 2.5 %collective-permute-start.3 = (f32[80,128]{1,0:T(8,128)S(1)}, f32[80,128]{1,0:T(8,128)S(1)}, u32[]{:S(2)}, u32[]{:S(2)}) collective-permute-start(f32[80,128]{1,0:T(8,128)S(1)} %shard_map.33), channel_id=1, source_target_pairs={{0,3},{1,2},{2,1},{3,0},{4,7},{5,6},{6,5},{7,4},{8,11},{9,10},{10,... | collective-permute-start | bytes 122888 | tf_op jit(solution)/shard_map/ppermute | solution.py:479
  15.3 3.5 %shard_map.34 = (f32[12,10,16,128]{3,2,1,0:T(8,128)S(1)}, f32[12,10,64,128]{3,2,1,0:T(8,128)S(1)}, f32[3,12,72,128]{3,2,1,0:T(8,128)S(1)}, f32[3,10,72,128]{3,2,...) custom-call(f32[3,12,88,128]{3,2,1,0:T(8,128)S(1)} %get-tuple-element.31.u_ref._0), custom_call_target="tpu_custom_call" | custom-call | flops 24576000 | tf_op jit(solution)/shard_map/pallas_call | solution.py:429
  18.7 0.0 collective-permute-done.4.second_ref
  18.7 1.1 %shard_map.35 = (f32[3,12,88,128]{3,2,1,0:T(8,128)S(1)}, f32[12,10,16,128]{3,2,1,0:T(8,128)S(1)}, f32[12,10,64,128]{3,2,1,0:T(8,128)S(1)}, f32[3,12,72,128]{3,2,...) custom-call(f32[3,2,64,128]{3,2,1,0:T(8,128)S(1)} %collective-permut, ...), custom_call_target="tpu_custom_call", output_to_operand_aliasing={{0}: (1, {}), {1}: (2, {}), {2}: (3, {}), {3}: (4, {}), {4}... | custom-call | flops 8192000 | tf_op jit(solution)/shard_map/pallas_call | solution.py:429
  19.8 0.0 collective-permute-done.2.first_ref
  19.8 0.0 collective-permute-done.3.second_ref
  19.8 0.8 %shard_map.36 = (f32[3,12,88,128]{3,2,1,0:T(8,128)S(1)}, f32[12,10,16,128]{3,2,1,0:T(8,128)S(1)}, f32[3,10,72,128]{3,2,1,0:T(8,128)S(1)}, f32[10,72,128]{2,1,0:T...) custom-call(f32[80,128]{1,0:T(8,128)S(1)} %collective-permute-done.2, ...), custom_call_target="tpu_custom_call", output_to_operand_aliasing={{0}: (2, {}), {1}: (3, {}), {2}: (4, {}), {3}: (5, {}), {4}... | custom-call | flops 4096000 | tf_op jit(solution)/shard_map/pallas_call | solution.py:429
  20.6 10.1 %all_to_all.11 = f32[32,2,128]{2,1,0:T(2,128)S(1)} all-to-all(f32[32,2,128]{2,1,0:T(2,128)S(1)} %bitcast.4), channel_id=1, replica_groups=mesh['gx'=8,'gz'=4] {'gx','gz'}, dimensions={0} | all-to-all | bytes 65536 | tf_op jit(solution)/shard_map/all_to_all | solution.py:504
  30.7 0.9 %shard_map.37 = (f32[1,64]{1,0:T(1,128)}, f32[8,64,128]{2,1,0:T(8,128)}) custom-call(f32[64,128]{1,0:T(8,128)S(1)} %bitcast.3, f32[8,64,128]{2,1,0:T(8,128)S(1)} %get-tuple-element.45.mag_ref), custom_call_target="tpu_custom_call" | custom-call | flops 2048000 | tf_op jit(solution)/shard_map/pallas_call | solution.py:429
  (1 shorter events, 0.0 us)
Async XLA Ops:
  0.6 1.1 %copy-start = (f32[3,8,64,128]{3,2,1,0:T(8,128)S(1)}, f32[3,8,64,128]{3,2,1,0:T(8,128)}, u32[]{:S(2)}) copy-start(f32[3,8,64,128]{3,2,1,0:T(8,128)} %vel_ref.3) | copy-start | bytes 2359300
  2.0 4.9 %collective-permute-start.1 = (f32[3,2,64,128]{3,2,1,0:T(8,128)S(1)}, f32[3,2,64,128]{3,2,1,0:T(8,128)S(1)}, u32[]{:S(2)}, u32[]{:S(2)}) collective-permute-start(f32[3,2,64,128]{3,2,1,0:T(8,128)S(1)} %get-tuple-element.26), channel_id=1, source_target_pairs={{0,4},{4,0},{8,12},{12,8},{16,20},{20,16},{24,28},{28,24},{1,5},{5... | collective-permute-start | bytes 589832 | tf_op jit(solution)/shard_map/ppermute | solution.py:471
  2.5 16.2 %collective-permute-start.4 = (f32[3,2,64,128]{3,2,1,0:T(8,128)S(1)}, f32[3,2,64,128]{3,2,1,0:T(8,128)S(1)}, u32[]{:S(2)}, u32[]{:S(2)}) collective-permute-start(f32[3,2,64,128]{3,2,1,0:T(8,128)S(1)} %get-tuple-element.30), channel_id=1, source_target_pairs={{0,28},{4,8},{8,4},{12,16},{16,12},{20,24},{24,20},{28,0},{1,29},{... | collective-permute-start | bytes 589832 | tf_op jit(solution)/shard_map/ppermute | solution.py:472
  6.1 4.8 %collective-permute-start = (f32[16,128]{1,0:T(8,128)S(1)}, f32[16,128]{1,0:T(8,128)S(1)}, u32[]{:S(2)}, u32[]{:S(2)}) collective-permute-start(f32[16,128]{1,0:T(8,128)S(1)} %get-tuple-element.25), channel_id=1, source_target_pairs={{0,28},{4,8},{8,4},{12,16},{16,12},{20,24},{24,20},{28,0},{1,29},{... | collective-permute-start | bytes 24584 | tf_op jit(solution)/shard_map/ppermute | solution.py:470
  10.9 8.9 %collective-permute-start.2 = (f32[80,128]{1,0:T(8,128)S(1)}, f32[80,128]{1,0:T(8,128)S(1)}, u32[]{:S(2)}, u32[]{:S(2)}) collective-permute-start(f32[80,128]{1,0:T(8,128)S(1)} %shard_map.33), channel_id=1, source_target_pairs={{0,1},{1,0},{2,3},{3,2},{4,5},{5,4},{6,7},{7,6},{8,9},{9,8},{10,11... | collective-permute-start | bytes 122888 | tf_op jit(solution)/shard_map/ppermute | solution.py:480
  12.8 7.1 %collective-permute-start.3 = (f32[80,128]{1,0:T(8,128)S(1)}, f32[80,128]{1,0:T(8,128)S(1)}, u32[]{:S(2)}, u32[]{:S(2)}) collective-permute-start(f32[80,128]{1,0:T(8,128)S(1)} %shard_map.33), channel_id=1, source_target_pairs={{0,3},{1,2},{2,1},{3,0},{4,7},{5,6},{6,5},{7,4},{8,11},{9,10},{10,... | collective-permute-start | bytes 122888 | tf_op jit(solution)/shard_map/ppermute | solution.py:479
